TPU v7x, 256 devices: a whole 4x4x8 slice. The times are simulated.
256 devices in a mesh: seq: 64 (over y, z, core), mp: 4 (over x).
Axes of the slice: x: 4, y: 4, z: 8, core: 2. Of those that a mesh axis runs over, the one named last changes fastest.
Arguments:
- hidden_in: bfloat16 [2, 8192, 2048], P(None, 'seq'), may hold values from -6 to 6
- attn_gain: float32 [2048], replicated, may hold values from 0.1 to 1.9
- q_weight: bfloat16 [2048, 2048], P(None, 'mp'), may hold values from -0.125 to 0.125
- q_bias: float32 [2048], P('mp'), may hold values from -60 to 60
- k_weight: bfloat16 [2048, 256], replicated, may hold values from -0.125 to 0.125
- k_bias: float32 [256], replicated, may hold values from -60 to 60
- v_weight: bfloat16 [2048, 256], replicated, may hold values from -0.125 to 0.125
- v_bias: float32 [256], replicated, may hold values from -3 to 3
- o_weight: bfloat16 [2048, 2048], P('mp'), may hold values from -0.125 to 0.125
- mlp_gain: float32 [2048], replicated, may hold values from 0.1 to 1.9
- gate_weight: bfloat16 [2048, 5632], P('seq', 'mp'), may hold values from -0.125 to 0.125
- up_weight: bfloat16 [2048, 5632], P('seq', 'mp'), may hold values from -0.125 to 0.125
- down_weight: bfloat16 [2048, 5632], P('seq', 'mp'), may hold values from -0.078125 to 0.078125
- lengths: int32 [2], replicated, may hold values from 4096 to 8192
Outputs:
- layer_out: bfloat16 [2, 8192, 2048], P(None, 'seq', 'mp')
- influence: float32 [2, 8192], P(None, 'seq')
- score: float32 [2], replicated
Inputs may be any that keep to these rules, and one draw needn't show every extreme that they name: `lengths`: tokens at positions 4096 and later may be invalid.
All inputs are finite; a program needn't handle non-finite values.
Results may differ from a plain program's by a relative error of at most 0.02.
The roundings to bfloat16 on the way count: a program that leaves them out, or rounds other values in their place, can miss the bound.
Values may be sent and summed in bfloat16 or wider, within the bound.
A program may use at most 192 MiB of HBM per device.

v0:
```python
import jax
import jax.numpy as jnp
from jax import lax
from jax.sharding import PartitionSpec as P

HEADS = 16
KV_HEADS = 2
HEAD = 128


rope_base = 1000000.0
norm_eps = 1e-06
masked_score = -1e30


def in_one_piece(arrays, axis, dim, along):
    ends, at = ([], 0)
    for a in arrays[:-1]:
        at += a.shape[along]
        ends.append(at)
    both = jnp.concatenate(arrays, axis=along)
    return tuple(jnp.split(lax.all_gather(both, axis, axis=dim, tiled=True), ends, axis=along))


def in_blocks(shard, dim, length):
    lengths = shard.shape
    parts = shard.reshape(*lengths[:dim], length, lengths[dim] // length, *lengths[dim + 1 :])
    return jnp.moveaxis(parts, dim, 0)


def sent_and_summed(shard, axis, dim):
    parts = in_blocks(shard, dim, lax.axis_size(axis))
    arrived = lax.all_to_all(parts, axis, split_axis=0, concat_axis=0, tiled=True)
    return arrived.astype(jnp.float32).sum(axis=0)


def joined_along(parts, dim):
    lengths = list(parts.shape[1:])
    lengths[dim] *= parts.shape[0]
    return jnp.moveaxis(parts, 0, dim).reshape(lengths)


def sent_to_all(shard, axis):
    length = lax.axis_size(axis)
    return lax.all_to_all(
        jnp.broadcast_to(shard[None], (length, *shard.shape)), axis, 0, 0, tiled=True
    )


def gather_directly(shard, axis, dim):
    return joined_along(sent_to_all(shard, axis), dim)


def of_everyone(shard, axis):
    return sent_to_all(shard, axis).sum(axis=0)


def in_one(arrays, axis):
    vector, at, finished = (jnp.concatenate([a.reshape(-1) for a in arrays]), 0, [])
    running = of_everyone(vector, axis)
    for a in arrays:
        finished.append(running[at : at + a.size].reshape(a.shape))
        at += a.size
    return tuple(finished)


def rms_scale(values, gain):
    widened = values.astype(jnp.float32)
    factor = lax.rsqrt(jnp.mean(widened * widened, axis=-1, keepdims=True) + norm_eps)
    return (widened * factor * gain).astype(jnp.bfloat16)


def rotate(values, positions):
    head_width = values.shape[-1]
    half_width = head_width // 2
    inv_freq = rope_base ** (-(jnp.arange(half_width, dtype=jnp.float32) * 2.0) / head_width)
    angles = positions.astype(jnp.float32)[:, None] * inv_freq[None, :]
    angles = jnp.concatenate([angles, angles], axis=-1)
    first_part = values[..., :half_width]
    second_part = values[..., half_width:]
    turned = jnp.concatenate([-second_part, first_part], axis=-1)
    return values * jnp.cos(angles) + turned * jnp.sin(angles)


def attend_update(state, queries, first_pos, key_piece, value_piece):
    run_max, run_sum, run_acc = state
    score_scale = queries.shape[-1] ** (-0.5)
    query_pos = first_pos + jnp.arange(queries.shape[2], dtype=jnp.int32)
    key_pos = jnp.arange(key_piece.shape[1], dtype=jnp.int32)
    scores = (
        jnp.einsum("shqd,skd->shqk", queries, key_piece, preferred_element_type=jnp.float32)
        * score_scale
    )
    allowed = key_pos[None, :] <= query_pos[:, None]
    scores = jnp.where(allowed, scores, masked_score)
    new_max = jnp.maximum(run_max, jnp.max(scores, axis=-1))
    weights = jnp.where(allowed, jnp.exp(scores - new_max[..., None]), 0.0)
    new_sum = jnp.sum(weights, axis=-1)
    mixed = jnp.einsum(
        "shqk,skd->shqd",
        weights.astype(jnp.bfloat16),
        value_piece,
        preferred_element_type=jnp.float32,
    )
    return (new_max, new_sum, mixed)


def local(
    hidden_in,
    attn_gain,
    q_weight,
    q_bias,
    k_weight,
    k_bias,
    v_weight,
    v_bias,
    o_weight,
    mlp_gain,
    gate_weight,
    up_weight,
    down_weight,
    lengths,
):
    seqs_n, tok_n, width = hidden_in.shape
    seq_rank = lax.axis_index("seq")
    mp_devices = lax.axis_size("mp")
    mp_rank = lax.axis_index("mp")
    heads_here = q_weight.shape[1] // HEAD
    group_size = HEADS // KV_HEADS
    kv_index = mp_rank * heads_here // group_size
    flat_in = hidden_in.reshape(seqs_n * tok_n, width)
    normed = rms_scale(flat_in, attn_gain)
    query_all = jnp.dot(normed, q_weight, preferred_element_type=jnp.float32) + q_bias
    key_cols = lax.dynamic_slice_in_dim(k_weight, kv_index * HEAD, HEAD, 1)
    value_cols = lax.dynamic_slice_in_dim(v_weight, kv_index * HEAD, HEAD, 1)
    key_shift = lax.dynamic_slice_in_dim(k_bias, kv_index * HEAD, HEAD, 0)
    value_shift = lax.dynamic_slice_in_dim(v_bias, kv_index * HEAD, HEAD, 0)
    key_all = jnp.dot(normed, key_cols, preferred_element_type=jnp.float32) + key_shift
    value_rows = (
        jnp.dot(normed, value_cols, preferred_element_type=jnp.float32) + value_shift
    ).astype(jnp.bfloat16)
    positions = seq_rank * tok_n + jnp.arange(tok_n, dtype=jnp.int32)
    rotated_q = rotate(
        query_all.reshape(seqs_n, tok_n, heads_here, HEAD).transpose(0, 2, 1, 3), positions
    ).astype(jnp.bfloat16)
    rotated_k = rotate(key_all.reshape(seqs_n, tok_n, HEAD), positions).astype(jnp.bfloat16)
    value_rows = value_rows.reshape(seqs_n, tok_n, HEAD)
    query_sets = ((rotated_q, seq_rank * tok_n),)
    initial = tuple(
        (
            (
                jnp.full(entry[0].shape[:3], masked_score, jnp.float32),
                jnp.zeros(entry[0].shape[:3], jnp.float32),
                jnp.zeros(entry[0].shape, jnp.float32),
            )
            for entry in query_sets
        )
    )
    key_start = jnp.int32(0)
    key_piece, value_piece = in_one_piece((rotated_k, value_rows), "seq", 1, 0)
    updated = []
    for state, query_entry in zip(initial, query_sets):
        queries, first_pos = query_entry
        last_pos = first_pos + queries.shape[2] - 1

        def run_update(current):
            return attend_update(current, queries, first_pos, key_piece, value_piece)

        def keep_state(current):
            return current

        updated.append(lax.cond(key_start <= last_pos, run_update, keep_state, state))
    results = tuple(updated)
    finished = [(entry[2] / entry[1][..., None]).astype(jnp.bfloat16) for entry in results]
    attn = finished[0]
    attn = attn.transpose(0, 2, 1, 3).reshape(seqs_n * tok_n, heads_here * HEAD)
    projected = jnp.dot(attn, o_weight, preferred_element_type=jnp.float32)
    quarter = width // mp_devices
    own_in = lax.dynamic_slice_in_dim(flat_in, mp_rank * quarter, quarter, 1)
    summed = sent_and_summed(projected.astype(jnp.bfloat16), "mp", 1)
    resid_part = (own_in.astype(jnp.float32) + summed).astype(jnp.bfloat16)
    residual = gather_directly(resid_part, "mp", 1)
    mlp_in = rms_scale(residual, mlp_gain)
    pieces = in_one_piece((gate_weight, up_weight), "seq", 0, 1)
    gate_sum = jnp.dot(mlp_in, pieces[0], preferred_element_type=jnp.float32)
    up_sum = jnp.dot(mlp_in, pieces[1], preferred_element_type=jnp.float32)
    activated = (jax.nn.silu(gate_sum) * up_sum).astype(jnp.bfloat16)
    down_part = lax.dot_general(
        activated,
        lax.all_gather(down_weight, "seq", axis=0, tiled=True),
        (((1,), (1,)), ((), ())),
        preferred_element_type=jnp.float32,
    )
    mlp_share = sent_and_summed(down_part.astype(jnp.bfloat16), "mp", 1)
    layer_part = (resid_part.astype(jnp.float32) + mlp_share).astype(jnp.bfloat16)
    in_share = own_in.astype(jnp.float32)
    out_share = layer_part.astype(jnp.float32)
    cross_part = jnp.sum(in_share * out_share, axis=-1).reshape(seqs_n, tok_n)
    out_part = jnp.sum(out_share * out_share, axis=-1).reshape(seqs_n, tok_n)
    cross, out_norm = in_one((cross_part, out_part), "mp")
    in_wide = flat_in.astype(jnp.float32)
    in_norm = jnp.sum(in_wide * in_wide, axis=-1).reshape(seqs_n, tok_n)
    cosine = cross / jnp.sqrt((in_norm + norm_eps) * (out_norm + norm_eps))
    valid = positions[None, :] < lengths[:, None]
    influence = jnp.where(valid, 1.0 - cosine, 0.0)
    seq_total = of_everyone(jnp.sum(influence, axis=1), "seq")
    score = seq_total / lengths.astype(jnp.float32)
    return (layer_part.reshape(seqs_n, tok_n, quarter), influence, score)


def solution(mesh):
    placed = (
        P(None, "seq", None),
        P(),
        P(None, "mp"),
        P("mp"),
        P(),
        P(),
        P(),
        P(),
        P("mp", None),
        P(),
        P("seq", "mp"),
        P("seq", "mp"),
        P("seq", "mp"),
        P(),
    )
    return jax.shard_map(
        local,
        mesh=mesh,
        in_specs=placed,
        out_specs=(P(None, "seq", "mp"), P(None, "seq"), P()),
        check_vma=False,
    )
```

profile of v0, /device:TPU:1, one launch (start us, length us, event | category | flops | bytes accessed | tf_op | source)
XLA Modules:
  0.0 335.8 jit_solution(13534737681419073449)
XLA Ops:
  7.3 1.6 multiply_reduce_fusion.1
  8.9 0.8 dynamic_slice.17
  9.7 1.5 multiply_convert_fusion
  11.2 1.5 convolution_add_fusion.2
  12.7 0.7 slice_negate_fusion.1
  13.5 0.3 fusion.43
  13.8 0.8 dynamic_slice.19
  14.6 1.5 fusion.28
  16.0 1.0 fusion.41
  17.1 0.7 pad_maximum_fusion.1
  17.8 1.6 pad_maximum_fusion
  19.5 0.7 all-gather.8.cloned.1.call-update
  20.2 3.1 convolution_add_fusion
  23.3 1.2 reshape.232
  24.5 0.2 slice_negate_fusion
  24.8 0.9 fusion.34
  25.7 79.4 %all-gather.4.cloned.1.call-done = bf16[4,8192,128]{2,1,0:T(8,128)(2,1)} async-done(((bf16[4,128,128]{2,1,0:T(8,128)(2,1)}), bf16[4,8192,128]{2,1,0:T(8,128)(2,1)}) %all-gather.4.cloned.1.call-update) | async-done | bytes 8388624 | tf_op jit(solution)/shard_map/all_gather | solution.py:22
  105.1 49.4 %conditional.1 = (f32[2,4,128]{2,1,0:T(4,128)S(1)}, f32[2,4,128,128]{3,2,1,0:T(8,128)}) conditional(s32[]{:T(128)} %convert_element_type.87, () %tuple.16, (s32[]{:T(128)}, bf16[4,8192,128]{2,1,0:T(8,128)(2,1)}, bf16[2,4,128,128]{3,2,1,0:T(8,128)(2,1)}) %tuple.17), branch_computations={%region_1.2_spmd, %region_2.5_spmd} | conditional | flops 4405066752 | bytes 114058256 | solution.py:172
  105.1 0.7 iota_compare_fusion
  105.7 15.8 %fusion = (f32[2,4,128]{2,1,0:T(4,128)S(1)}, f32[2,4,128,8192]{3,2,1,0:T(8,128)}) fusion(pred[128,8192]{1,0:T(8,128)(4,1)S(1)} %iota_compare_fusion, bf16[2,4,128,128]{3,2,1,0:T(8,128)(2,1)} %get-tuple-element.10, bf16[4,8192,128]{2,1,0:T(8,128)(2,1)} %get-tuple-element.11), kind=kOutput, calls=%fused_computation.2 | convolution fusion | flops 2172648448 | bytes 39063552 | tf_op jit(solution)/shard_map/cond/branch_1_fun/shqd,skd->shqk/dot_general | solution.py:91
  121.6 17.3 %fusion.3 = f32[2,4,128,128]{3,2,1,0:T(8,128)} fusion(f32[2,4,128,8192]{3,2,1,0:T(8,128)} %get-tuple-element.25, f32[2,4,128]{2,1,0:T(4,128)S(1)} %broadcast_maximum_fusion, pred[128,8192]{1,0:T(8,128)(4,1)S(1)} %iota_compare_fusion, bf16[4,8192,128]{2,1,0:T(8,128)(2,1)} %get-tuple-element.11), kind=kOutput, calls=%fused_computation.5 | convolution fusion | flops 2189426688 | bytes 39325696 | tf_op jit(solution)/shard_map/cond/branch_1_fun/shqk,skd->shqd/dot_general | solution.py:99
  138.9 15.6 %fusion.2 = f32[2,4,128]{2,1,0:T(4,128)S(1)} fusion(f32[2,4,128,8192]{3,2,1,0:T(8,128)} %get-tuple-element.25, f32[2,4,128]{2,1,0:T(4,128)S(1)} %broadcast_maximum_fusion, pred[128,8192]{1,0:T(8,128)(4,1)S(1)} %iota_compare_fusion), kind=kLoop, calls=%fused_computation.4 | loop fusion | flops 41942016 | bytes 34611200 | tf_op jit(solution)/shard_map/cond/branch_1_fun/reduce_sum | solution.py:98
  154.5 1.3 fusion.39
  155.8 0.2 copy.37
  156.1 0.7 convolution_convert_fusion
  156.8 1.1 copy.66
  157.9 4.2 %all-to-all-start = ((bf16[4,256,512]{2,1,0:T(8,128)(2,1)}), bf16[4,256,512]{2,1,0:T(8,128)(2,1)}, u32[]{:S(2)}, u32[]{:S(2)}) async-start(bf16[4,256,512]{2,1,0:T(8,128)(2,1)} %bitcast.79), calls=%async_computation | async-start | bytes 2097152 | tf_op jit(solution)/shard_map/all_to_all | solution.py:33
  162.1 14.8 %all-to-all-done = bf16[4,256,512]{2,1,0:T(8,128)(2,1)} async-done(((bf16[4,256,512]{2,1,0:T(8,128)(2,1)}), bf16[4,256,512]{2,1,0:T(8,128)(2,1)}, u32[]{:S(2)}, u32[]{:S(2)}) %all-to-all-start) | async-done | bytes 1048608 | tf_op jit(solution)/shard_map/all_to_all | solution.py:33
  177.0 1.4 convert_reduce_fusion.1
  178.5 0.8 copy.40
  179.3 1.0 broadcast_in_dim.33
  180.4 16.3 %all_to_all.27 = bf16[4,256,512]{1,2,0:T(8,128)(2,1)S(1)} all-to-all(bf16[4,256,512]{1,2,0:T(8,128)(2,1)S(1)} %broadcast_in_dim.33), channel_id=1, replica_groups=mesh['seq'=64,'mp'=4] {'mp'}, dimensions={0} | all-to-all | bytes 2097152 | tf_op jit(solution)/shard_map/all_to_all | solution.py:45
  196.7 0.3 multiply_reduce_fusion
  197.0 1.3 fusion.25
  198.4 5.9 %fusion.16 = f32[256,1408]{1,0:T(8,128)} fusion(bf16[256,2048]{0,1:T(8,128)(2,1)} %fusion.25, bf16[2048,2816]{1,0:T(8,128)(2,1)} %all-gather.6.cloned.1.call-done), kind=kOutput, calls=%fused_computation.20 | convolution fusion | flops 1476395008 | bytes 8257536 | tf_op jit(solution)/shard_map/dot_general | solution.py:185
  204.3 67.9 %all-gather.8.cloned.1.call-done = bf16[2048,1408]{1,0:T(8,128)(2,1)} async-done(((bf16[32,1408]{1,0:T(8,128)(2,1)}), bf16[2048,1408]{1,0:T(8,128)(2,1)}) %all-gather.8.cloned.1.call-update) | async-done | bytes 5767184 | tf_op jit(solution)/shard_map/all_gather | solution.py:190
  272.2 9.5 %convolution_convert_fusion.1 = bf16[256,2048]{1,0:T(8,128)(2,1)} fusion(bf16[2048,1408]{1,0:T(8,128)(2,1)} %all-gather.8.cloned.1.call-done, bf16[256,2048]{0,1:T(8,128)(2,1)} %fusion.25, bf16[2048,2816]{1,0:T(8,128)(2,1)} %all-gather.6.cloned.1.call-done, f32[256,1408]{1,0:T(8,128)} %fusion.16), kind=kOutput, calls=%fused_computation.25 | convolution fusion | flops 2955476992 | bytes 15073280 | tf_op jit(solution)/shard_map/dot_general | solution.py:188
  281.8 1.3 copy.65
  283.1 18.4 %all_to_all.28 = bf16[4,256,512]{2,1,0:T(8,128)(2,1)S(1)} all-to-all(bf16[4,256,512]{2,1,0:T(8,128)(2,1)S(1)} %bitcast.81), channel_id=1, replica_groups=mesh['seq'=64,'mp'=4] {'mp'}, dimensions={0} | all-to-all | bytes 2097152 | tf_op jit(solution)/shard_map/all_to_all | solution.py:33
  301.5 0.1 convert_reduce_fusion
  301.6 0.8 fusion.31
  302.5 0.6 broadcast_in_dim.34
  303.1 3.2 all-to-all-start.3
  306.3 4.1 %all-to-all-done.3 = f32[4,1,512]{2,1,0:T(1,128)S(1)} async-done(((f32[4,1,512]{2,1,0:T(1,128)}), f32[4,1,512]{2,1,0:T(1,128)S(1)}, u32[]{:S(2)}, u32[]{:S(2)}) %all-to-all-start.3) | async-done | bytes 8224 | tf_op jit(solution)/shard_map/all_to_all | solution.py:45
  310.5 0.7 fusion.51
  311.3 17.4 %all_to_all.29 = f32[64,1,2]{2,1,0:T(1,128)S(1)} all-to-all(f32[64,1,2]{2,1,0:T(1,128)S(1)} %broadcast_in_dim.36), channel_id=1, replica_groups=mesh['seq'=64,'mp'=4] {'seq'}, dimensions={0} | all-to-all | bytes 1024 | tf_op jit(solution)/shard_map/all_to_all | solution.py:45
  328.7 0.1 reduce_sum.102
  328.7 0.5 convert_divide_fusion
  (29 shorter events, 0.5 us)
Async XLA Ops:
  7.2 148.9 %copy-start = (bf16[512,2048]{1,0:T(8,128)(2,1)S(1)}, bf16[512,2048]{1,0:T(8,128)(2,1)}, u32[]{:S(2)}) copy-start(bf16[512,2048]{1,0:T(8,128)(2,1)} %param.24) | copy-start | bytes 6291460
  7.2 13.0 %copy-start.4 = (f32[512]{0:T(512)S(1)}, f32[512]{0:T(512)}, u32[]{:S(2)}) copy-start(f32[512]{0:T(512)} %param.19) | copy-start | bytes 6148
  7.2 97.9 %all-gather.4.cloned.1.call-start = ((), (), s32[]{:S(2)}) async-start(), calls=%async_computation.5 | async-start | bytes 8519680 | tf_op jit(solution)/shard_map/all_gather | solution.py:22
  17.8 180.6 %all-gather.6.cloned.1.call-start = ((), (), s32[]{:S(2)}) async-start(), calls=%async_computation.6 | async-start | bytes 11714560 | tf_op jit(solution)/shard_map/all_gather | solution.py:22
  19.4 252.8 %all-gather.8.cloned.1.call-start = ((), (), s32[]{:S(2)}) async-start(), calls=%async_computation.7 | async-start | bytes 5857280 | tf_op jit(solution)/shard_map/all_gather | solution.py:190
  154.5 23.9 %copy-start.1 = (bf16[2,128,2048]{2,1,0:T(8,128)(2,1)S(1)}, bf16[2,128,2048]{2,1,0:T(8,128)(2,1)}, u32[]{:S(2)}) copy-start(bf16[2,128,2048]{2,1,0:T(8,128)(2,1)} %param.16) | copy-start | bytes 3145732
  156.8 40.2 %copy-start.2 = (f32[2048]{0:T(1024)S(1)}, f32[2048]{0:T(1024)}, u32[]{:S(2)}) copy-start(f32[2048]{0:T(1024)} %param.25) | copy-start | bytes 24580
  157.9 19.1 %all-to-all-start = ((bf16[4,256,512]{2,1,0:T(8,128)(2,1)}), bf16[4,256,512]{2,1,0:T(8,128)(2,1)}, u32[]{:S(2)}, u32[]{:S(2)}) async-start(bf16[4,256,512]{2,1,0:T(8,128)(2,1)} %bitcast.79), calls=%async_computation | async-start | bytes 2097152 | tf_op jit(solution)/shard_map/all_to_all | solution.py:33
  281.8 28.7 %copy-start.3 = (s32[2]{0:T(128)S(1)}, s32[2]{0:T(128)}, u32[]{:S(2)}) copy-start(s32[2]{0:T(128)} %param.29) | copy-start | bytes 28
  303.1 7.4 %all-to-all-start.3 = ((f32[4,1,512]{2,1,0:T(1,128)}), f32[4,1,512]{2,1,0:T(1,128)S(1)}, u32[]{:S(2)}, u32[]{:S(2)}) async-start(f32[4,1,512]{2,1,0:T(1,128)} %broadcast_in_dim.34), calls=%async_computation.3 | async-start | bytes 16384 | tf_op jit(solution)/shard_map/all_to_all | solution.py:45
Sparse Core Ops, SparseCore 0:
  17.9 87.1 all-gather.3
  107.8 84.6 all-gather.5
  195.2 76.9 all-gather.7
where the time goes:
time: 337 us; the launch traced here: 336 us
  waiting for transfers between devices  167 us (50%)
  matrix products  55.3 us (16%)
  blocking collectives  52.1 us (15%)
  other arithmetic  31.8 us (9%)
  between operations  14 us (4%)
  local copies, waits for them, and re-layouts  7.89 us (2%)
  starting transfers between devices  7.61 us (2%)
    all_gather x2, waiting for transfers between devices, in_one_piece(): lax.all_gather(both, axis, axis=dim, tiled=True)  79.4 us
    all_gather x1, waiting for transfers between devices, local(): lax.all_gather(down_weight, 'seq', axis=0, tiled=True)  67.9 us
    all_to_all x2, blocking collectives, sent_to_all(): lax.all_to_all(jnp.broadcast_to(shard[None], (length, *shard.shape)), axi...  33.7 us
    all_to_all x1, blocking collectives, sent_and_summed(): lax.all_to_all(parts, axis, split_axis=0, concat_axis=0, tiled=True)  18.4 us
    dot_general x1, matrix products, attend_update(): jnp.einsum('shqk,skd->shqd', weights.astype(jnp.bfloat16), value_piece, p...  17.3 us
    dot_general x1, matrix products, attend_update(): jnp.einsum('shqd,skd->shqk', queries, key_piece, preferred_element_type=j...  15.8 us
    reduce_sum x1, other arithmetic, attend_update(): new_sum = jnp.sum(weights, axis=-1)  15.6 us
    all_to_all x1, waiting for transfers between devices, sent_and_summed(): lax.all_to_all(parts, axis, split_axis=0, concat_axis=0, tiled=True)  14.8 us
  transfers between devices with their start and end apart: 5, of which 4 were waited for; matrix products, arithmetic and copies ran while one was open for 21% of the time, Pallas kernels for 0%

commit v1 on v0

v1 whole, which is shorter than its diff:
```python
import jax
import jax.numpy as jnp
from jax import lax
from jax.experimental import pallas as pl
from jax.experimental.pallas import tpu as pltpu
from jax.sharding import PartitionSpec as P

HEADS = 16
KV_HEADS = 2
HEAD = 128
D = 2048
NY, NZ = 4, 8
MP = 4
TOK = 128
ROWS = 2 * TOK
OWN_HEADS = HEADS // MP
QCOLS = OWN_HEADS * HEAD
QUART = D // MP
FFP = 1408
WR = 32

rope_base = 1000000.0
norm_eps = 1e-06
masked_score = -1e30
EXP2_SCALE = HEAD ** (-0.5) * 1.4426950408889634

MESH = pl.DeviceIdType.MESH
F32, BF16 = jnp.float32, jnp.bfloat16

Z_OFF = (0, -1, 1, -2, 2, -3, 3, -4)


def layer_kernel(
    hid_hbm, ag_ref, qw_hbm, qb_ref, kw_hbm, kb_ref, vw_hbm, vb_ref, ow_hbm, mg_ref,
    gate_hbm, up_hbm, down_hbm, cos_ref, sin_ref, len_ref,
    out_ref, infl_ref, score_ref,
    hid, hidq, normed, qw, kvw, ow, qbuf, kv, gate, ud, mbuf, lbuf, accbuf, attn,
    stage, rs1, resid, rs2, mlp_in, act, innp, sums, tot1, tot2, gbuf,
    lsem, a_send, a_recv, b_send, b_recv, x_send, x_recv, t_send, t_recv,
):
    s = lax.axis_index("seq")
    m = lax.axis_index("mp")
    y = s // (2 * NZ)
    z = lax.rem(s // 2, NZ)
    c = lax.rem(s, 2)
    kvi = m // 2

    def wrap(v, n):
        return lax.rem(v + 2 * n, n)

    def dev(yy, zz, cc):
        return (wrap(yy, NY) * NZ + wrap(zz, NZ)) * 2 + cc

    zp, zm = dev(y, z + 1, c), dev(y, z - 1, c)
    yp, ym = dev(y + 1, z, c), dev(y - 1, z, c)
    partner = dev(y, z, 1 - c)

    def rc(src, dst, ssem, rsem, sdev):
        return pltpu.make_async_remote_copy(
            src_ref=src, dst_ref=dst, send_sem=ssem, recv_sem=rsem,
            device_id={"seq": sdev, "mp": m}, device_id_type=MESH,
        )

    def rcx(src, dst, ssem, rsem, mdev):
        return pltpu.make_async_remote_copy(
            src_ref=src, dst_ref=dst, send_sem=ssem, recv_sem=rsem,
            device_id={"seq": s, "mp": mdev}, device_id_type=MESH,
        )

    own_gate = gate.at[y, z, c]
    own_up = ud.at[y, z, c, 0]
    own_down = ud.at[y, z, c, 1]
    loads = [
        pltpu.make_async_copy(up_hbm, own_up, lsem.at[0]),
        pltpu.make_async_copy(down_hbm, own_down, lsem.at[1]),
        pltpu.make_async_copy(gate_hbm, own_gate, lsem.at[2]),
        pltpu.make_async_copy(hid_hbm, hid, lsem.at[3]),
        pltpu.make_async_copy(
            kw_hbm.at[:, pl.ds(pl.multiple_of(kvi * HEAD, HEAD), HEAD)],
            kvw.at[:, pl.ds(0, HEAD)], lsem.at[4]),
        pltpu.make_async_copy(
            vw_hbm.at[:, pl.ds(pl.multiple_of(kvi * HEAD, HEAD), HEAD)],
            kvw.at[:, pl.ds(HEAD, HEAD)], lsem.at[5]),
        pltpu.make_async_copy(qw_hbm, qw, lsem.at[6]),
        pltpu.make_async_copy(
            hid_hbm.at[:, pl.ds(pl.multiple_of(m * QUART, QUART), QUART)], hidq, lsem.at[7]),
    ] + [
        pltpu.make_async_copy(ow_hbm.at[:, pl.ds(q * QUART, QUART)], ow.at[q], lsem.at[8 + q])
        for q in range(MP)
    ]
    for copy in loads:
        copy.start()

    bar = pltpu.get_barrier_semaphore()

    def greet_plane(i, _):
        pl.semaphore_signal(
            bar, inc=1, device_id={"seq": y * (2 * NZ) + lax.rem(s + i, 2 * NZ), "mp": m},
            device_id_type=MESH)
        return 0

    lax.fori_loop(1, 2 * NZ, greet_plane, 0)
    for i in range(1, NY):
        pl.semaphore_signal(bar, inc=1, device_id={"seq": dev(y + i, z, c), "mp": m}, device_id_type=MESH)
    for i in range(1, MP):
        pl.semaphore_signal(bar, inc=1, device_id={"seq": s, "mp": wrap(m + i, MP)}, device_id_type=MESH)
    pl.semaphore_wait(bar, 2 * NZ - 1 + NY - 1 + MP - 1)

    ZS, YPS, YMS, HPS, HMS, DS = range(6)

    def block(st, yy, zz):
        buf = kv if st == 0 else gate
        return buf.at[wrap(yy, NY), wrap(zz, NZ), c]

    def half(st, ref, i):
        return ref.at[i] if st == 0 else ref.at[pl.ds(i * (WR // 2), WR // 2)]

    def z_copy(st, k_to, zoff_here, right):
        ref = block(st, y, z + zoff_here)
        return rc(ref, ref, a_send.at[st, ZS, k_to], a_recv.at[st, ZS, k_to], zp if right else zm)

    def yp_copy(st, k, zz):
        ref = block(st, y, zz)
        return rc(ref, ref, a_send.at[st, YPS, k], a_recv.at[st, YPS, k], yp)

    def ym_copy(st, k, zz):
        ref = block(st, y, zz)
        return rc(ref, ref, a_send.at[st, YMS, k], a_recv.at[st, YMS, k], ym)

    def yp_recv(st, k, zz):
        ref = block(st, y - 1, zz)
        return rc(ref, ref, a_send.at[st, YPS, k], a_recv.at[st, YPS, k], yp)

    def ym_recv(st, k, zz):
        ref = block(st, y + 1, zz)
        return rc(ref, ref, a_send.at[st, YMS, k], a_recv.at[st, YMS, k], ym)

    def hp_copy(st, k, zz):
        ref = half(st, block(st, y - 1, zz), 0)
        return rc(ref, ref, a_send.at[st, HPS, k], a_recv.at[st, HPS, k], yp)

    def hm_copy(st, k, zz):
        ref = half(st, block(st, y + 1, zz), 1)
        return rc(ref, ref, a_send.at[st, HMS, k], a_recv.at[st, HMS, k], ym)

    def hp_recv(st, k, zz):
        ref = half(st, block(st, y + 2, zz), 0)
        return rc(ref, ref, a_send.at[st, HPS, k], a_recv.at[st, HPS, k], yp)

    def hm_recv(st, k, zz):
        ref = half(st, block(st, y + 2, zz), 1)
        return rc(ref, ref, a_send.at[st, HMS, k], a_recv.at[st, HMS, k], ym)

    def d_copy(st, k, zz):
        buf = kv if st == 0 else gate
        ref = buf.at[:, wrap(zz, NZ), c]
        return rc(ref, ref, a_send.at[st, DS, k], a_recv.at[st, DS, k], partner)

    def d_recv(st, k, zz):
        buf = kv if st == 0 else gate
        ref = buf.at[:, wrap(zz, NZ), 1 - c]
        return rc(ref, ref, a_send.at[st, DS, k], a_recv.at[st, DS, k], partner)

    def zk_of(k):
        return z + jnp.where(lax.rem(k, 2) == 1, -((k + 1) // 2), k // 2)

    def z_start(st):
        z_copy(st, 1, 0, True).start()
        z_copy(st, 2, 0, False).start()

    def z_hop(st, h, with_y):
        for k in (2 * h - 1, 2 * h):
            if k >= NZ:
                continue
            right = k % 2 == 1
            z_copy(st, k, Z_OFF[k], right).wait_recv()
            if k + 2 < NZ:
                z_copy(st, k + 2, Z_OFF[k], right).start()
            if with_y:
                yp_copy(st, k, z + Z_OFF[k]).start()
                ym_copy(st, k, z + Z_OFF[k]).start()

    BYP, BYM, BHP, BHM = range(4)
    RZ, LZ, DZ = 4, 12, 20

    def b_block(yy, w=None):
        ref = ud.at[wrap(yy, NY), z, c]
        return ref if w is None else ref.at[w]

    def b_copy(ref, i, d):
        return rc(ref, ref, b_send.at[i], b_recv.at[i], d)

    def group(zz, w):
        return ud.at[:, wrap(zz, NZ), c, w]

    def r_copy(i, w):
        return b_copy(group(z - (i - 1), w), RZ + 2 * (i - 1) + w, zp)

    def r_recv(i, w):
        return b_copy(group(z - i, w), RZ + 2 * (i - 1) + w, zp)

    def l_copy(i, w):
        return b_copy(group(z + (i - 1), w), LZ + 2 * (i - 1) + w, zm)

    def l_recv(i, w):
        return b_copy(group(z + i, w), LZ + 2 * (i - 1) + w, zm)

    def r_steps(w):
        return 4 if w == 0 else 3

    def l_steps(w):
        return 3 if w == 0 else 4

    def bd_copy(k):
        return b_copy(ud.at[:, wrap(z + Z_OFF[k], NZ), c], DZ + k, partner)

    def bd_recv(k):
        return b_copy(ud.at[:, wrap(z + Z_OFF[k], NZ), 1 - c], DZ + k, partner)

    def b_hop(h, w):
        if h <= r_steps(w):
            r_recv(h, w).wait_recv()
            if h + 1 <= r_steps(w):
                r_copy(h + 1, w).start()
        if h <= l_steps(w):
            l_recv(h, w).wait_recv()
            if h + 1 <= l_steps(w):
                l_copy(h + 1, w).start()

    loads[0].wait()
    loads[1].wait()
    b_copy(b_block(y), BYP, yp).start()
    b_copy(b_block(y), BYM, ym).start()
    loads[2].wait()
    z_start(1)

    loads[3].wait()

    def norm_rows(i, _):
        r = pl.ds(pl.multiple_of(i * 16, 16), 16)
        x = hid[r, :].astype(F32)
        sq = x * x
        part = sq[:, 0:HEAD]
        for j in range(1, D // HEAD):
            part = part + sq[:, j * HEAD:(j + 1) * HEAD]
        innp[r, :] = part
        factor = lax.rsqrt(jnp.sum(part, axis=-1, keepdims=True) * (1.0 / D) + norm_eps)
        normed[r, :] = (x * factor * ag_ref[...]).astype(BF16)
        return 0

    lax.fori_loop(0, ROWS // 16, norm_rows, 0)

    cos = cos_ref[...]
    sin = sin_ref[...]

    def rope(u):
        return u * cos + pltpu.roll(u, HEAD // 2, 1) * sin

    loads[4].wait()
    loads[5].wait()
    kv_all = jnp.dot(normed[...], kvw[...], preferred_element_type=F32)
    kb = kb_ref[pl.ds(kvi, 1), :]
    vb = vb_ref[pl.ds(kvi, 1), :]
    for sq in range(2):
        kk = kv_all[sq * TOK:(sq + 1) * TOK, 0:HEAD] + kb
        vv = kv_all[sq * TOK:(sq + 1) * TOK, HEAD:2 * HEAD] + vb
        kv[y, z, c, sq, :, 0:HEAD] = rope(kk).astype(BF16)
        kv[y, z, c, sq, :, HEAD:2 * HEAD] = vv.astype(BF16)

    loads[6].wait()
    q_all = jnp.dot(normed[...], qw[...], preferred_element_type=F32) + qb_ref[...]
    for sq in range(2):
        for h in range(OWN_HEADS):
            u = q_all[sq * TOK:(sq + 1) * TOK, h * HEAD:(h + 1) * HEAD]
            qbuf[sq, h * TOK:(h + 1) * TOK, :] = rope(u).astype(BF16)

    z_start(0)
    yp_copy(0, 0, z).start()
    ym_copy(0, 0, z).start()

    b_copy(b_block(y - 1), BYP, yp).wait_recv()
    b_copy(b_block(y - 1, 0), BHP, yp).start()
    b_copy(b_block(y + 1), BYM, ym).wait_recv()
    b_copy(b_block(y + 1, 1), BHM, ym).start()

    z_hop(1, 1, False)
    z_hop(0, 1, True)
    z_hop(1, 2, False)
    z_hop(0, 2, True)
    z_hop(1, 3, False)
    z_hop(0, 3, True)
    z_hop(1, 4, False)
    z_hop(0, 4, True)

    b_copy(b_block(y + 2, 0), BHP, yp).wait_recv()
    b_copy(b_block(y + 2, 1), BHM, ym).wait_recv()
    for w in range(2):
        r_copy(1, w).start()
        l_copy(1, w).start()
    bd_copy(0).start()

    for sq in range(2):
        mbuf[sq] = jnp.full((OWN_HEADS * TOK, HEAD), masked_score, F32)
        lbuf[sq] = jnp.zeros((OWN_HEADS * TOK, HEAD), F32)
        accbuf[sq] = jnp.zeros((OWN_HEADS * TOK, HEAD), F32)

    def attend(sq, yk, zk, diagonal):
        pair = kv[yk, zk, :, sq]
        kb_ = pair[:, :, 0:HEAD].reshape(2 * TOK, HEAD)
        vb_ = pair[:, :, HEAD:2 * HEAD].reshape(2 * TOK, HEAD)
        sc = lax.dot_general(qbuf[sq], kb_, (((1,), (1,)), ((), ())), preferred_element_type=F32)
        if diagonal:
            row = lax.rem(lax.broadcasted_iota(jnp.int32, sc.shape, 0), TOK) + c * TOK
            col = lax.broadcasted_iota(jnp.int32, sc.shape, 1)
            sc = jnp.where(col <= row, sc, masked_score)
        m_old = mbuf[sq]
        m_new = jnp.maximum(m_old, jnp.max(sc, axis=1, keepdims=True))
        p = jnp.exp2((sc - jnp.concatenate([m_new, m_new], axis=1)) * EXP2_SCALE)
        alpha = jnp.exp2((m_old - m_new) * EXP2_SCALE)
        mbuf[sq] = m_new
        lbuf[sq] = lbuf[sq] * alpha + jnp.sum(p, axis=1, keepdims=True)
        accbuf[sq] = accbuf[sq] * alpha + jnp.dot(p.astype(BF16), vb_, preferred_element_type=F32)

    def attend_round(k):
        zk = wrap(zk_of(k), NZ)

        @pl.when(k == 0)
        def _():
            for sq in range(2):
                attend(sq, y, zk, True)

        def step(yk, _):
            for sq in range(2):
                attend(sq, yk, zk, False)
            return 0

        lax.fori_loop(0, y + jnp.where(zk < z, 1, 0), step, 0)

    def kv_round(k, _):
        @pl.when(k < NZ)
        def _():
            zk = zk_of(k)
            yp_recv(0, k, zk).wait_recv()
            hp_copy(0, k, zk).start()
            ym_recv(0, k, zk).wait_recv()
            hm_copy(0, k, zk).start()

        @pl.when((k >= 1) & (k < NZ + 1))
        def _():
            zk = zk_of(k - 1)
            hp_recv(0, k - 1, zk).wait_recv()
            hm_recv(0, k - 1, zk).wait_recv()
            d_copy(0, k - 1, zk).start()

        @pl.when(k >= 2)
        def _():
            d_recv(0, k - 2, zk_of(k - 2)).wait_recv()
            attend_round(k - 2)

        return 0

    lax.fori_loop(0, NZ + 2, kv_round, 0)

    def gate_send(k, _):
        yp_copy(1, k, zk_of(k)).start()
        ym_copy(1, k, zk_of(k)).start()
        return 0

    lax.fori_loop(0, NZ, gate_send, 0)
    b_hop(1, 0)
    b_hop(1, 1)
    bd_copy(1).start()
    bd_copy(2).start()

    for sq in range(2):
        for h in range(OWN_HEADS):
            r = slice(h * TOK, (h + 1) * TOK)
            attn[sq * TOK:(sq + 1) * TOK, h * HEAD:(h + 1) * HEAD] = (
                accbuf[sq, r, :] / lbuf[sq, r, :]
            ).astype(BF16)
    for q in range(MP):
        loads[8 + q].wait()

    def x_copy(ph, j, dst_buf):
        return rcx(stage.at[ph, j], dst_buf.at[m], x_send.at[ph, j], x_recv.at[ph, j], wrap(m + j, MP))

    def x_recv_of(ph, j, dst_buf):
        src = wrap(m - j, MP)
        return rcx(dst_buf.at[src], dst_buf.at[src], x_send.at[ph, j], x_recv.at[ph, j], src)

    for j in (2, 1, 3, 0):
        q = wrap(m + j, MP)
        part = jnp.dot(attn[...], ow[q], preferred_element_type=F32).astype(BF16)
        if j == 0:
            rs1[m] = part
        else:
            stage[0, j] = part
    for j in (2, 1, 3):
        x_copy(0, j, rs1).start()

    def gate_round(k, _):
        zk = zk_of(k)
        yp_recv(1, k, zk).wait_recv()
        hp_copy(1, k, zk).start()
        ym_recv(1, k, zk).wait_recv()
        hm_copy(1, k, zk).start()
        return 0

    lax.fori_loop(0, NZ // 2, gate_round, 0)
    b_hop(2, 0)

    loads[7].wait()
    for j in (1, 3, 2):
        x_recv_of(0, j, rs1).wait_recv()
    total = hidq[...].astype(F32)
    add = rs1[0].astype(F32)
    for q in range(1, MP):
        add = add + rs1[q].astype(F32)
    resid[m] = (total + add).astype(BF16)
    b_hop(2, 1)
    bd_copy(3).start()
    bd_copy(4).start()
    lax.fori_loop(NZ // 2, NZ, gate_round, 0)

    def ag_copy(j):
        return rcx(resid.at[m], resid.at[m], x_send.at[1, j], x_recv.at[1, j], wrap(m + j, MP))

    for j in (2, 1, 3):
        ag_copy(j).start()

    def gate_last(k, _):
        zk = zk_of(k)
        hp_recv(1, k, zk).wait_recv()
        hm_recv(1, k, zk).wait_recv()
        d_copy(1, k, zk).start()
        return 0

    lax.fori_loop(0, NZ, gate_last, 0)
    b_hop(3, 0)
    b_hop(3, 1)
    bd_copy(5).start()
    bd_copy(6).start()
    for j in (1, 3, 2):
        x_recv_of(1, j, resid).wait_recv()

    def norm2_rows(i, _):
        r = pl.ds(pl.multiple_of(i * 16, 16), 16)
        xs = [resid[q, r, :].astype(F32) for q in range(MP)]
        part = None
        for x in xs:
            sq = x * x
            for j in range(QUART // HEAD):
                t = sq[:, j * HEAD:(j + 1) * HEAD]
                part = t if part is None else part + t
        factor = lax.rsqrt(jnp.sum(part, axis=-1, keepdims=True) * (1.0 / D) + norm_eps)
        for q in range(MP):
            cols = slice(q * QUART, (q + 1) * QUART)
            mlp_in[r, cols] = (xs[q] * factor * mg_ref[:, cols]).astype(BF16)
        return 0

    lax.fori_loop(0, ROWS // 16, norm2_rows, 0)

    def gate_in(k, _):
        d_recv(1, k, zk_of(k)).wait_recv()
        return 0

    lax.fori_loop(0, NZ, gate_in, 0)
    gbuf[...] = jnp.dot(mlp_in[...], gate[...].reshape(D, FFP), preferred_element_type=F32)
    b_hop(4, 0)
    b_hop(4, 1)
    bd_copy(7).start()
    for k in range(NZ):
        bd_recv(k).wait_recv()
    up_sum = jnp.dot(mlp_in[...], ud[:, :, :, 0].reshape(D, FFP), preferred_element_type=F32)
    g = gbuf[...]
    act[...] = (g / (1.0 + jnp.exp(-g)) * up_sum).astype(BF16)

    for j in (2, 1, 3, 0):
        q = wrap(m + j, MP)
        rows = ud[q, :, :, 1].reshape(QUART, FFP)
        part = lax.dot_general(
            act[...], rows, (((1,), (1,)), ((), ())), preferred_element_type=F32
        ).astype(BF16)
        if j == 0:
            rs2[m] = part
        else:
            stage[1, j] = part
            rcx(stage.at[1, j], rs2.at[m], x_send.at[2, j], x_recv.at[2, j], q).start()

    def stream_done(k, _):
        for st in range(2):
            yp_copy(st, k, zk_of(k)).wait_send()
            ym_copy(st, k, zk_of(k)).wait_send()
            hp_copy(st, k, zk_of(k)).wait_send()
            hm_copy(st, k, zk_of(k)).wait_send()
            d_copy(st, k, zk_of(k)).wait_send()
        return 0

    lax.fori_loop(0, NZ, stream_done, 0)
    for st in range(2):
        for k in range(1, NZ):
            z_copy(st, k, 0, True).wait_send()
    b_copy(b_block(y), BYP, yp).wait_send()
    b_copy(b_block(y), BYM, ym).wait_send()
    b_copy(b_block(y, 0), BHP, yp).wait_send()
    b_copy(b_block(y, 1), BHM, ym).wait_send()
    for w in range(2):
        for i in range(1, r_steps(w) + 1):
            r_copy(i, w).wait_send()
        for i in range(1, l_steps(w) + 1):
            l_copy(i, w).wait_send()
    for k in range(NZ):
        bd_copy(k).wait_send()
    for j in (1, 2, 3):
        x_copy(0, j, rs1).wait_send()
        ag_copy(j).wait_send()

    def lane_sums(part):
        return jnp.sum(part.T, axis=0, keepdims=True)

    in_norm = lane_sums(innp[...])

    def x2_recv(j):
        src = wrap(m - j, MP)
        return rcx(rs2.at[src], rs2.at[src], x_send.at[2, j], x_recv.at[2, j], src)

    for j in (1, 3, 2):
        x2_recv(j).wait_recv()

    add = rs2[0].astype(F32)
    for q in range(1, MP):
        add = add + rs2[q].astype(F32)
    layer = (resid[m].astype(F32) + add).astype(BF16)
    out_ref[...] = layer
    wide = layer.astype(F32)
    cp = hidq[...].astype(F32) * wide
    op = wide * wide
    cpart, opart = cp[:, 0:HEAD], op[:, 0:HEAD]
    for j in range(1, QUART // HEAD):
        cols = slice(j * HEAD, (j + 1) * HEAD)
        cpart = cpart + cp[:, cols]
        opart = opart + op[:, cols]
    rowi = lax.broadcasted_iota(jnp.int32, (8, ROWS), 0)
    sums[m] = jnp.where(rowi == 0, lane_sums(cpart), lane_sums(opart))

    def s_copy(j):
        return rcx(sums.at[m], sums.at[m], t_send.at[0, j], t_recv.at[0, j], wrap(m + j, MP))

    def s_recv(j):
        src = wrap(m - j, MP)
        return rcx(sums.at[src], sums.at[src], t_send.at[0, j], t_recv.at[0, j], src)

    for j in (2, 1, 3):
        s_copy(j).start()
    for j in (1, 3, 2):
        s_recv(j).wait_recv()
    both = sums[0] + sums[1] + sums[2] + sums[3]
    cross, out_norm = both[0:1, :], both[1:2, :]
    cosine = cross / jnp.sqrt((in_norm + norm_eps) * (out_norm + norm_eps))
    lane = lax.broadcasted_iota(jnp.int32, (1, ROWS), 1)
    pos = s * TOK + lax.rem(lane, TOK)
    limit = jnp.where(lane < TOK, len_ref[0], len_ref[1])
    influence = jnp.where(pos < limit, 1.0 - cosine, 0.0)
    infl_ref[0:1, :] = influence[:, 0:TOK]
    infl_ref[1:2, :] = influence[:, TOK:2 * TOK]
    t0 = jnp.sum(influence[:, 0:TOK], axis=1, keepdims=True)
    t1 = jnp.sum(influence[:, TOK:2 * TOK], axis=1, keepdims=True)
    row = lax.broadcasted_iota(jnp.int32, (8, HEAD), 0)
    i1 = lax.rem(s, 2 * NZ)
    tot1[i1] = jnp.where(row == 0, t0, t1)

    def t1_copy(i):
        return rc(tot1.at[i1], tot1.at[i1], t_send.at[1, i], t_recv.at[1, i],
                  y * (2 * NZ) + lax.rem(i1 + i, 2 * NZ))

    def t1_recv(i):
        src = lax.rem(i1 + 2 * NZ - i, 2 * NZ)
        return rc(tot1.at[src], tot1.at[src], t_send.at[1, i], t_recv.at[1, i], y * (2 * NZ) + src)

    def t1_start(i, _):
        t1_copy(i).start()
        return 0

    def t1_wait(i, _):
        t1_recv(i).wait_recv()
        t1_copy(i).wait_send()
        return 0

    lax.fori_loop(1, 2 * NZ, t1_start, 0)
    lax.fori_loop(1, 2 * NZ, t1_wait, 0)
    acc = tot1[0]
    for i in range(1, 2 * NZ):
        acc = acc + tot1[i]
    tot2[y] = acc

    def t2_copy(i):
        return rc(tot2.at[y], tot2.at[y], t_send.at[2, i], t_recv.at[2, i], dev(y + i, z, c))

    def t2_recv(i):
        src = wrap(y - i, NY)
        return rc(tot2.at[src], tot2.at[src], t_send.at[2, i], t_recv.at[2, i], dev(y - i, z, c))

    for i in range(1, NY):
        t2_copy(i).start()
    for i in range(1, NY):
        t2_recv(i).wait_recv()
        t2_copy(i).wait_send()
    acc = tot2[0] + tot2[1] + tot2[2] + tot2[3]
    tokens = jnp.where(row == 0, len_ref[0], len_ref[1]).astype(F32)
    score_ref[...] = acc / tokens

    for j in (1, 2, 3):
        rcx(stage.at[1, j], rs2.at[m], x_send.at[2, j], x_recv.at[2, j], wrap(m + j, MP)).wait_send()
        s_copy(j).wait_send()


def local(
    hidden_in, attn_gain, q_weight, q_bias, k_weight, k_bias, v_weight, v_bias, o_weight,
    mlp_gain, gate_weight, up_weight, down_weight, lengths,
):
    seqs_n, tok_n, width = hidden_in.shape
    seq_rank = lax.axis_index("seq")
    positions = seq_rank * tok_n + jnp.arange(tok_n, dtype=jnp.int32)
    half_width = HEAD // 2
    inv_freq = rope_base ** (-(jnp.arange(half_width, dtype=jnp.float32) * 2.0) / HEAD)
    angles = positions.astype(jnp.float32)[:, None] * inv_freq[None, :]
    cos = jnp.cos(angles)
    sin = jnp.sin(angles)
    cos_t = jnp.concatenate([cos, cos], axis=-1)
    sin_t = jnp.concatenate([-sin, sin], axis=-1)

    hbm = pl.BlockSpec(memory_space=pltpu.HBM)
    vmem = pl.BlockSpec(memory_space=pltpu.VMEM)
    smem = pl.BlockSpec(memory_space=pltpu.SMEM)
    dma = pltpu.SemaphoreType.DMA
    layer_part, influence, score = pl.pallas_call(
        layer_kernel,
        out_shape=(
            jax.ShapeDtypeStruct((ROWS, QUART), BF16),
            jax.ShapeDtypeStruct((2, TOK), F32),
            jax.ShapeDtypeStruct((8, HEAD), F32),
        ),
        in_specs=[
            hbm, vmem, hbm, vmem, hbm, vmem, hbm, vmem, hbm, vmem,
            hbm, hbm, hbm, vmem, vmem, smem,
        ],
        out_specs=(vmem, vmem, vmem),
        scratch_shapes=[
            pltpu.VMEM((ROWS, D), BF16),
            pltpu.VMEM((ROWS, QUART), BF16),
            pltpu.VMEM((ROWS, D), BF16),
            pltpu.VMEM((D, QCOLS), BF16),
            pltpu.VMEM((D, 2 * HEAD), BF16),
            pltpu.VMEM((MP, QCOLS, QUART), BF16),
            pltpu.VMEM((2, OWN_HEADS * TOK, HEAD), BF16),
            pltpu.VMEM((NY, NZ, 2, 2, TOK, 2 * HEAD), BF16),
            pltpu.VMEM((NY, NZ, 2, WR, FFP), BF16),
            pltpu.VMEM((NY, NZ, 2, 2, WR, FFP), BF16),
            pltpu.VMEM((2, OWN_HEADS * TOK, HEAD), F32),
            pltpu.VMEM((2, OWN_HEADS * TOK, HEAD), F32),
            pltpu.VMEM((2, OWN_HEADS * TOK, HEAD), F32),
            pltpu.VMEM((ROWS, QCOLS), BF16),
            pltpu.VMEM((2, MP, ROWS, QUART), BF16),
            pltpu.VMEM((MP, ROWS, QUART), BF16),
            pltpu.VMEM((MP, ROWS, QUART), BF16),
            pltpu.VMEM((MP, ROWS, QUART), BF16),
            pltpu.VMEM((ROWS, D), BF16),
            pltpu.VMEM((ROWS, FFP), BF16),
            pltpu.VMEM((ROWS, HEAD), F32),
            pltpu.VMEM((MP, 8, ROWS), F32),
            pltpu.VMEM((2 * NZ, 8, HEAD), F32),
            pltpu.VMEM((NY, 8, HEAD), F32),
            pltpu.VMEM((ROWS, FFP), F32),
            dma((12,)),
            dma((2, 6, NZ)),
            dma((2, 6, NZ)),
            dma((28,)),
            dma((28,)),
            dma((3, MP)),
            dma((3, MP)),
            dma((3, 2 * NZ)),
            dma((3, 2 * NZ)),
        ],
        compiler_params=pltpu.CompilerParams(
            collective_id=0, has_side_effects=True, vmem_limit_bytes=62 * 1024 * 1024
        ),
        name="layer",
    )(
        hidden_in.reshape(ROWS, width), attn_gain.reshape(1, width), q_weight,
        q_bias.reshape(1, QCOLS), k_weight, k_bias.reshape(KV_HEADS, HEAD), v_weight,
        v_bias.reshape(KV_HEADS, HEAD), o_weight, mlp_gain.reshape(1, width), gate_weight,
        up_weight, down_weight, cos_t, sin_t, lengths,
    )
    return layer_part.reshape(seqs_n, tok_n, QUART), influence, score[0:2, 0]


def solution(mesh):
    placed = (
        P(None, "seq", None), P(), P(None, "mp"), P("mp"), P(), P(), P(), P(),
        P("mp", None), P(), P("seq", "mp"), P("seq", "mp"), P("seq", "mp"), P(),
    )
    return jax.shard_map(
        local, mesh=mesh, in_specs=placed,
        out_specs=(P(None, "seq", "mp"), P(None, "seq"), P()), check_vma=False,
    )
```

time: 337 us -> 146 us (0.43)
  waiting for transfers between devices: 167 us -> 0 us
  Pallas kernels: 0 us -> 140 us
  matrix products: 55.3 us -> 0 us
  blocking collectives: 52.1 us -> 0 us
  other arithmetic: 31.8 us -> 1.08 us
  between operations: 14 us -> 0.66 us
  starting transfers between devices: 7.61 us -> 0 us
  local copies, waits for them, and re-layouts: 7.89 us -> 4.17 us
    all_gather x3 -> x0, waiting for transfers between devices: 147 us -> none  [the longest x2 79.4 us: in_one_piece(): lax.all_gather(both, axis, axis=dim, tiled=True)]
    pallas_call x0 -> x1, Pallas kernels: none -> 140 us  [local(): pl.pallas_call(layer_kernel, out_shape=(jax.ShapeDtypeStruct((ROWS, QUART...]
    dot_general x8 -> x0, matrix products: 55.3 us -> none  [the longest x1 17.3 us: attend_update(): jnp.einsum('shqk,skd->shqd', weights.astype(jnp.bfloat16), value_piece, p...]
    all_to_all x3 -> x0, blocking collectives: 52.1 us -> none  [the longest x2 33.7 us: sent_to_all(): lax.all_to_all(jnp.broadcast_to(shard[None], (length, *shard.shape)), axi...]
    reduce_sum x9 -> x0, other arithmetic: 20.7 us -> none  [the longest x1 15.6 us: attend_update(): new_sum = jnp.sum(weights, axis=-1)]
    all_to_all x2 -> x0, waiting for transfers between devices: 19 us -> none  [the longest x1 14.8 us: sent_and_summed(): lax.all_to_all(parts, axis, split_axis=0, concat_axis=0, tiled=True)]
    all_to_all x2 -> x0, starting transfers between devices: 7.49 us -> none  [the longest x1 4.24 us: sent_and_summed(): lax.all_to_all(parts, axis, split_axis=0, concat_axis=0, tiled=True)]
    convert_element_type x6 -> x1, other arithmetic: 4.89 us -> 0.01 us  [local(): angles = positions.astype(jnp.float32)[:, None] * inv_freq[None, :]]
  transfers between devices with their start and end apart: 5 -> 0, of which waited for: 4 -> 0; matrix products, arithmetic and copies ran while one was open for 21% -> 0% of each run, Pallas kernels for 0% -> 0%
where the time goes in v1:
time: 146 us
  Pallas kernels  140 us (96%)
  local copies, waits for them, and re-layouts  4.17 us (3%)
    pallas_call x1, Pallas kernels, local(): pl.pallas_call(layer_kernel, out_shape=(jax.ShapeDtypeStruct((ROWS, QUART...  140 us

profile of v1, /device:TPU:1, one launch (start us, length us, event | category | flops | bytes accessed | tf_op | source)
XLA Modules:
  0.0 145.9 jit_solution(7955163596017229477)
XLA Ops:
  0.7 0.3 fusion
  1.0 0.8 pad_maximum_fusion
  1.7 140.0 %layer.1 = (bf16[256,512]{1,0:T(8,128)(2,1)}, f32[2,128]{1,0:T(2,128)}, f32[8,128]{1,0:T(8,128)}) custom-call(bf16[256,2048]{1,0:T(8,128)(2,1)} %bitcast.7, f32[1,2048]{1,0:T(1,128)} %bitcast.9, bf16[2048,512]{1,0:T(8,128)(2,1)} %qw_hbm.1, f32[1,512]{1,0:T(1,128)} %bitcast.11, bf16[2048,256]{1,0:T(8,128)(2,1)} %kw_hbm.1, f32[2,128]{1,0:T(2,128)} %bitcast.12, ...), custom_call_target="tpu_custom_call" | custom-call | tf_op jit(solution)/shard_map/layer/pallas_call | solution.py:636
  141.8 1.3 slice_reduce_fusion
  143.1 1.7 %copy.19 = bf16[2,128,512]{2,1,0:T(8,128)(2,1)} copy(bf16[2,128,512]{2,1,0:T(8,128)(2,1)} %bitcast.8) | data formatting | bytes 524288
  144.8 1.2 copy.20
  (2 shorter events, 0.0 us)

commit v2 on v1

v2 whole, which is shorter than its diff:
```python
import jax
import jax.numpy as jnp
from jax import lax
from jax.experimental import pallas as pl
from jax.experimental.pallas import tpu as pltpu
from jax.sharding import PartitionSpec as P

HEADS = 16
KV_HEADS = 2
HEAD = 128
D = 2048
NY, NZ = 4, 8
MP = 4
TOK = 128
ROWS = 2 * TOK
OWN_HEADS = HEADS // MP
QCOLS = OWN_HEADS * HEAD
QUART = D // MP
FFP = 1408
WR = 32
NS = NY * NZ * 2

rope_base = 1000000.0
norm_eps = 1e-06
masked_score = -1e30
EXP2_SCALE = HEAD ** (-0.5) * 1.4426950408889634

MESH = pl.DeviceIdType.MESH
F32, BF16 = jnp.float32, jnp.bfloat16

Z_OFF = (0, -1, 1, -2, 2, -3, 3, -4)


def layer_kernel(
    hid_hbm, ag_ref, qw_hbm, qb_ref, kw_hbm, kb_ref, vw_hbm, vb_ref, ow_hbm, mg_ref,
    gate_hbm, up_hbm, down_hbm, cos_ref, sin_ref, len_ref,
    out_hbm, infl_ref, score_ref,
    hid, hidq, normed, qw, kvw, ow, qbuf, kv, gate, up, down, mbuf, lbuf, accbuf, attn,
    stage1, rs1, resid, stage2, rs2, mlp_in, act, innp, sums, tot, gbuf, layer_v,
    lsem, osem, a_send, a_recv, b_send, b_recv, x_send, x_recv, r_send, r_recv,
    s_send, s_recv, t_send, t_recv,
):
    s = lax.axis_index("seq")
    m = lax.axis_index("mp")
    y = s // (2 * NZ)
    z = lax.rem(s // 2, NZ)
    c = lax.rem(s, 2)
    kvi = m // 2

    def wrap(v, n):
        return lax.rem(v + 2 * n, n)

    def dev(yy, zz, cc):
        return (wrap(yy, NY) * NZ + wrap(zz, NZ)) * 2 + cc

    zp, zm = dev(y, z + 1, c), dev(y, z - 1, c)
    yp, ym = dev(y + 1, z, c), dev(y - 1, z, c)
    partner = dev(y, z, 1 - c)

    def rc(src, dst, ssem, rsem, sdev):
        return pltpu.make_async_remote_copy(
            src_ref=src, dst_ref=dst, send_sem=ssem, recv_sem=rsem,
            device_id={"seq": sdev, "mp": m}, device_id_type=MESH,
        )

    def rcx(src, dst, ssem, rsem, mdev):
        return pltpu.make_async_remote_copy(
            src_ref=src, dst_ref=dst, send_sem=ssem, recv_sem=rsem,
            device_id={"seq": s, "mp": mdev}, device_id_type=MESH,
        )

    kv_cols = pl.ds(pl.multiple_of(kvi * HEAD, HEAD), HEAD)
    loads = [
        pltpu.make_async_copy(up_hbm, up.at[y, z, c], lsem.at[0]),
        pltpu.make_async_copy(gate_hbm, gate.at[y, z, c], lsem.at[1]),
        pltpu.make_async_copy(down_hbm, down.at[y, z, c], lsem.at[2]),
        pltpu.make_async_copy(hid_hbm, hid, lsem.at[3]),
        pltpu.make_async_copy(kw_hbm.at[:, kv_cols], kvw.at[:, pl.ds(0, HEAD)], lsem.at[4]),
        pltpu.make_async_copy(vw_hbm.at[:, kv_cols], kvw.at[:, pl.ds(HEAD, HEAD)], lsem.at[5]),
        pltpu.make_async_copy(qw_hbm, qw, lsem.at[6]),
        pltpu.make_async_copy(
            hid_hbm.at[:, pl.ds(pl.multiple_of(m * QUART, QUART), QUART)], hidq, lsem.at[7]),
    ] + [
        pltpu.make_async_copy(ow_hbm.at[:, pl.ds(q * QUART, QUART)], ow.at[q], lsem.at[8 + q])
        for q in range(MP)
    ]
    for copy in loads:
        copy.start()

    bar = pltpu.get_barrier_semaphore()
    for peer in (zp, zm, yp, ym, partner):
        pl.semaphore_signal(bar, inc=1, device_id={"seq": peer, "mp": m}, device_id_type=MESH)
    for i in range(1, MP):
        pl.semaphore_signal(bar, inc=1, device_id={"seq": s, "mp": wrap(m + i, MP)}, device_id_type=MESH)
    pl.semaphore_wait(bar, 5 + MP - 1)

    ZS, YPS, YMS, HPS, HMS, DS = range(6)
    A_HALF = (TOK // 2, WR // 2, WR // 2)
    ALL = slice(None)

    def a_ref(st, yy, zz, cc):
        if st == 0:
            return kv.at[0, yy, zz, cc]
        return (gate, down)[st - 1].at[yy, zz, cc]

    def block(st, yy, zz):
        return a_ref(st, wrap(yy, NY), wrap(zz, NZ), c)

    def half(st, ref, i):
        return ref.at[pl.ds(i * A_HALF[st], A_HALF[st])]

    def a_copy(ref, st, kind, k, d):
        return rc(ref, ref, a_send.at[st, kind, k], a_recv.at[st, kind, k], d)

    def zk_of(k):
        if isinstance(k, int):
            return z + Z_OFF[k]
        return z + jnp.where(lax.rem(k, 2) == 1, -((k + 1) // 2), k // 2)

    def z_copy(st, k_to, zz, right):
        return a_copy(block(st, y, zz), st, ZS, k_to, zp if right else zm)

    def y_send(st, k):
        ref = block(st, y, zk_of(k))
        a_copy(ref, st, YPS, k, yp).start()
        a_copy(ref, st, YMS, k, ym).start()

    def y_pass(st, k):
        zz = zk_of(k)
        ref = block(st, y - 1, zz)
        a_copy(ref, st, YPS, k, yp).wait_recv()
        a_copy(half(st, ref, 0), st, HPS, k, yp).start()
        ref = block(st, y + 1, zz)
        a_copy(ref, st, YMS, k, ym).wait_recv()
        a_copy(half(st, ref, 1), st, HMS, k, ym).start()

    def y_last(st, k):
        zz = zk_of(k)
        ref = block(st, y + 2, zz)
        a_copy(half(st, ref, 0), st, HPS, k, yp).wait_recv()
        a_copy(half(st, ref, 1), st, HMS, k, ym).wait_recv()
        a_copy(a_ref(st, ALL, wrap(zz, NZ), c), st, DS, k, partner).start()

    def a_wait(st, k):
        a_copy(a_ref(st, ALL, wrap(zk_of(k), NZ), 1 - c), st, DS, k, partner).wait_recv()

    def z_start(st):
        z_copy(st, 1, z, True).start()
        z_copy(st, 2, z, False).start()

    def z_hop(st, h, with_y=False):
        far_right = st != 1
        for k in (2 * h - 1, 2 * h):
            if k >= NZ:
                continue
            right = far_right if k == 7 else k % 2 == 1
            z_copy(st, k, zk_of(k), right).wait_recv()
            if k + 2 < NZ - 1:
                z_copy(st, k + 2, zk_of(k), right).start()
            if k == (5 if far_right else 6):
                z_copy(st, 7, zk_of(k), far_right).start()
            if with_y:
                y_send(st, k)

    BYP, BYM, BHP, BHM = range(4)
    RZ, LZ, DZ = 4, 12, 20
    B_HALF = (TOK // 2, WR // 2)

    def b_ref(st, yy, zz, cc):
        return kv.at[1, yy, zz, cc] if st == 0 else up.at[yy, zz, cc]

    def b_copy(st, ref, i, d):
        return rc(ref, ref, b_send.at[st, i], b_recv.at[st, i], d)

    def b_block(st, yy, w=None):
        ref = b_ref(st, wrap(yy, NY), z, c)
        return ref if w is None else ref.at[pl.ds(w * B_HALF[st], B_HALF[st])]

    def group(st, zz, w):
        rows = pl.ds(w * B_HALF[st], B_HALF[st])
        if st == 0:
            return kv.at[1, :, wrap(zz, NZ), c, rows]
        return up.at[:, wrap(zz, NZ), c, rows]

    def r_copy(st, i, w):
        return b_copy(st, group(st, z - (i - 1), w), RZ + 2 * (i - 1) + w, zp)

    def r_from(st, i, w):
        return b_copy(st, group(st, z - i, w), RZ + 2 * (i - 1) + w, zp)

    def l_copy(st, i, w):
        return b_copy(st, group(st, z + (i - 1), w), LZ + 2 * (i - 1) + w, zm)

    def l_from(st, i, w):
        return b_copy(st, group(st, z + i, w), LZ + 2 * (i - 1) + w, zm)

    def r_steps(w):
        return 4 if w == 0 else 3

    def l_steps(w):
        return 3 if w == 0 else 4

    def by_start(st):
        b_copy(st, b_block(st, y), BYP, yp).start()
        b_copy(st, b_block(st, y), BYM, ym).start()

    def by_pass(st):
        b_copy(st, b_block(st, y - 1), BYP, yp).wait_recv()
        b_copy(st, b_block(st, y - 1, 0), BHP, yp).start()
        b_copy(st, b_block(st, y + 1), BYM, ym).wait_recv()
        b_copy(st, b_block(st, y + 1, 1), BHM, ym).start()

    def by_last(st):
        b_copy(st, b_block(st, y + 2, 0), BHP, yp).wait_recv()
        b_copy(st, b_block(st, y + 2, 1), BHM, ym).wait_recv()

    def bz_start(st):
        for w in range(2):
            r_copy(st, 1, w).start()
            l_copy(st, 1, w).start()

    def bd_start(st, k):
        b_copy(st, b_ref(st, ALL, wrap(zk_of(k), NZ), c), DZ + k, partner).start()

    def b_wait(st, k):
        b_copy(st, b_ref(st, ALL, wrap(zk_of(k), NZ), 1 - c), DZ + k, partner).wait_recv()

    def b_hop(st, h, w):
        if h <= r_steps(w):
            r_from(st, h, w).wait_recv()
            if h + 1 <= r_steps(w):
                r_copy(st, h + 1, w).start()
        if h <= l_steps(w):
            l_from(st, h, w).wait_recv()
            if h + 1 <= l_steps(w):
                l_copy(st, h + 1, w).start()
        if w == 1:
            for k in (2 * h - 1, 2 * h):
                if k < NZ:
                    bd_start(st, k)

    loads[0].wait()
    by_start(1)
    loads[1].wait()
    z_start(1)

    loads[3].wait()

    def norm_rows(i, _):
        r = pl.ds(pl.multiple_of(i * 16, 16), 16)
        x = hid[r, :].astype(F32)
        sq = x * x
        part = sq[:, 0:HEAD]
        for j in range(1, D // HEAD):
            part = part + sq[:, j * HEAD:(j + 1) * HEAD]
        innp[r, :] = part
        factor = lax.rsqrt(jnp.sum(part, axis=-1, keepdims=True) * (1.0 / D) + norm_eps)
        normed[r, :] = (x * factor * ag_ref[...]).astype(BF16)
        return 0

    lax.fori_loop(0, ROWS // 16, norm_rows, 0, unroll=4)

    cos = cos_ref[...]
    sin = sin_ref[...]

    def rope(u):
        return u * cos + pltpu.roll(u, HEAD // 2, 1) * sin

    loads[4].wait()
    loads[5].wait()
    kv_all = jnp.dot(normed[...], kvw[...], preferred_element_type=F32)
    kb = kb_ref[pl.ds(kvi, 1), :]
    vb = vb_ref[pl.ds(kvi, 1), :]
    for sq in range(2):
        kk = kv_all[sq * TOK:(sq + 1) * TOK, 0:HEAD] + kb
        vv = kv_all[sq * TOK:(sq + 1) * TOK, HEAD:2 * HEAD] + vb
        kv[sq, y, z, c, :, 0:HEAD] = rope(kk).astype(BF16)
        kv[sq, y, z, c, :, HEAD:2 * HEAD] = vv.astype(BF16)

    loads[6].wait()
    q_all = jnp.dot(normed[...], qw[...], preferred_element_type=F32) + qb_ref[...]
    for sq in range(2):
        for h in range(OWN_HEADS):
            u = q_all[sq * TOK:(sq + 1) * TOK, h * HEAD:(h + 1) * HEAD]
            qbuf[sq, h * TOK:(h + 1) * TOK, :] = rope(u).astype(BF16)

    for sq in range(2):
        mbuf[sq] = jnp.full((OWN_HEADS * TOK, HEAD), masked_score, F32)
        lbuf[sq] = jnp.zeros((OWN_HEADS * TOK, HEAD), F32)
        accbuf[sq] = jnp.zeros((OWN_HEADS * TOK, HEAD), F32)

    def attend(sq, yks, zk, diagonal):
        pairs = [kv[sq, yk, zk] for yk in yks]
        kb_ = jnp.concatenate([p[:, :, 0:HEAD].reshape(2 * TOK, HEAD) for p in pairs], axis=0)
        vb_ = jnp.concatenate([p[:, :, HEAD:2 * HEAD].reshape(2 * TOK, HEAD) for p in pairs], axis=0)
        sc = lax.dot_general(qbuf[sq], kb_, (((1,), (1,)), ((), ())), preferred_element_type=F32)
        if diagonal:
            row = lax.rem(lax.broadcasted_iota(jnp.int32, sc.shape, 0), TOK) + c * TOK
            col = lax.broadcasted_iota(jnp.int32, sc.shape, 1)
            sc = jnp.where(col <= row, sc, masked_score)
        m_old = mbuf[sq]
        m_new = jnp.maximum(m_old, jnp.max(sc, axis=1, keepdims=True))
        p = jnp.exp2((sc - jnp.concatenate([m_new] * (2 * len(yks)), axis=1)) * EXP2_SCALE)
        alpha = jnp.exp2((m_old - m_new) * EXP2_SCALE)
        mbuf[sq] = m_new
        lbuf[sq] = lbuf[sq] * alpha + jnp.sum(p, axis=1, keepdims=True)
        accbuf[sq] = accbuf[sq] * alpha + jnp.dot(p.astype(BF16), vb_, preferred_element_type=F32)

    def attend_round(sq, k):
        zk = wrap(zk_of(k), NZ)

        @pl.when(k == 0)
        def _():
            attend(sq, (y,), zk, True)

        n = y + jnp.where(zk < z, 1, 0)

        def step(i, _):
            attend(sq, (2 * i, 2 * i + 1), zk, False)
            return 0

        lax.fori_loop(0, n // 2, step, 0)

        @pl.when(lax.rem(n, 2) == 1)
        def _():
            attend(sq, (n - 1,), zk, False)

    def seq_rows(sq):
        return pl.ds(sq * TOK, TOK)

    def rs1_send(sq, j):
        return rcx(stage1.at[sq, j], rs1.at[m, seq_rows(sq)], x_send.at[0, sq, j],
                   x_recv.at[0, sq, j], wrap(m + j, MP))

    def rs1_recv(sq, j):
        ref = rs1.at[wrap(m - j, MP), seq_rows(sq)]
        return rcx(ref, ref, x_send.at[0, sq, j], x_recv.at[0, sq, j], wrap(m - j, MP))

    def o_project(sq):
        if sq == 0:
            for q in range(MP):
                loads[8 + q].wait()
        for h in range(OWN_HEADS):
            r = slice(h * TOK, (h + 1) * TOK)
            attn[sq * TOK:(sq + 1) * TOK, h * HEAD:(h + 1) * HEAD] = (
                accbuf[sq, r, :] / lbuf[sq, r, :]
            ).astype(BF16)
        here = attn[sq * TOK:(sq + 1) * TOK, :]
        for j in (2, 1, 3, 0):
            part = jnp.dot(here, ow[wrap(m + j, MP)], preferred_element_type=F32).astype(BF16)
            if j == 0:
                rs1[m, seq_rows(sq), :] = part
            else:
                stage1[sq, j] = part
        for j in (2, 1, 3):
            rs1_send(sq, j).start()

    def ag_send(sq, j):
        ref = resid.at[m, seq_rows(sq)]
        return rcx(ref, ref, x_send.at[1, sq, j], x_recv.at[1, sq, j], wrap(m + j, MP))

    def ag_recv(sq, j):
        ref = resid.at[wrap(m - j, MP), seq_rows(sq)]
        return rcx(ref, ref, x_send.at[1, sq, j], x_recv.at[1, sq, j], wrap(m - j, MP))

    def residual(sq):
        if sq == 0:
            loads[7].wait()
        for j in (1, 3, 2):
            rs1_recv(sq, j).wait_recv()
        r = seq_rows(sq)
        add = rs1[0, r, :].astype(F32)
        for q in range(1, MP):
            add = add + rs1[q, r, :].astype(F32)
        resid[m, r, :] = (hidq[r, :].astype(F32) + add).astype(BF16)
        for j in (2, 1, 3):
            ag_send(sq, j).start()

    def second_norm(sq):
        for j in (1, 3, 2):
            ag_recv(sq, j).wait_recv()

        def norm2_rows(i, _):
            r = pl.ds(pl.multiple_of(sq * TOK + i * 16, 16), 16)
            xs = [resid[q, r, :].astype(F32) for q in range(MP)]
            part = None
            for x in xs:
                sqr = x * x
                for j in range(QUART // HEAD):
                    t = sqr[:, j * HEAD:(j + 1) * HEAD]
                    part = t if part is None else part + t
            factor = lax.rsqrt(jnp.sum(part, axis=-1, keepdims=True) * (1.0 / D) + norm_eps)
            for q in range(MP):
                cols = slice(q * QUART, (q + 1) * QUART)
                mlp_in[r, cols] = (xs[q] * factor * mg_ref[:, cols]).astype(BF16)
            return 0

        lax.fori_loop(0, TOK // 16, norm2_rows, 0, unroll=4)

    def gate_dot():
        for k in range(NZ):
            a_wait(1, k)
        gbuf[...] = jnp.dot(mlp_in[...], gate[...].reshape(D, FFP), preferred_element_type=F32)

    def up_dot():
        for k in range(NZ):
            b_wait(1, k)
        up_sum = jnp.dot(mlp_in[...], up[...].reshape(D, FFP), preferred_element_type=F32)
        g = gbuf[...]
        act[...] = (g / (1.0 + jnp.exp(-g)) * up_sum).astype(BF16)

    odd = lax.rem(z, 2)

    def z_pair(i):
        turn = (0, 2 * odd - 1, 1 - 2 * odd, 2)[i]
        return wrap(z // 2 + turn, NZ // 2)

    def rs2_send(i, j):
        q = wrap(m + j, MP)
        return rcx(stage2.at[i, q], rs2.at[i, m], r_send.at[i, j], r_recv.at[i, j], q)

    def rs2_recv(i, j):
        ref = rs2.at[i, wrap(m - j, MP)]
        return rcx(ref, ref, r_send.at[i, j], r_recv.at[i, j], wrap(m - j, MP))

    def down_stage(i):
        for k in ((0, 1, 2), (3, 4), (5, 6), (7,))[i]:
            a_wait(2, k)
        p = z_pair(i)
        for q0 in (0, 2):
            rows = down[q0:q0 + 2, pl.ds(2 * p, 2)].reshape(2 * HEAD, FFP)
            part = lax.dot_general(
                act[...], rows, (((1,), (1,)), ((), ())), preferred_element_type=F32
            ).astype(BF16)
            stage2[i, q0] = part[:, 0:HEAD]
            stage2[i, q0 + 1] = part[:, HEAD:2 * HEAD]
        for j in (2, 1, 3):
            rs2_send(i, j).start()

    def layer_stage(i, so_far):
        for j in (1, 3, 2):
            rs2_recv(i, j).wait_recv()
        cols = pl.ds(pl.multiple_of(z_pair(i) * HEAD, HEAD), HEAD)
        add = stage2[i, m].astype(F32)
        for j in range(1, MP):
            add = add + rs2[i, wrap(m - j, MP)].astype(F32)
        layer = (resid[m, :, cols].astype(F32) + add).astype(BF16)
        layer_v[:, cols] = layer
        wide = layer.astype(F32)
        cp, op = hidq[:, cols].astype(F32) * wide, wide * wide
        return (cp, op) if so_far is None else (so_far[0] + cp, so_far[1] + op)

    plan = []

    def at(time, act_, *args):
        plan.append((time, len(plan), act_, args))

    def kv_start():
        z_start(0)
        y_send(0, 0)
        by_start(0)
        loads[2].wait()
        z_start(2)

    at(3.2, kv_start)
    at(3.5, by_pass, 1)
    at(4.0, z_hop, 1, 1)
    at(6.5, z_hop, 0, 1, True)
    at(7.0, by_pass, 0)
    at(8.0, y_pass, 0, 0)
    at(9.5, z_hop, 0, 2, True)
    at(9.7, by_last, 0)
    at(9.71, bz_start, 0)
    at(9.72, bd_start, 0, 0)
    at(10.0, z_hop, 2, 1)
    at(10.1, z_hop, 1, 2)
    at(10.2, y_last, 0, 0)
    at(11.0, y_pass, 0, 1)
    at(11.1, y_pass, 0, 2)
    at(13.0, z_hop, 0, 3, True)
    at(13.5, y_last, 0, 1)
    at(13.6, y_last, 0, 2)
    at(14.0, y_pass, 0, 3)
    at(14.1, y_pass, 0, 4)
    at(16.0, b_hop, 0, 1, 0)
    at(16.5, z_hop, 0, 4, True)
    at(17.0, y_last, 0, 3)
    at(17.1, y_last, 0, 4)
    at(17.2, y_pass, 0, 5)
    at(17.3, y_pass, 0, 6)
    at(18.5, b_hop, 0, 1, 1)
    at(19.5, by_last, 1)
    at(19.6, bd_start, 1, 0)
    at(20.0, z_hop, 1, 3)
    at(20.1, z_hop, 2, 2)
    at(20.5, y_last, 0, 5)
    at(20.6, y_last, 0, 6)
    at(20.7, y_pass, 0, 7)
    at(21.5, b_hop, 0, 2, 0)
    for k in range(5):
        at(21.6 + k / 100, y_send, 1, k)
    at(22.0, y_last, 0, 7)
    at(24.0, b_hop, 0, 2, 1)
    at(26.6, o_project, 0)
    at(27.0, b_hop, 0, 3, 0)
    at(27.1, bz_start, 1)
    at(28.0, z_hop, 1, 4)
    for k in range(5, NZ):
        at(28.1 + k / 100, y_send, 1, k)
    at(29.5, b_hop, 0, 3, 1)
    at(30.0, z_hop, 2, 3)
    at(32.0, b_hop, 0, 4, 0)
    at(32.1, b_hop, 0, 4, 1)
    for i, (time, sq, k) in enumerate((
        (11.5, 0, 0), (12.0, 1, 0), (15.0, 0, 1), (15.1, 0, 2), (18.0, 0, 3), (18.1, 0, 4),
        (21.0, 1, 1), (21.1, 1, 2), (22.5, 0, 5), (22.6, 0, 6), (22.7, 0, 7),
        (26.0, 1, 3), (26.1, 1, 4), (31.0, 1, 5), (31.1, 1, 6), (34.0, 1, 7),
    )):
        at(time, "attend", sq, k)
    for k in range(NZ):
        at(27.5 + 2.6 * k, y_pass, 1, k)
        at(31.5 + 2.6 * k, y_last, 1, k)
    at(34.5, residual, 0)
    at(35.0, b_hop, 1, 1, 0)
    at(36.0, o_project, 1)
    at(37.0, z_hop, 2, 4)
    at(39.0, b_hop, 1, 1, 1)
    for k in range(NZ):
        at(39.0 + 1.5 * k, y_send, 2, k)
        at(49.0 + 2.6 * k, y_pass, 2, k)
        at(52.0 + 2.6 * k, y_last, 2, k)
    at(42.5, b_hop, 1, 2, 0)
    at(45.0, second_norm, 0)
    at(46.4, b_hop, 1, 2, 1)
    at(48.5, residual, 1)
    at(50.0, b_hop, 1, 3, 0)
    at(54.0, b_hop, 1, 3, 1)
    at(56.5, second_norm, 1)
    at(57.0, gate_dot)
    at(58.0, b_hop, 1, 4, 0)
    at(58.1, b_hop, 1, 4, 1)
    at(60.0, up_dot)
    at(60.5, down_stage, 0)
    at(63.0, down_stage, 1)
    at(68.6, down_stage, 2)
    at(72.0, down_stage, 3)

    plan.sort(key=lambda e: e[:2])
    items, before, after = [], [], []
    for _, _, act_, args in plan:
        if act_ == "attend":
            items.append(args)
            before.append(after)
            after = []
        else:
            after.append((act_, args))

    def run(events):
        for act_, args in events:
            act_(*args)

    def pick(t, values):
        total = 0
        for i, v in enumerate(values):
            if v:
                total = total + jnp.where(t == i, v, 0)
        return total

    def item(t, _):
        for i, events in enumerate(before):
            if events:
                pl.when(t == i)(lambda events=events: run(events))
        sq = pick(t, [e[0] for e in items])
        k = pick(t, [e[1] for e in items])

        @pl.when(sq == 0)
        def _():
            a_wait(0, k)

        @pl.when(sq == 1)
        def _():
            b_wait(0, k)

        attend_round(sq, k)
        return 0

    lax.fori_loop(0, len(items), item, 0)
    run(after)

    def sent(k, _):
        for st in range(3):
            ref = block(st, y, zk_of(k))
            a_copy(ref, st, YPS, k, yp).wait_send()
            a_copy(ref, st, YMS, k, ym).wait_send()
            a_copy(half(st, ref, 0), st, HPS, k, yp).wait_send()
            a_copy(half(st, ref, 1), st, HMS, k, ym).wait_send()
            a_copy(a_ref(st, ALL, wrap(zk_of(k), NZ), c), st, DS, k, partner).wait_send()
        for st in range(2):
            b_copy(st, b_ref(st, ALL, wrap(zk_of(k), NZ), c), DZ + k, partner).wait_send()
        return 0

    lax.fori_loop(0, NZ, sent, 0)
    for st in range(3):
        for k in range(1, NZ):
            z_copy(st, k, z, True).wait_send()
    for st in range(2):
        b_copy(st, b_block(st, y), BYP, yp).wait_send()
        b_copy(st, b_block(st, y), BYM, ym).wait_send()
        b_copy(st, b_block(st, y, 0), BHP, yp).wait_send()
        b_copy(st, b_block(st, y, 1), BHM, ym).wait_send()
        for w in range(2):
            for i in range(1, r_steps(w) + 1):
                r_copy(st, i, w).wait_send()
            for i in range(1, l_steps(w) + 1):
                l_copy(st, i, w).wait_send()
    for sq in range(2):
        for j in (1, 2, 3):
            rs1_send(sq, j).wait_send()
            ag_send(sq, j).wait_send()

    def lane_sums(part):
        return jnp.sum(part.T, axis=0, keepdims=True)

    in_norm = lane_sums(innp[...])

    so_far = None
    for i in range(4):
        so_far = layer_stage(i, so_far)
    out_copy = pltpu.make_async_copy(layer_v, out_hbm, osem.at[0])
    rowi = lax.broadcasted_iota(jnp.int32, (8, ROWS), 0)
    sums[m] = jnp.where(rowi == 0, lane_sums(so_far[0]), lane_sums(so_far[1]))

    def s_copy(j):
        return rcx(sums.at[m], sums.at[m], s_send.at[j], s_recv.at[j], wrap(m + j, MP))

    def s_from(j):
        src = wrap(m - j, MP)
        return rcx(sums.at[src], sums.at[src], s_send.at[j], s_recv.at[j], src)

    for j in (2, 1, 3):
        s_copy(j).start()
    out_copy.start()
    for j in (1, 3, 2):
        s_from(j).wait_recv()
    both = sums[0] + sums[1] + sums[2] + sums[3]
    cross, out_norm = both[0:1, :], both[1:2, :]
    cosine = cross / jnp.sqrt((in_norm + norm_eps) * (out_norm + norm_eps))
    lane = lax.broadcasted_iota(jnp.int32, (1, ROWS), 1)
    pos = s * TOK + lax.rem(lane, TOK)
    limit = jnp.where(lane < TOK, len_ref[0], len_ref[1])
    influence = jnp.where(pos < limit, 1.0 - cosine, 0.0)
    infl_ref[0:1, :] = influence[:, 0:TOK]
    infl_ref[1:2, :] = influence[:, TOK:2 * TOK]
    t0 = jnp.sum(influence[:, 0:TOK], axis=1, keepdims=True)
    t1 = jnp.sum(influence[:, TOK:2 * TOK], axis=1, keepdims=True)
    lane = lax.broadcasted_iota(jnp.int32, (1, HEAD), 1)
    one = pl.ds(0, 1)
    tot[s, one, :] = jnp.where(lane < HEAD // 2, t0, t1)

    def t_copy(i):
        ref = tot.at[s, one]
        return rc(ref, ref, t_send.at[0], t_recv.at[0], lax.rem(s + i, NS))

    def t_start(i, _):
        t_copy(i).start()
        return 0

    lax.fori_loop(1, NS, t_start, 0)
    every = tot.at[pl.ds(0, NS - 1), one]
    rc(every, every, t_send.at[0], t_recv.at[0], partner).wait()
    total = jnp.sum(tot[:, 0, :], axis=0, keepdims=True)
    tokens = jnp.where(lane < HEAD // 2, len_ref[0], len_ref[1]).astype(F32)
    score = total / tokens
    score_ref[0] = jnp.sum(jnp.where(lane == 0, score, 0.0))
    score_ref[1] = jnp.sum(jnp.where(lane == HEAD - 1, score, 0.0))

    for i in range(4):
        for j in (1, 2, 3):
            rs2_send(i, j).wait_send()
    for j in (1, 2, 3):
        s_copy(j).wait_send()
    out_copy.wait()


def finish_kernel(layer_hbm, infl_ref, score_ref, out_hbm, infl_out, score_out, buf, sem):
    into = pltpu.make_async_copy(layer_hbm, buf, sem.at[0])
    into.start()
    infl_out[...] = infl_ref[...]
    score_out[0] = score_ref[0]
    score_out[1] = score_ref[1]
    into.wait()
    out = pltpu.make_async_copy(buf, out_hbm, sem.at[1])
    out.start()
    out.wait()


def local(
    hidden_in, attn_gain, q_weight, q_bias, k_weight, k_bias, v_weight, v_bias, o_weight,
    mlp_gain, gate_weight, up_weight, down_weight, lengths,
):
    seqs_n, tok_n, width = hidden_in.shape
    seq_rank = lax.axis_index("seq")
    positions = seq_rank * tok_n + jnp.arange(tok_n, dtype=jnp.int32)
    half_width = HEAD // 2
    inv_freq = rope_base ** (-(jnp.arange(half_width, dtype=jnp.float32) * 2.0) / HEAD)
    angles = positions.astype(jnp.float32)[:, None] * inv_freq[None, :]
    cos = jnp.cos(angles)
    sin = jnp.sin(angles)
    cos_t = jnp.concatenate([cos, cos], axis=-1)
    sin_t = jnp.concatenate([-sin, sin], axis=-1)

    hbm = pl.BlockSpec(memory_space=pltpu.HBM)
    vmem = pl.BlockSpec(memory_space=pltpu.VMEM)
    smem = pl.BlockSpec(memory_space=pltpu.SMEM)
    dma = pltpu.SemaphoreType.DMA
    results = (
        jax.ShapeDtypeStruct((ROWS, QUART), BF16),
        jax.ShapeDtypeStruct((2, TOK), F32),
        jax.ShapeDtypeStruct((2,), F32),
    )
    layer_part, influence, score = pl.pallas_call(
        layer_kernel,
        out_shape=results,
        in_specs=[
            hbm, vmem, hbm, vmem, hbm, vmem, hbm, vmem, hbm, vmem,
            hbm, hbm, hbm, vmem, vmem, smem,
        ],
        out_specs=(hbm, vmem, smem),
        scratch_shapes=[
            pltpu.VMEM((ROWS, D), BF16),
            pltpu.VMEM((ROWS, QUART), BF16),
            pltpu.VMEM((ROWS, D), BF16),
            pltpu.VMEM((D, QCOLS), BF16),
            pltpu.VMEM((D, 2 * HEAD), BF16),
            pltpu.VMEM((MP, QCOLS, QUART), BF16),
            pltpu.VMEM((2, OWN_HEADS * TOK, HEAD), BF16),
            pltpu.VMEM((2, NY, NZ, 2, TOK, 2 * HEAD), BF16),
            pltpu.VMEM((NY, NZ, 2, WR, FFP), BF16),
            pltpu.VMEM((NY, NZ, 2, WR, FFP), BF16),
            pltpu.VMEM((NY, NZ, 2, WR, FFP), BF16),
            pltpu.VMEM((2, OWN_HEADS * TOK, HEAD), F32),
            pltpu.VMEM((2, OWN_HEADS * TOK, HEAD), F32),
            pltpu.VMEM((2, OWN_HEADS * TOK, HEAD), F32),
            pltpu.VMEM((ROWS, QCOLS), BF16),
            pltpu.VMEM((2, MP, TOK, QUART), BF16),
            pltpu.VMEM((MP, ROWS, QUART), BF16),
            pltpu.VMEM((MP, ROWS, QUART), BF16),
            pltpu.VMEM((4, MP, ROWS, HEAD), BF16),
            pltpu.VMEM((4, MP, ROWS, HEAD), BF16),
            pltpu.VMEM((ROWS, D), BF16),
            pltpu.VMEM((ROWS, FFP), BF16),
            pltpu.VMEM((ROWS, HEAD), F32),
            pltpu.VMEM((MP, 8, ROWS), F32),
            pltpu.VMEM((NS, 8, HEAD), F32),
            pltpu.VMEM((ROWS, FFP), F32),
            pltpu.VMEM((ROWS, QUART), BF16),
            dma((12,)),
            dma((1,)),
            dma((3, 6, NZ)),
            dma((3, 6, NZ)),
            dma((2, 28)),
            dma((2, 28)),
            dma((2, 2, MP)),
            dma((2, 2, MP)),
            dma((4, MP)),
            dma((4, MP)),
            dma((MP,)),
            dma((MP,)),
            dma((1,)),
            dma((1,)),
        ],
        compiler_params=pltpu.CompilerParams(
            collective_id=0, has_side_effects=True, vmem_limit_bytes=62 * 1024 * 1024
        ),
        name="layer",
    )(
        hidden_in.reshape(ROWS, width), attn_gain.reshape(1, width), q_weight,
        q_bias.reshape(1, QCOLS), k_weight, k_bias.reshape(KV_HEADS, HEAD), v_weight,
        v_bias.reshape(KV_HEADS, HEAD), o_weight, mlp_gain.reshape(1, width), gate_weight,
        up_weight, down_weight, cos_t, sin_t, lengths,
    )
    layer_part, influence, score = pl.pallas_call(
        finish_kernel,
        out_shape=results,
        in_specs=[hbm, vmem, smem],
        out_specs=(hbm, vmem, smem),
        scratch_shapes=[pltpu.VMEM((ROWS, QUART), BF16), dma((2,))],
        name="finish",
    )(layer_part, influence, score)
    return layer_part.reshape(seqs_n, tok_n, QUART), influence, score


def solution(mesh):
    placed = (
        P(None, "seq", None), P(), P(None, "mp"), P("mp"), P(), P(), P(), P(),
        P("mp", None), P(), P("seq", "mp"), P("seq", "mp"), P("seq", "mp"), P(),
    )
    return jax.shard_map(
        local, mesh=mesh, in_specs=placed,
        out_specs=(P(None, "seq", "mp"), P(None, "seq"), P()), check_vma=False,
    )
```

time: 146 us -> 133 us (0.911)
  Pallas kernels: 140 us -> 131 us
  local copies, waits for them, and re-layouts: 4.17 us -> 0 us
    pallas_call x1 -> x2, Pallas kernels: 140 us -> 131 us  [the longest x1 128 us: local(): pl.pallas_call(layer_kernel, out_shape=results, in_specs=[hbm, vmem, hbm,...]
    unnamed x2 -> x0, local copies, waits for them, and re-layouts: 2.86 us -> none
where the time goes in v2:
time: 133 us
  Pallas kernels  131 us (98%)
    pallas_call x1, Pallas kernels, local(): pl.pallas_call(layer_kernel, out_shape=results, in_specs=[hbm, vmem, hbm,...  128 us
    pallas_call x1, Pallas kernels, local(): pl.pallas_call(finish_kernel, out_shape=results, in_specs=[hbm, vmem, sme...  3.04 us

profile of v2, /device:TPU:1, one launch (start us, length us, event | category | flops | bytes accessed | tf_op | source)
XLA Modules:
  0.0 132.9 jit_solution(16849886566183263447)
XLA Ops:
  0.7 0.3 fusion
  1.0 0.8 pad_maximum_fusion
  1.7 128.2 %layer.1 = (bf16[256,512]{1,0:T(8,128)(2,1)}, f32[2,128]{1,0:T(2,128)}, f32[2]{0:T(128)}) custom-call(bf16[256,2048]{1,0:T(8,128)(2,1)} %bitcast.7, f32[1,2048]{1,0:T(1,128)} %bitcast.8, bf16[2048,512]{1,0:T(8,128)(2,1)} %qw_hbm.1, f32[1,512]{1,0:T(1,128)} %bitcast.10, bf16[2048,256]{1,0:T(8,128)(2,1)} %kw_hbm.1, f32[2,128]{1,0:T(2,128)} %bitcast.11, ...), custom_call_target="tpu_custom_call" | custom-call | tf_op jit(solution)/shard_map/layer/pallas_call | solution.py:721
  129.9 3.0 %finish.1 = (bf16[256,512]{1,0:T(8,128)(2,1)}, f32[2,128]{1,0:T(2,128)}, f32[2]{0:T(128)}) custom-call(bf16[256,512]{1,0:T(8,128)(2,1)} %get-tuple-element.9.layer_hbm, f32[2,128]{1,0:T(2,128)} %get-tuple-element.10.infl_ref, f32[2]{0:T(128)} %get-tuple-element.11.score_ref), custom_call_target="tpu_custom_call" | custom-call | tf_op jit(solution)/shard_map/finish/pallas_call | solution.py:782
  (2 shorter events, 0.0 us)

commit v3 on v2

v3 whole, which is shorter than its diff:
```python
import jax
import jax.numpy as jnp
from jax import lax
from jax.experimental import pallas as pl
from jax.experimental.pallas import tpu as pltpu
from jax.sharding import PartitionSpec as P

HEADS = 16
KV_HEADS = 2
HEAD = 128
D = 2048
NY, NZ = 4, 8
MP = 4
TOK = 128
ROWS = 2 * TOK
OWN_HEADS = HEADS // MP
QCOLS = OWN_HEADS * HEAD
QUART = D // MP
FFP = 1408
WR = 32
GU_CUT = 2048
DN_CUT = 640
NS = NY * NZ * 2

rope_base = 1000000.0
norm_eps = 1e-06
masked_score = -1e30
EXP2_SCALE = HEAD ** (-0.5) * 1.4426950408889634

MESH = pl.DeviceIdType.MESH
F32, BF16 = jnp.float32, jnp.bfloat16

Z_OFF = (0, -1, 1, -2, 2, -3, 3, -4)

FAR_RIGHT = (True, True, True)

EARLY = (
    ("bs", 1), ("bs", 2), ("zs", 1),
)
LATER = (
    ("zs", 0), ("bs", 0), ("ys", 0, 0), ("bp", 1), ("zs", 2), ("ys", 1, 0), ("bp", 2), ("zh", 1, 1),
    ("bp", 0), ("zh", 0, 1), ("yp", 0, 0), ("bl", 1), ("zh", 2, 1), ("zh", 1, 2), ("yp", 1, 0), ("bl", 2),
    ("zh", 0, 2), ("bl", 0), ("bz", 0), ("yp", 0, 1), ("at", 1, 0), ("yl", 0, 0), ("yp", 0, 2), ("yl", 1, 0),
    ("zh", 0, 3), ("at", 0, 0), ("yp", 0, 3), ("yp", 0, 4), ("bh", 0, 1, 0), ("yl", 0, 1), ("yl", 0, 2),
    ("ys", 1, 1), ("at", 0, 1), ("bh", 0, 1, 1), ("yp", 0, 5), ("at", 0, 2), ("zh", 0, 4), ("yp", 0, 6),
    ("yl", 0, 3), ("yl", 0, 4), ("at", 1, 1), ("bh", 0, 2, 0), ("at", 1, 2), ("ys", 1, 2), ("yp", 1, 1),
    ("at", 0, 3), ("yl", 0, 5), ("bh", 0, 2, 1), ("at", 0, 4), ("yl", 0, 6), ("yp", 0, 7), ("zh", 1, 3),
    ("at", 0, 5), ("bh", 0, 3, 0), ("ys", 1, 3), ("at", 1, 3), ("at", 0, 6), ("yl", 0, 7), ("bh", 0, 3, 1),
    ("yl", 1, 1), ("yp", 1, 2), ("at", 1, 4), ("ys", 1, 4), ("at", 0, 7), ("bz", 1), ("yp", 1, 3),
    ("zh", 1, 4), ("op", 0), ("at", 1, 5), ("bh", 0, 4, 0), ("bh", 0, 4, 1), ("yl", 1, 2), ("ys", 1, 5),
    ("at", 1, 6), ("yp", 1, 4), ("zh", 2, 2), ("at", 1, 7), ("bh", 1, 1, 0), ("yl", 1, 3), ("op", 1),
    ("ys", 1, 6), ("bh", 1, 1, 1), ("yp", 1, 5), ("re", 0), ("zh", 2, 3), ("yl", 1, 4), ("bh", 1, 2, 0),
    ("ys", 1, 7), ("bh", 1, 2, 1), ("yp", 1, 6), ("zh", 2, 4), ("yl", 1, 5), ("re", 1), ("ys", 2, 0),
    ("bz", 2), ("bh", 1, 3, 0), ("ys", 2, 1), ("ys", 2, 2), ("yp", 1, 7), ("bh", 1, 3, 1), ("yl", 1, 6),
    ("ys", 2, 3), ("yp", 2, 0), ("bh", 2, 1, 0), ("sn", 0), ("ys", 2, 4), ("yp", 2, 1), ("yp", 2, 2),
    ("bh", 2, 1, 1), ("ys", 2, 5), ("yl", 1, 7), ("ys", 2, 6), ("yp", 2, 3), ("bh", 1, 4, 0), ("bh", 1, 4, 1),
    ("yl", 2, 0), ("ys", 2, 7), ("yp", 2, 4), ("yl", 2, 1), ("yl", 2, 2), ("sn", 1), ("bh", 2, 2, 0), ("gd",),
    ("bh", 2, 2, 1), ("ud",), ("ds", 0), ("bh", 2, 3, 0), ("yl", 2, 3), ("yl", 2, 4), ("yp", 2, 5),
    ("yp", 2, 6), ("yp", 2, 7), ("bh", 2, 3, 1), ("ds", 1), ("yl", 2, 5), ("yl", 2, 6), ("yl", 2, 7),
    ("bh", 2, 4, 0), ("ds", 2), ("bh", 2, 4, 1), ("ds", 3),
)


def layer_kernel(
    hid_hbm, ag_ref, qw_hbm, qb_ref, kw_hbm, kb_ref, vw_hbm, vb_ref, ow_hbm, mg_ref,
    gate_hbm, up_hbm, down_hbm, cos_ref, sin_ref, len_ref,
    out_hbm, infl_ref, score_ref,
    hid, hidq, normed, qw, kvw, ow, qbuf, kv, gu, down, mbuf, lbuf, accbuf, attn,
    stage1, rs1, resid, stage2, rs2, mlp_in, act, innp, sums, tot, gbuf, layer_v,
    lsem, osem, a_send, a_recv, b_send, b_recv, x_send, x_recv, r_send, r_recv,
    s_sem, t_sem,
):
    s = lax.axis_index("seq")
    m = lax.axis_index("mp")
    y = s // (2 * NZ)
    z = lax.rem(s // 2, NZ)
    c = lax.rem(s, 2)
    kvi = m // 2

    def wrap(v, n):
        return lax.rem(v + 2 * n, n)

    def dev(yy, zz, cc):
        return (wrap(yy, NY) * NZ + wrap(zz, NZ)) * 2 + cc

    zp, zm = dev(y, z + 1, c), dev(y, z - 1, c)
    yp, ym = dev(y + 1, z, c), dev(y - 1, z, c)
    partner = dev(y, z, 1 - c)

    def rc(src, dst, ssem, rsem, sdev):
        return pltpu.make_async_remote_copy(
            src_ref=src, dst_ref=dst, send_sem=ssem, recv_sem=rsem,
            device_id={"seq": sdev, "mp": m}, device_id_type=MESH,
        )

    def rcx(src, dst, ssem, rsem, mdev):
        return pltpu.make_async_remote_copy(
            src_ref=src, dst_ref=dst, send_sem=ssem, recv_sem=rsem,
            device_id={"seq": s, "mp": mdev}, device_id_type=MESH,
        )

    kv_cols = pl.ds(pl.multiple_of(kvi * HEAD, HEAD), HEAD)
    own = gu.at[y, z, c]
    loads = {
        "up": [pltpu.make_async_copy(up_hbm, own.at[:, pl.ds(FFP, FFP)], lsem.at[0])],
        "gate": [pltpu.make_async_copy(gate_hbm, own.at[:, pl.ds(0, FFP)], lsem.at[1])],
        "hid": [pltpu.make_async_copy(hid_hbm, hid, lsem.at[3])],
        "kv": [
            pltpu.make_async_copy(kw_hbm.at[:, kv_cols], kvw.at[:, pl.ds(0, HEAD)], lsem.at[4]),
            pltpu.make_async_copy(vw_hbm.at[:, kv_cols], kvw.at[:, pl.ds(HEAD, HEAD)], lsem.at[8]),
        ],
        "q": [pltpu.make_async_copy(qw_hbm, qw, lsem.at[5])],
        "down": [pltpu.make_async_copy(down_hbm, down.at[y, z, c], lsem.at[2])],
        "hidq": [pltpu.make_async_copy(
            hid_hbm.at[:, pl.ds(pl.multiple_of(m * QUART, QUART), QUART)], hidq, lsem.at[6])],
        "ow": [
            pltpu.make_async_copy(ow_hbm.at[:, pl.ds(q * QUART, QUART)], ow.at[q], lsem.at[9 + q])
            for q in range(MP)
        ],
    }
    for copies in loads.values():
        for copy in copies:
            copy.start()

    def need(name):
        for copy in loads.pop(name, ()):
            copy.wait()

    bar = pltpu.get_barrier_semaphore()
    for peer in (zp, zm, yp, ym, partner):
        pl.semaphore_signal(bar, inc=1, device_id={"seq": peer, "mp": m}, device_id_type=MESH)
    for i in range(1, MP):
        pl.semaphore_signal(bar, inc=1, device_id={"seq": s, "mp": wrap(m + i, MP)}, device_id_type=MESH)
    pl.semaphore_wait(bar, 5 + MP - 1)

    ALL = slice(None)
    ZR, YR, HR, DR = 0, 4, 12, 20
    A_HALF = (TOK // 2, WR // 2, WR // 2)
    WGU, WDN = ("gate", "up"), ("down",)

    def a_ref(st, yy, zz, cc):
        if st == 0:
            return kv.at[0, yy, zz, cc]
        if st == 1:
            return gu.at[yy, zz, cc, :, pl.ds(0, GU_CUT)]
        return down.at[yy, zz, cc, :, pl.ds(0, DN_CUT)]

    def load_of(st):
        for name in ((), WGU, WDN)[st]:
            need(name)

    def block(st, yy, zz):
        return a_ref(st, wrap(yy, NY), wrap(zz, NZ), c)

    def half(st, ref, i):
        return ref.at[pl.ds(i * A_HALF[st], A_HALF[st])]

    def a_copy(ref, st, ssem, rsem, d):
        return rc(ref, ref, a_send.at[st, ssem], a_recv.at[st, rsem], d)

    def a_wait_recv(st, rsem, *size):
        a_copy(a_ref(st, *size), st, 0, rsem, partner).wait_recv()

    def zk_of(k):
        if isinstance(k, int):
            return z + Z_OFF[k]
        return z + jnp.where(lax.rem(k, 2) == 1, -((k + 1) // 2), k // 2)

    def z_copy(st, k_to, zz, right):
        return a_copy(block(st, y, zz), st, 0, ZR + (k_to - 1) // 2, zp if right else zm)

    def y_send(st, k):
        load_of(st)
        ref = block(st, y, zk_of(k))
        a_copy(ref, st, 1, YR + k, yp).start()
        a_copy(ref, st, 1, YR + k, ym).start()

    TWO = pl.ds(0, 2)

    def y_pass(st, k):
        zz = zk_of(k)
        a_wait_recv(st, YR + k, TWO, 0, 0)
        a_copy(half(st, block(st, y - 1, zz), 0), st, 1, HR + k, yp).start()
        a_copy(half(st, block(st, y + 1, zz), 1), st, 1, HR + k, ym).start()

    def d_index(st, k):
        return DR + (k, 0, max(0, (k - 1) // 2))[st]

    def y_last(st, k):
        a_wait_recv(st, HR + k, 0, 0, 0)
        a_copy(a_ref(st, ALL, wrap(zk_of(k), NZ), c), st, 1, d_index(st, k), partner).start()

    def z_start(st):
        load_of(st)
        z_copy(st, 1, z, True).start()
        z_copy(st, 2, z, False).start()

    def z_hop(st, h):
        far_right = FAR_RIGHT[st]
        a_wait_recv(st, ZR + h - 1, TWO if h < 4 else 0, 0, 0)
        for k in (2 * h - 1, 2 * h):
            if k >= NZ:
                continue
            right = far_right if k == 7 else k % 2 == 1
            if k + 2 < NZ - 1:
                z_copy(st, k + 2, zk_of(k), right).start()
            if k == (5 if far_right else 6):
                z_copy(st, 7, zk_of(k), far_right).start()
            if st == 0:
                y_send(st, k)

    BY, BH, BZ, BD = 0, 1, 2, 10
    B_HALF = (TOK // 2, WR // 2, WR // 2)

    def b_ref(st, yy, zz, cc):
        if st == 0:
            return kv.at[1, yy, zz, cc]
        if st == 1:
            return gu.at[yy, zz, cc, :, pl.ds(GU_CUT, 2 * FFP - GU_CUT)]
        return down.at[yy, zz, cc, :, pl.ds(DN_CUT, FFP - DN_CUT)]

    def b_copy(st, ref, ssem, rsem, d):
        return rc(ref, ref, b_send.at[st, ssem], b_recv.at[st, rsem], d)

    def b_wait_recv(st, rsem, *size):
        b_copy(st, b_ref(st, *size), 0, rsem, partner).wait_recv()

    def b_block(st, yy, w=None):
        ref = b_ref(st, wrap(yy, NY), z, c)
        return ref if w is None else ref.at[pl.ds(w * B_HALF[st], B_HALF[st])]

    def group(st, zz, w):
        rows = pl.ds(w * B_HALF[st], B_HALF[st])
        zz = wrap(zz, NZ)
        if st == 0:
            return kv.at[1, :, zz, c, rows]
        if st == 1:
            return gu.at[:, zz, c, rows, pl.ds(GU_CUT, 2 * FFP - GU_CUT)]
        return down.at[:, zz, c, rows, pl.ds(DN_CUT, FFP - DN_CUT)]

    def r_copy(st, i, w):
        return b_copy(st, group(st, z - (i - 1), w), 1, BZ + 2 * (i - 1) + w, zp)

    def l_copy(st, i, w):
        return b_copy(st, group(st, z + (i - 1), w), 1, BZ + 2 * (i - 1) + w, zm)

    def r_steps(w):
        return 4 if w == 0 else 3

    def l_steps(w):
        return 3 if w == 0 else 4

    def by_start(st):
        for name in ((), WGU[1:], WDN)[st]:
            need(name)
        b_copy(st, b_block(st, y), 0, BY, yp).start()
        b_copy(st, b_block(st, y), 0, BY, ym).start()

    def by_pass(st):
        b_wait_recv(st, BY, TWO, 0, 0)
        b_copy(st, b_block(st, y - 1, 0), 0, BH, yp).start()
        b_copy(st, b_block(st, y + 1, 1), 0, BH, ym).start()

    def bd_start(st, k):
        b_copy(st, b_ref(st, ALL, wrap(zk_of(k), NZ), c), 2,
               BD + (k, 0, max(0, (k - 1) // 2))[st], partner).start()

    def by_last(st):
        b_wait_recv(st, BH, 0, 0, 0)
        bd_start(st, 0)

    def bz_start(st):
        for w in range(2):
            r_copy(st, 1, w).start()
            l_copy(st, 1, w).start()

    def b_hop(st, h, w):
        b_wait_recv(st, BZ + 2 * (h - 1) + w, ALL if h < 4 else TWO, 0, 0)
        if h + 1 <= r_steps(w):
            r_copy(st, h + 1, w).start()
        if h + 1 <= l_steps(w):
            l_copy(st, h + 1, w).start()
        if w == 1:
            for k in (2 * h - 1, 2 * h):
                if k < NZ:
                    bd_start(st, k)

    TASKS = {
        "zs": z_start, "zh": z_hop, "ys": y_send, "yp": y_pass, "yl": y_last,
        "bs": by_start, "bp": by_pass, "bl": by_last, "bz": bz_start, "bh": b_hop,
    }
    for name, *args in EARLY:
        TASKS[name](*args)

    need("hid")

    def norm_rows(i, _):
        r = pl.ds(pl.multiple_of(i * 16, 16), 16)
        x = hid[r, :].astype(F32)
        sq = x * x
        part = sq[:, 0:HEAD]
        for j in range(1, D // HEAD):
            part = part + sq[:, j * HEAD:(j + 1) * HEAD]
        innp[r, :] = part
        factor = lax.rsqrt(jnp.sum(part, axis=-1, keepdims=True) * (1.0 / D) + norm_eps)
        normed[r, :] = (x * factor * ag_ref[...]).astype(BF16)
        return 0

    lax.fori_loop(0, ROWS // 16, norm_rows, 0, unroll=4)

    cos = cos_ref[...]
    sin = sin_ref[...]

    def rope(u):
        return u * cos + pltpu.roll(u, HEAD // 2, 1) * sin

    need("kv")
    kv_all = jnp.dot(normed[...], kvw[...], preferred_element_type=F32)
    kb = kb_ref[pl.ds(kvi, 1), :]
    vb = vb_ref[pl.ds(kvi, 1), :]
    for sq in range(2):
        kk = kv_all[sq * TOK:(sq + 1) * TOK, 0:HEAD] + kb
        vv = kv_all[sq * TOK:(sq + 1) * TOK, HEAD:2 * HEAD] + vb
        kv[sq, y, z, c, :, 0:HEAD] = rope(kk).astype(BF16)
        kv[sq, y, z, c, :, HEAD:2 * HEAD] = vv.astype(BF16)

    need("q")
    q_all = jnp.dot(normed[...], qw[...], preferred_element_type=F32) + qb_ref[...]
    for sq in range(2):
        for h in range(OWN_HEADS):
            u = q_all[sq * TOK:(sq + 1) * TOK, h * HEAD:(h + 1) * HEAD]
            qbuf[sq, h * TOK:(h + 1) * TOK, :] = rope(u).astype(BF16)

    for sq in range(2):
        mbuf[sq] = jnp.full((OWN_HEADS * TOK, HEAD), masked_score, F32)
        lbuf[sq] = jnp.zeros((OWN_HEADS * TOK, HEAD), F32)
        accbuf[sq] = jnp.zeros((OWN_HEADS * TOK, HEAD), F32)

    def attend(sq, yks, zk, diagonal):
        pairs = [kv[sq, yk, zk] for yk in yks]
        kb_ = jnp.concatenate([p[:, :, 0:HEAD].reshape(2 * TOK, HEAD) for p in pairs], axis=0)
        vb_ = jnp.concatenate([p[:, :, HEAD:2 * HEAD].reshape(2 * TOK, HEAD) for p in pairs], axis=0)
        sc = lax.dot_general(qbuf[sq], kb_, (((1,), (1,)), ((), ())), preferred_element_type=F32)
        if diagonal:
            row = lax.rem(lax.broadcasted_iota(jnp.int32, sc.shape, 0), TOK) + c * TOK
            col = lax.broadcasted_iota(jnp.int32, sc.shape, 1)
            sc = jnp.where(col <= row, sc, masked_score)
        m_old = mbuf[sq]
        m_new = jnp.maximum(m_old, jnp.max(sc, axis=1, keepdims=True))
        p = jnp.exp2((sc - jnp.concatenate([m_new] * (2 * len(yks)), axis=1)) * EXP2_SCALE)
        alpha = jnp.exp2((m_old - m_new) * EXP2_SCALE)
        mbuf[sq] = m_new
        lbuf[sq] = lbuf[sq] * alpha + jnp.sum(p, axis=1, keepdims=True)
        accbuf[sq] = accbuf[sq] * alpha + jnp.dot(p.astype(BF16), vb_, preferred_element_type=F32)

    def attend_round(sq, k):
        zk = wrap(zk_of(k), NZ)

        @pl.when(k == 0)
        def _():
            attend(sq, (y,), zk, True)

        n = y + jnp.where(zk < z, 1, 0)

        def step(i, _):
            attend(sq, (2 * i, 2 * i + 1), zk, False)
            return 0

        lax.fori_loop(0, n // 2, step, 0)

        @pl.when(lax.rem(n, 2) == 1)
        def _():
            attend(sq, (n - 1,), zk, False)

    def seq_rows(sq):
        return pl.ds(sq * TOK, TOK)

    def rs1_send(sq, j):
        return rcx(stage1.at[sq, j], rs1.at[m, seq_rows(sq)], x_send.at[0], x_recv.at[0, sq],
                   wrap(m + j, MP))

    def three(buf, sq):
        return buf.at[pl.ds(0, MP - 1), seq_rows(sq)]

    def o_project(sq):
        need("ow")
        for h in range(OWN_HEADS):
            r = slice(h * TOK, (h + 1) * TOK)
            attn[sq * TOK:(sq + 1) * TOK, h * HEAD:(h + 1) * HEAD] = (
                accbuf[sq, r, :] / lbuf[sq, r, :]
            ).astype(BF16)
        here = attn[sq * TOK:(sq + 1) * TOK, :]
        for j in (2, 1, 3, 0):
            part = jnp.dot(here, ow[wrap(m + j, MP)], preferred_element_type=F32).astype(BF16)
            if j == 0:
                rs1[m, seq_rows(sq), :] = part
            else:
                stage1[sq, j] = part
        for j in (2, 1, 3):
            rs1_send(sq, j).start()

    def ag_send(sq, j):
        ref = resid.at[m, seq_rows(sq)]
        return rcx(ref, ref, x_send.at[1], x_recv.at[1, sq], wrap(m + j, MP))

    def residual(sq):
        need("hidq")
        rcx(three(rs1, sq), three(rs1, sq), x_send.at[0], x_recv.at[0, sq], wrap(m + 1, MP)).wait_recv()
        r = seq_rows(sq)
        add = rs1[0, r, :].astype(F32)
        for q in range(1, MP):
            add = add + rs1[q, r, :].astype(F32)
        resid[m, r, :] = (hidq[r, :].astype(F32) + add).astype(BF16)
        for j in (2, 1, 3):
            ag_send(sq, j).start()

    def second_norm(sq):
        rcx(three(resid, sq), three(resid, sq), x_send.at[1], x_recv.at[1, sq], wrap(m + 1, MP)).wait_recv()

        def norm2_rows(i, _):
            r = pl.ds(pl.multiple_of(sq * TOK + i * 16, 16), 16)
            xs = [resid[q, r, :].astype(F32) for q in range(MP)]
            part = None
            for x in xs:
                sqr = x * x
                for j in range(QUART // HEAD):
                    t = sqr[:, j * HEAD:(j + 1) * HEAD]
                    part = t if part is None else part + t
            factor = lax.rsqrt(jnp.sum(part, axis=-1, keepdims=True) * (1.0 / D) + norm_eps)
            for q in range(MP):
                cols = slice(q * QUART, (q + 1) * QUART)
                mlp_in[r, cols] = (xs[q] * factor * mg_ref[:, cols]).astype(BF16)
            return 0

        lax.fori_loop(0, TOK // 16, norm2_rows, 0, unroll=4)

    def gate_dot():
        a_wait_recv(1, DR, ALL, ALL, 0)
        rows = gu[:, :, :, :, 0:FFP].reshape(D, FFP)
        gbuf[...] = jnp.dot(mlp_in[...], rows, preferred_element_type=F32)

    def up_dot():
        b_wait_recv(1, BD, ALL, ALL, 0)
        rows = gu[:, :, :, :, FFP:2 * FFP].reshape(D, FFP)
        up_sum = jnp.dot(mlp_in[...], rows, preferred_element_type=F32)
        g = gbuf[...]
        act[...] = (g / (1.0 + jnp.exp(-g)) * up_sum).astype(BF16)

    odd = lax.rem(z, 2)

    def z_pair(i):
        turn = (0, 2 * odd - 1, 1 - 2 * odd, 2)[i]
        return wrap(z // 2 + turn, NZ // 2)

    def rs2_send(i, j):
        q = wrap(m + j, MP)
        return rcx(stage2.at[i, q], rs2.at[i, m], r_send.at[0], r_recv.at[i], q)

    def down_stage(i):
        rounds = pl.ds(0, (3, 2, 2, 1)[i])
        a_wait_recv(2, DR + i, ALL, rounds, 0)
        b_wait_recv(2, BD + i, ALL, rounds, 0)
        p = z_pair(i)
        for q0 in (0, 2):
            rows = down[q0:q0 + 2, pl.ds(2 * p, 2)].reshape(2 * HEAD, FFP)
            part = lax.dot_general(
                act[...], rows, (((1,), (1,)), ((), ())), preferred_element_type=F32
            ).astype(BF16)
            stage2[i, q0] = part[:, 0:HEAD]
            stage2[i, q0 + 1] = part[:, HEAD:2 * HEAD]
        for j in (2, 1, 3):
            rs2_send(i, j).start()

    def layer_stage(i, so_far):
        came = rs2.at[i, pl.ds(0, MP - 1)]
        rcx(came, came, r_send.at[0], r_recv.at[i], wrap(m + 1, MP)).wait_recv()
        cols = pl.ds(pl.multiple_of(z_pair(i) * HEAD, HEAD), HEAD)
        add = stage2[i, m].astype(F32)
        for j in range(1, MP):
            add = add + rs2[i, wrap(m - j, MP)].astype(F32)
        layer = (resid[m, :, cols].astype(F32) + add).astype(BF16)
        layer_v[:, cols] = layer
        wide = layer.astype(F32)
        cp, op = hidq[:, cols].astype(F32) * wide, wide * wide
        return (cp, op) if so_far is None else (so_far[0] + cp, so_far[1] + op)

    TASKS.update(
        op=o_project, re=residual, sn=second_norm, gd=gate_dot, ud=up_dot, ds=down_stage,
    )
    items, before, after = [], [], []
    for name, *args in LATER:
        if name == "at":
            items.append(args)
            before.append(after)
            after = []
        else:
            after.append((TASKS[name], args))

    def run(events):
        for act_, args in events:
            act_(*args)

    def pick(t, values):
        total = 0
        for i, v in enumerate(values):
            if v:
                total = total + jnp.where(t == i, v, 0)
        return total

    def item(t, _):
        for i, events in enumerate(before):
            if events:
                pl.when(t == i)(lambda events=events: run(events))
        sq = pick(t, [e[0] for e in items])
        k = pick(t, [e[1] for e in items])

        @pl.when(sq == 0)
        def _():
            a_wait_recv(0, DR + k, ALL, 0, 0)

        @pl.when(sq == 1)
        def _():
            b_wait_recv(0, BD + k, ALL, 0, 0)

        attend_round(sq, k)
        return 0

    lax.fori_loop(0, len(items), item, 0)
    run(after)

    seven = pl.ds(0, NZ - 1)
    for st in range(3):
        a_copy(a_ref(st, 0, seven, 0), st, 0, 0, partner).wait_send()
        a_copy(a_ref(st, ALL, seven, ALL), st, 1, 0, partner).wait_send()
        b_copy(st, b_ref(st, 0, pl.ds(0, 3), 0), 0, 0, partner).wait_send()
        b_copy(st, b_ref(st, ALL, seven, 0), 1, 0, partner).wait_send()
        b_copy(st, b_ref(st, ALL, ALL, 0), 2, 0, partner).wait_send()
    six = rs1.at[pl.ds(0, MP - 1)]
    for phase in range(2):
        rcx(six, six, x_send.at[phase], x_recv.at[0, 0], wrap(m + 1, MP)).wait_send()

    def lane_sums(part):
        return jnp.sum(part.T, axis=0, keepdims=True)

    in_norm = lane_sums(innp[...])

    so_far = None
    for i in range(4):
        so_far = layer_stage(i, so_far)
    out_copy = pltpu.make_async_copy(layer_v, out_hbm, osem.at[0])
    rowi = lax.broadcasted_iota(jnp.int32, (8, ROWS), 0)
    sums[m] = jnp.where(rowi == 0, lane_sums(so_far[0]), lane_sums(so_far[1]))

    def s_copy(j):
        return rcx(sums.at[m], sums.at[m], s_sem.at[0], s_sem.at[1], wrap(m + j, MP))

    for j in (2, 1, 3):
        s_copy(j).start()
    out_copy.start()
    came = sums.at[pl.ds(0, MP - 1)]
    rcx(came, came, s_sem.at[0], s_sem.at[1], wrap(m + 1, MP)).wait()
    both = sums[0] + sums[1] + sums[2] + sums[3]
    cross, out_norm = both[0:1, :], both[1:2, :]
    cosine = cross / jnp.sqrt((in_norm + norm_eps) * (out_norm + norm_eps))
    lane = lax.broadcasted_iota(jnp.int32, (1, ROWS), 1)
    pos = s * TOK + lax.rem(lane, TOK)
    limit = jnp.where(lane < TOK, len_ref[0], len_ref[1])
    influence = jnp.where(pos < limit, 1.0 - cosine, 0.0)
    infl_ref[0:1, :] = influence[:, 0:TOK]
    infl_ref[1:2, :] = influence[:, TOK:2 * TOK]
    t0 = jnp.sum(influence[:, 0:TOK], axis=1, keepdims=True)
    t1 = jnp.sum(influence[:, TOK:2 * TOK], axis=1, keepdims=True)
    lane = lax.broadcasted_iota(jnp.int32, (1, HEAD), 1)
    one = pl.ds(0, 1)
    tot[s, one, :] = jnp.where(lane < HEAD // 2, t0, t1)

    def t_copy(i):
        ref = tot.at[s, one]
        return rc(ref, ref, t_sem.at[0], t_sem.at[1], lax.rem(s + i, NS))

    def t_start(i, _):
        t_copy(i).start()
        return 0

    lax.fori_loop(1, NS, t_start, 0)
    every = tot.at[pl.ds(0, NS - 1), one]
    rc(every, every, t_sem.at[0], t_sem.at[1], partner).wait()
    total = jnp.sum(tot[:, 0, :], axis=0, keepdims=True)
    tokens = jnp.where(lane < HEAD // 2, len_ref[0], len_ref[1]).astype(F32)
    score = total / tokens
    score_ref[0] = jnp.sum(jnp.where(lane == 0, score, 0.0))
    score_ref[1] = jnp.sum(jnp.where(lane == HEAD - 1, score, 0.0))

    gone = rs2.at[pl.ds(0, MP - 1)]
    rcx(gone, gone, r_send.at[0], r_recv.at[0], wrap(m + 1, MP)).wait_send()
    out_copy.wait()


def finish_kernel(layer_hbm, infl_hbm, score_hbm, out_hbm, infl_out, score_out, buf, sem):
    into = pltpu.make_async_copy(layer_hbm, buf, sem.at[0])
    small = [
        pltpu.make_async_copy(infl_hbm, infl_out, sem.at[1]),
        pltpu.make_async_copy(score_hbm, score_out, sem.at[2]),
    ]
    into.start()
    for copy in small:
        copy.start()
    into.wait()
    out = pltpu.make_async_copy(buf, out_hbm, sem.at[3])
    out.start()
    for copy in small:
        copy.wait()
    out.wait()


def local(
    hidden_in, attn_gain, q_weight, q_bias, k_weight, k_bias, v_weight, v_bias, o_weight,
    mlp_gain, gate_weight, up_weight, down_weight, lengths,
):
    seqs_n, tok_n, width = hidden_in.shape
    seq_rank = lax.axis_index("seq")
    positions = seq_rank * tok_n + jnp.arange(tok_n, dtype=jnp.int32)
    half_width = HEAD // 2
    inv_freq = rope_base ** (-(jnp.arange(half_width, dtype=jnp.float32) * 2.0) / HEAD)
    angles = positions.astype(jnp.float32)[:, None] * inv_freq[None, :]
    cos = jnp.cos(angles)
    sin = jnp.sin(angles)
    cos_t = jnp.concatenate([cos, cos], axis=-1)
    sin_t = jnp.concatenate([-sin, sin], axis=-1)

    hbm = pl.BlockSpec(memory_space=pltpu.HBM)
    vmem = pl.BlockSpec(memory_space=pltpu.VMEM)
    smem = pl.BlockSpec(memory_space=pltpu.SMEM)
    dma = pltpu.SemaphoreType.DMA
    results = (
        jax.ShapeDtypeStruct((ROWS, QUART), BF16),
        jax.ShapeDtypeStruct((2, TOK), F32),
        jax.ShapeDtypeStruct((2,), F32),
    )
    layer_part, influence, score = pl.pallas_call(
        layer_kernel,
        out_shape=results,
        in_specs=[
            hbm, vmem, hbm, vmem, hbm, vmem, hbm, vmem, hbm, vmem,
            hbm, hbm, hbm, vmem, vmem, smem,
        ],
        out_specs=(hbm, vmem, smem),
        scratch_shapes=[
            pltpu.VMEM((ROWS, D), BF16),
            pltpu.VMEM((ROWS, QUART), BF16),
            pltpu.VMEM((ROWS, D), BF16),
            pltpu.VMEM((D, QCOLS), BF16),
            pltpu.VMEM((D, 2 * HEAD), BF16),
            pltpu.VMEM((MP, QCOLS, QUART), BF16),
            pltpu.VMEM((2, OWN_HEADS * TOK, HEAD), BF16),
            pltpu.VMEM((2, NY, NZ, 2, TOK, 2 * HEAD), BF16),
            pltpu.VMEM((NY, NZ, 2, WR, 2 * FFP), BF16),
            pltpu.VMEM((NY, NZ, 2, WR, FFP), BF16),
            pltpu.VMEM((2, OWN_HEADS * TOK, HEAD), F32),
            pltpu.VMEM((2, OWN_HEADS * TOK, HEAD), F32),
            pltpu.VMEM((2, OWN_HEADS * TOK, HEAD), F32),
            pltpu.VMEM((ROWS, QCOLS), BF16),
            pltpu.VMEM((2, MP, TOK, QUART), BF16),
            pltpu.VMEM((MP, ROWS, QUART), BF16),
            pltpu.VMEM((MP, ROWS, QUART), BF16),
            pltpu.VMEM((4, MP, ROWS, HEAD), BF16),
            pltpu.VMEM((4, MP, ROWS, HEAD), BF16),
            pltpu.VMEM((ROWS, D), BF16),
            pltpu.VMEM((ROWS, FFP), BF16),
            pltpu.VMEM((ROWS, HEAD), F32),
            pltpu.VMEM((MP, 8, ROWS), F32),
            pltpu.VMEM((NS, 8, HEAD), F32),
            pltpu.VMEM((ROWS, FFP), F32),
            pltpu.VMEM((ROWS, QUART), BF16),
            dma((13,)),
            dma((1,)),
            dma((3, 2)),
            dma((3, 28)),
            dma((3, 3)),
            dma((3, 18)),
            dma((2,)),
            dma((2, 2)),
            dma((1,)),
            dma((4,)),
            dma((2,)),
            dma((2,)),
        ],
        compiler_params=pltpu.CompilerParams(
            collective_id=0, has_side_effects=True, vmem_limit_bytes=62 * 1024 * 1024
        ),
        name="layer",
    )(
        hidden_in.reshape(ROWS, width), attn_gain.reshape(1, width), q_weight,
        q_bias.reshape(1, QCOLS), k_weight, k_bias.reshape(KV_HEADS, HEAD), v_weight,
        v_bias.reshape(KV_HEADS, HEAD), o_weight, mlp_gain.reshape(1, width), gate_weight,
        up_weight, down_weight, cos_t, sin_t, lengths,
    )
    layer_part, influence, score = pl.pallas_call(
        finish_kernel,
        out_shape=results,
        in_specs=[hbm, hbm, hbm],
        out_specs=(hbm, hbm, hbm),
        scratch_shapes=[pltpu.VMEM((ROWS, QUART), BF16), dma((4,))],
        name="finish",
    )(layer_part, influence, score)
    return layer_part.reshape(seqs_n, tok_n, QUART), influence, score


def solution(mesh):
    placed = (
        P(None, "seq", None), P(), P(None, "mp"), P("mp"), P(), P(), P(), P(),
        P("mp", None), P(), P("seq", "mp"), P("seq", "mp"), P("seq", "mp"), P(),
    )
    return jax.shard_map(
        local, mesh=mesh, in_specs=placed,
        out_specs=(P(None, "seq", "mp"), P(None, "seq"), P()), check_vma=False,
    )
```

time: 133 us -> 110 us (0.83)
  Pallas kernels: 131 us -> 108 us
    pallas_call x1, Pallas kernels: 128 us -> 106 us  [local(): pl.pallas_call(layer_kernel, out_shape=results, in_specs=[hbm, vmem, hbm,...]
    pallas_call x1, Pallas kernels: 3.04 us -> 1.69 us  [local(): pl.pallas_call(finish_kernel, out_shape=results, in_specs=[hbm, hbm, hbm]...]
where the time goes in v3:
time: 110 us
  Pallas kernels  108 us (98%)
    pallas_call x1, Pallas kernels, local(): pl.pallas_call(layer_kernel, out_shape=results, in_specs=[hbm, vmem, hbm,...  106 us

profile of v3, /device:TPU:1, one launch (start us, length us, event | category | flops | bytes accessed | tf_op | source)
XLA Modules:
  0.0 109.7 jit_solution(11929253223628679570)
XLA Ops:
  0.7 0.3 fusion
  1.0 0.8 pad_maximum_fusion
  1.7 106.3 %layer.1 = (bf16[256,512]{1,0:T(8,128)(2,1)}, f32[2,128]{1,0:T(2,128)}, f32[2]{0:T(128)}) custom-call(bf16[256,2048]{1,0:T(8,128)(2,1)} %bitcast.7, f32[1,2048]{1,0:T(1,128)} %bitcast.8, bf16[2048,512]{1,0:T(8,128)(2,1)} %qw_hbm.1, f32[1,512]{1,0:T(1,128)} %bitcast.10, bf16[2048,256]{1,0:T(8,128)(2,1)} %kw_hbm.1, f32[2,128]{1,0:T(2,128)} %bitcast.11, ...), custom_call_target="tpu_custom_call" | custom-call | tf_op jit(solution)/shard_map/layer/pallas_call | solution.py:640
  108.0 1.7 %finish.1 = (bf16[256,512]{1,0:T(8,128)(2,1)}, f32[2,128]{1,0:T(2,128)}, f32[2]{0:T(128)}) custom-call(bf16[256,512]{1,0:T(8,128)(2,1)} %get-tuple-element.9.layer_hbm, f32[2,128]{1,0:T(2,128)} %get-tuple-element.10.infl_hbm, f32[2]{0:T(128)} %get-tuple-element.11.score_hbm), custom_call_target="tpu_custom_call" | custom-call | tf_op jit(solution)/shard_map/finish/pallas_call | solution.py:698
  (2 shorter events, 0.0 us)

commit v4 on v3

--- a/solution.py
+++ b/solution.py
@@ -1,5 +1,6 @@
 import jax
 import jax.numpy as jnp
+import numpy as np
 from jax import lax
 from jax.experimental import pallas as pl
 from jax.experimental.pallas import tpu as pltpu
@@ -18,7 +19,7 @@
 QUART = D // MP
 FFP = 1408
 WR = 32
-GU_CUT = 2048
+GU_CUT = 1792
 DN_CUT = 640
 NS = NY * NZ * 2
 
@@ -27,47 +28,60 @@
 masked_score = -1e30
 EXP2_SCALE = HEAD ** (-0.5) * 1.4426950408889634
 
+
+def rotation_tables():
+    freq = rope_base ** (-2.0 * np.arange(HEAD // 2) / HEAD)
+    freq = np.concatenate([freq, freq])
+    near = np.arange(TOK)[:, None] * freq
+    far = TOK * np.arange(NS)[:, None] * freq
+    return np.stack([np.cos(near), np.sin(near)]).astype(np.float32), np.stack(
+        [np.cos(far), np.sin(far)]).astype(np.float32)
+
+
 MESH = pl.DeviceIdType.MESH
 F32, BF16 = jnp.float32, jnp.bfloat16
 
 Z_OFF = (0, -1, 1, -2, 2, -3, 3, -4)
 
-FAR_RIGHT = (True, True, True)
+FAR_RIGHT = (False, True, True)
 
 EARLY = (
-    ("bs", 1), ("bs", 2), ("zs", 1),
+    ("bs", 2), ("zs", 2), ("zs", 1), ("bs", 1),
 )
 LATER = (
-    ("zs", 0), ("bs", 0), ("ys", 0, 0), ("bp", 1), ("zs", 2), ("ys", 1, 0), ("bp", 2), ("zh", 1, 1),
-    ("bp", 0), ("zh", 0, 1), ("yp", 0, 0), ("bl", 1), ("zh", 2, 1), ("zh", 1, 2), ("yp", 1, 0), ("bl", 2),
-    ("zh", 0, 2), ("bl", 0), ("bz", 0), ("yp", 0, 1), ("at", 1, 0), ("yl", 0, 0), ("yp", 0, 2), ("yl", 1, 0),
-    ("zh", 0, 3), ("at", 0, 0), ("yp", 0, 3), ("yp", 0, 4), ("bh", 0, 1, 0), ("yl", 0, 1), ("yl", 0, 2),
-    ("ys", 1, 1), ("at", 0, 1), ("bh", 0, 1, 1), ("yp", 0, 5), ("at", 0, 2), ("zh", 0, 4), ("yp", 0, 6),
-    ("yl", 0, 3), ("yl", 0, 4), ("at", 1, 1), ("bh", 0, 2, 0), ("at", 1, 2), ("ys", 1, 2), ("yp", 1, 1),
-    ("at", 0, 3), ("yl", 0, 5), ("bh", 0, 2, 1), ("at", 0, 4), ("yl", 0, 6), ("yp", 0, 7), ("zh", 1, 3),
-    ("at", 0, 5), ("bh", 0, 3, 0), ("ys", 1, 3), ("at", 1, 3), ("at", 0, 6), ("yl", 0, 7), ("bh", 0, 3, 1),
-    ("yl", 1, 1), ("yp", 1, 2), ("at", 1, 4), ("ys", 1, 4), ("at", 0, 7), ("bz", 1), ("yp", 1, 3),
-    ("zh", 1, 4), ("op", 0), ("at", 1, 5), ("bh", 0, 4, 0), ("bh", 0, 4, 1), ("yl", 1, 2), ("ys", 1, 5),
-    ("at", 1, 6), ("yp", 1, 4), ("zh", 2, 2), ("at", 1, 7), ("bh", 1, 1, 0), ("yl", 1, 3), ("op", 1),
-    ("ys", 1, 6), ("bh", 1, 1, 1), ("yp", 1, 5), ("re", 0), ("zh", 2, 3), ("yl", 1, 4), ("bh", 1, 2, 0),
-    ("ys", 1, 7), ("bh", 1, 2, 1), ("yp", 1, 6), ("zh", 2, 4), ("yl", 1, 5), ("re", 1), ("ys", 2, 0),
-    ("bz", 2), ("bh", 1, 3, 0), ("ys", 2, 1), ("ys", 2, 2), ("yp", 1, 7), ("bh", 1, 3, 1), ("yl", 1, 6),
-    ("ys", 2, 3), ("yp", 2, 0), ("bh", 2, 1, 0), ("sn", 0), ("ys", 2, 4), ("yp", 2, 1), ("yp", 2, 2),
-    ("bh", 2, 1, 1), ("ys", 2, 5), ("yl", 1, 7), ("ys", 2, 6), ("yp", 2, 3), ("bh", 1, 4, 0), ("bh", 1, 4, 1),
-    ("yl", 2, 0), ("ys", 2, 7), ("yp", 2, 4), ("yl", 2, 1), ("yl", 2, 2), ("sn", 1), ("bh", 2, 2, 0), ("gd",),
-    ("bh", 2, 2, 1), ("ud",), ("ds", 0), ("bh", 2, 3, 0), ("yl", 2, 3), ("yl", 2, 4), ("yp", 2, 5),
-    ("yp", 2, 6), ("yp", 2, 7), ("bh", 2, 3, 1), ("ds", 1), ("yl", 2, 5), ("yl", 2, 6), ("yl", 2, 7),
-    ("bh", 2, 4, 0), ("ds", 2), ("bh", 2, 4, 1), ("ds", 3),
+    ("ys", 2, 0), ("bs", 0), ("zs", 0), ("ys", 0, 0), ("zh", 2, 1), ("bp", 2), ("bp", 1), ("zh", 1, 1),
+    ("yp", 2, 0), ("bp", 0), ("zh", 0, 1), ("yp", 0, 0), ("zh", 2, 2), ("bl", 2), ("bl", 1), ("yl", 2, 0),
+    ("bl", 0), ("bz", 0), ("ys", 1, 0), ("yp", 0, 1), ("zh", 0, 2), ("yp", 0, 2), ("zh", 2, 3), ("yl", 0, 0),
+    ("xl", 0), ("bh", 0, 1, 0), ("at", 0, 0), ("bh", 0, 1, 1), ("yl", 0, 1), ("yp", 1, 0), ("at", 1, 0),
+    ("zh", 1, 2), ("zh", 2, 4), ("zh", 0, 3), ("yp", 0, 3), ("at", 0, 1), ("bh", 0, 2, 0), ("yp", 0, 4),
+    ("yl", 0, 2), ("bh", 0, 2, 1), ("yl", 1, 0), ("xl", 1), ("at", 0, 2), ("yp", 0, 5), ("ys", 1, 1),
+    ("zh", 1, 3), ("at", 1, 1), ("xl", 2), ("zh", 0, 4), ("yp", 0, 6), ("yl", 0, 3), ("yl", 0, 4),
+    ("bh", 0, 3, 0), ("yl", 0, 5), ("xl", 3), ("bh", 0, 3, 1), ("at", 1, 2), ("ys", 1, 2), ("bz", 1),
+    ("at", 0, 3), ("zh", 1, 4), ("yp", 1, 1), ("at", 0, 4), ("bh", 0, 4, 0), ("xl", 4), ("yl", 0, 6),
+    ("bh", 0, 4, 1), ("yp", 0, 7), ("at", 1, 3), ("at", 0, 5), ("xl", 5), ("ys", 1, 3), ("yp", 1, 2),
+    ("bh", 1, 1, 0), ("at", 1, 4), ("yl", 1, 1), ("yl", 0, 7), ("at", 0, 6), ("xl", 6), ("bh", 1, 1, 1),
+    ("ys", 1, 4), ("at", 1, 5), ("at", 0, 7), ("yp", 1, 3), ("xl", 7), ("yl", 1, 2), ("op", 0), ("bz", 2),
+    ("at", 1, 6), ("ys", 1, 5), ("at", 1, 7), ("yp", 1, 4), ("op", 1), ("bh", 1, 2, 0), ("yl", 1, 3),
+    ("bh", 1, 2, 1), ("rm", 0), ("bh", 2, 1, 0), ("ys", 1, 6), ("yp", 1, 5), ("bh", 2, 1, 1), ("rm", 1),
+    ("yl", 1, 4), ("ys", 1, 7), ("bh", 1, 3, 0), ("re", 0), ("yp", 1, 6), ("yl", 1, 5), ("bh", 1, 3, 1),
+    ("ys", 2, 1), ("re", 1), ("ys", 2, 2), ("yp", 1, 7), ("bh", 2, 2, 0), ("yl", 1, 6), ("ap", 0),
+    ("ys", 2, 3), ("yp", 2, 1), ("bh", 2, 2, 1), ("yp", 2, 2), ("ys", 2, 4), ("yl", 1, 7), ("ys", 2, 5),
+    ("ap", 1), ("yp", 2, 3), ("yl", 2, 1), ("bh", 1, 4, 0), ("bh", 1, 4, 1), ("ys", 2, 6), ("sn", 0),
+    ("yl", 2, 2), ("ys", 2, 7), ("yp", 2, 4), ("yp", 2, 5), ("bh", 2, 3, 0), ("sn", 1), ("gd",),
+    ("bh", 2, 3, 1), ("yp", 2, 6), ("yl", 2, 3), ("yp", 2, 7), ("ud",), ("bh", 2, 4, 0), ("yl", 2, 4),
+    ("yl", 2, 5), ("ds", 0), ("yl", 2, 6), ("yl", 2, 7), ("ds", 1), ("bh", 2, 4, 1), ("ds", 2), ("dm", 0),
+    ("ds", 3), ("dm", 1), ("dm", 2), ("dm", 3),
 )
 
 
 def layer_kernel(
-    hid_hbm, ag_ref, qw_hbm, qb_ref, kw_hbm, kb_ref, vw_hbm, vb_ref, ow_hbm, mg_ref,
-    gate_hbm, up_hbm, down_hbm, cos_ref, sin_ref, len_ref,
+    hid_hbm, ag_hbm, qw_hbm, qb_hbm, kw_hbm, kb_hbm, vw_hbm, vb_hbm, ow_hbm, mg_hbm,
+    gate_hbm, up_hbm, down_hbm, near_hbm, far_hbm, len_ref,
     out_hbm, infl_ref, score_ref,
-    hid, hidq, normed, qw, kvw, ow, qbuf, kv, gu, down, mbuf, lbuf, accbuf, attn,
-    stage1, rs1, resid, stage2, rs2, mlp_in, act, innp, sums, tot, gbuf, layer_v,
-    lsem, osem, a_send, a_recv, b_send, b_recv, x_send, x_recv, r_send, r_recv,
+    hid, hidq, normed, qw, kvw, ow, qbuf, kv, gu, down, mbuf, accbuf, attn,
+    stage1, tr1, rs1, resid, stage2, tr2, rs2, mlp_in, act, innp, sums, tot, gbuf, layer_v,
+    ag_ref, mg_ref, qb_ref, kb_ref, vb_ref, near_ref, far_ref,
+    lsem, osem, a_send, a_recv, b_send, b_recv, k_send, k_recv, x_send, x_recv, r_send, r_recv,
     s_sem, t_sem,
 ):
     s = lax.axis_index("seq")
@@ -101,22 +115,23 @@
 
     kv_cols = pl.ds(pl.multiple_of(kvi * HEAD, HEAD), HEAD)
     own = gu.at[y, z, c]
+
+    def group_of(index, *pairs):
+        return [pltpu.make_async_copy(a, b, lsem.at[index + i]) for i, (a, b) in enumerate(pairs)]
+
     loads = {
-        "up": [pltpu.make_async_copy(up_hbm, own.at[:, pl.ds(FFP, FFP)], lsem.at[0])],
-        "gate": [pltpu.make_async_copy(gate_hbm, own.at[:, pl.ds(0, FFP)], lsem.at[1])],
-        "hid": [pltpu.make_async_copy(hid_hbm, hid, lsem.at[3])],
-        "kv": [
-            pltpu.make_async_copy(kw_hbm.at[:, kv_cols], kvw.at[:, pl.ds(0, HEAD)], lsem.at[4]),
-            pltpu.make_async_copy(vw_hbm.at[:, kv_cols], kvw.at[:, pl.ds(HEAD, HEAD)], lsem.at[8]),
-        ],
-        "q": [pltpu.make_async_copy(qw_hbm, qw, lsem.at[5])],
-        "down": [pltpu.make_async_copy(down_hbm, down.at[y, z, c], lsem.at[2])],
-        "hidq": [pltpu.make_async_copy(
-            hid_hbm.at[:, pl.ds(pl.multiple_of(m * QUART, QUART), QUART)], hidq, lsem.at[6])],
-        "ow": [
-            pltpu.make_async_copy(ow_hbm.at[:, pl.ds(q * QUART, QUART)], ow.at[q], lsem.at[9 + q])
-            for q in range(MP)
-        ],
+        "up": group_of(0, (up_hbm, own.at[:, pl.ds(FFP, FFP)])),
+        "gate": group_of(1, (gate_hbm, own.at[:, pl.ds(0, FFP)])),
+        "hid": group_of(2, (hid_hbm, hid), (ag_hbm, ag_ref)),
+        "kv": group_of(
+            4, (kw_hbm.at[:, kv_cols], kvw.at[:, pl.ds(0, HEAD)]),
+            (vw_hbm.at[:, kv_cols], kvw.at[:, pl.ds(HEAD, HEAD)]),
+            (kb_hbm, kb_ref), (vb_hbm, vb_ref), (near_hbm, near_ref), (far_hbm, far_ref)),
+        "q": group_of(10, (qw_hbm, qw), (qb_hbm, qb_ref)),
+        "down": group_of(12, (down_hbm, down.at[y, z, c])),
+        "hidq": group_of(
+            13, (hid_hbm.at[:, pl.ds(pl.multiple_of(m * QUART, QUART), QUART)], hidq), (mg_hbm, mg_ref)),
+        "ow": group_of(15, *((ow_hbm.at[:, pl.ds(q * QUART, QUART)], ow.at[q]) for q in range(MP))),
     }
     for copies in loads.values():
         for copy in copies:
@@ -210,15 +225,22 @@
                 y_send(st, k)
 
     BY, BH, BZ, BD = 0, 1, 2, 10
-    B_HALF = (TOK // 2, WR // 2, WR // 2)
-
-    def b_ref(st, yy, zz, cc):
+    B_HALF = (TOK // 4, WR // 2, WR // 2)
+    mine = pl.multiple_of(lax.rem(m, 2) * (TOK // 2), TOK // 2)
+    other = pl.multiple_of(TOK // 2 - mine, TOK // 2)
+
+    def b_full(st, yy, zz, cc):
         if st == 0:
             return kv.at[1, yy, zz, cc]
         if st == 1:
             return gu.at[yy, zz, cc, :, pl.ds(GU_CUT, 2 * FFP - GU_CUT)]
         return down.at[yy, zz, cc, :, pl.ds(DN_CUT, FFP - DN_CUT)]
 
+    def b_ref(st, yy, zz, cc):
+        if st == 0:
+            return kv.at[1, yy, zz, cc, pl.ds(mine, TOK // 2)]
+        return b_full(st, yy, zz, cc)
+
     def b_copy(st, ref, ssem, rsem, d):
         return rc(ref, ref, b_send.at[st, ssem], b_recv.at[st, rsem], d)
 
@@ -233,6 +255,7 @@
         rows = pl.ds(w * B_HALF[st], B_HALF[st])
         zz = wrap(zz, NZ)
         if st == 0:
+            rows = pl.ds(pl.multiple_of(mine + w * B_HALF[st], B_HALF[st]), B_HALF[st])
             return kv.at[1, :, zz, c, rows]
         if st == 1:
             return gu.at[:, zz, c, rows, pl.ds(GU_CUT, 2 * FFP - GU_CUT)]
@@ -261,13 +284,42 @@
         b_copy(st, b_block(st, y - 1, 0), 0, BH, yp).start()
         b_copy(st, b_block(st, y + 1, 1), 0, BH, ym).start()
 
+    def b_all_wait(st, rsem, *size):
+        ref = b_full(st, *size)
+        rc(ref, ref, b_send.at[st, 2], b_recv.at[st, rsem], partner).wait_recv()
+
     def bd_start(st, k):
-        b_copy(st, b_ref(st, ALL, wrap(zk_of(k), NZ), c), 2,
+        b_copy(st, b_full(st, ALL, wrap(zk_of(k), NZ), c), 2,
                BD + (k, 0, max(0, (k - 1) // 2))[st], partner).start()
+
+    pair = m + 1 - 2 * lax.rem(m, 2)
+
+    def k_copy(ref, k):
+        return rcx(ref, ref, k_send.at[min(k, 1)], k_recv.at[k], pair)
+
+    def swap_start(k):
+        zz = wrap(zk_of(k), NZ)
+        rows = pl.ds(mine, TOK // 2)
+        if k == 0:
+            for i in range(1, NY):
+                k_copy(kv.at[1, wrap(y + i, NY), zz, c, rows], k).start()
+        else:
+            k_copy(kv.at[1, :, zz, c, rows], k).start()
+
+    def swap_last(k):
+        some = kv.at[1, pl.ds(0, NY - 1) if k == 0 else ALL, 0, 0, pl.ds(0, TOK // 2)]
+        k_copy(some, k).wait_recv()
+        bd_start(0, k)
+
+    def b_done(st, k):
+        if st == 0:
+            swap_start(k)
+        else:
+            bd_start(st, k)
 
     def by_last(st):
         b_wait_recv(st, BH, 0, 0, 0)
-        bd_start(st, 0)
+        b_done(st, 0)
 
     def bz_start(st):
         for w in range(2):
@@ -283,7 +335,7 @@
         if w == 1:
             for k in (2 * h - 1, 2 * h):
                 if k < NZ:
-                    bd_start(st, k)
+                    b_done(st, k)
 
     TASKS = {
         "zs": z_start, "zh": z_hop, "ys": y_send, "yp": y_pass, "yl": y_last,
@@ -308,13 +360,17 @@
 
     lax.fori_loop(0, ROWS // 16, norm_rows, 0, unroll=4)
 
-    cos = cos_ref[...]
-    sin = sin_ref[...]
+    need("kv")
+    far_cos, far_sin = far_ref[0, pl.ds(s, 1), :], far_ref[1, pl.ds(s, 1), :]
+    near_cos, near_sin = near_ref[0], near_ref[1]
+    cos = near_cos * far_cos - near_sin * far_sin
+    sin = near_sin * far_cos + near_cos * far_sin
+    first = lax.broadcasted_iota(jnp.int32, sin.shape, 1) < HEAD // 2
+    sin = jnp.where(first, -sin, sin)
 
     def rope(u):
         return u * cos + pltpu.roll(u, HEAD // 2, 1) * sin
 
-    need("kv")
     kv_all = jnp.dot(normed[...], kvw[...], preferred_element_type=F32)
     kb = kb_ref[pl.ds(kvi, 1), :]
     vb = vb_ref[pl.ds(kvi, 1), :]
@@ -333,13 +389,13 @@
 
     for sq in range(2):
         mbuf[sq] = jnp.full((OWN_HEADS * TOK, HEAD), masked_score, F32)
-        lbuf[sq] = jnp.zeros((OWN_HEADS * TOK, HEAD), F32)
-        accbuf[sq] = jnp.zeros((OWN_HEADS * TOK, HEAD), F32)
+        accbuf[sq] = jnp.zeros((OWN_HEADS * TOK, 2 * HEAD), F32)
 
     def attend(sq, yks, zk, diagonal):
         pairs = [kv[sq, yk, zk] for yk in yks]
         kb_ = jnp.concatenate([p[:, :, 0:HEAD].reshape(2 * TOK, HEAD) for p in pairs], axis=0)
         vb_ = jnp.concatenate([p[:, :, HEAD:2 * HEAD].reshape(2 * TOK, HEAD) for p in pairs], axis=0)
+        vb_ = jnp.concatenate([vb_, jnp.ones_like(vb_)], axis=1)
         sc = lax.dot_general(qbuf[sq], kb_, (((1,), (1,)), ((), ())), preferred_element_type=F32)
         if diagonal:
             row = lax.rem(lax.broadcasted_iota(jnp.int32, sc.shape, 0), TOK) + c * TOK
@@ -350,8 +406,7 @@
         p = jnp.exp2((sc - jnp.concatenate([m_new] * (2 * len(yks)), axis=1)) * EXP2_SCALE)
         alpha = jnp.exp2((m_old - m_new) * EXP2_SCALE)
         mbuf[sq] = m_new
-        lbuf[sq] = lbuf[sq] * alpha + jnp.sum(p, axis=1, keepdims=True)
-        accbuf[sq] = accbuf[sq] * alpha + jnp.dot(p.astype(BF16), vb_, preferred_element_type=F32)
+        accbuf[sq] = accbuf[sq] * jnp.concatenate([alpha, alpha], axis=1) + jnp.dot(p.astype(BF16), vb_, preferred_element_type=F32)
 
     def attend_round(sq, k):
         zk = wrap(zk_of(k), NZ)
@@ -375,47 +430,56 @@
     def seq_rows(sq):
         return pl.ds(sq * TOK, TOK)
 
-    def rs1_send(sq, j):
-        return rcx(stage1.at[sq, j], rs1.at[m, seq_rows(sq)], x_send.at[0], x_recv.at[0, sq],
-                   wrap(m + j, MP))
-
-    def three(buf, sq):
-        return buf.at[pl.ds(0, MP - 1), seq_rows(sq)]
+    right, left = wrap(m + 1, MP), wrap(m + MP - 1, MP)
+    FROM_LEFT, FROM_RIGHT = 0, 1
+    X_TR, X_RS, X_AG, X_AGH = range(4)
+
+    def x_copy(src, dst, phase, sq, to):
+        return rcx(src, dst, x_send.at[phase], x_recv.at[phase, sq], to)
+
+    def x_wait(ref, phase, sq):
+        x_copy(ref, ref, phase, sq, right).wait_recv()
 
     def o_project(sq):
         need("ow")
         for h in range(OWN_HEADS):
             r = slice(h * TOK, (h + 1) * TOK)
             attn[sq * TOK:(sq + 1) * TOK, h * HEAD:(h + 1) * HEAD] = (
-                accbuf[sq, r, :] / lbuf[sq, r, :]
+                accbuf[sq, r, 0:HEAD] / accbuf[sq, r, HEAD:2 * HEAD]
             ).astype(BF16)
         here = attn[sq * TOK:(sq + 1) * TOK, :]
         for j in (2, 1, 3, 0):
             part = jnp.dot(here, ow[wrap(m + j, MP)], preferred_element_type=F32).astype(BF16)
-            if j == 0:
-                rs1[m, seq_rows(sq), :] = part
-            else:
-                stage1[sq, j] = part
-        for j in (2, 1, 3):
-            rs1_send(sq, j).start()
-
-    def ag_send(sq, j):
-        ref = resid.at[m, seq_rows(sq)]
-        return rcx(ref, ref, x_send.at[1], x_recv.at[1, sq], wrap(m + j, MP))
+            stage1[sq, j] = part
+            if j == 1:
+                for i, to in ((FROM_LEFT, right), (FROM_RIGHT, left)):
+                    x_copy(stage1.at[sq, 2, pl.ds(i * (TOK // 2), TOK // 2)], tr1.at[sq, i], X_TR, sq, to).start()
+
+    def rs1_mid(sq):
+        x_wait(tr1.at[sq], X_TR, sq)
+        for i, j, to in ((FROM_LEFT, 1, right), (FROM_RIGHT, 3, left)):
+            r = slice(i * (TOK // 2), (i + 1) * (TOK // 2))
+            both = stage1[sq, j, r, :].astype(F32) + tr1[sq, i].astype(F32)
+            stage1[sq, j, r, :] = both.astype(BF16)
+            x_copy(stage1.at[sq, j], rs1.at[i, seq_rows(sq)], X_RS, sq, to).start()
 
     def residual(sq):
         need("hidq")
-        rcx(three(rs1, sq), three(rs1, sq), x_send.at[0], x_recv.at[0, sq], wrap(m + 1, MP)).wait_recv()
         r = seq_rows(sq)
-        add = rs1[0, r, :].astype(F32)
-        for q in range(1, MP):
-            add = add + rs1[q, r, :].astype(F32)
+        x_wait(rs1.at[:, r], X_RS, sq)
+        add = stage1[sq, 0].astype(F32) + rs1[0, r, :].astype(F32) + rs1[1, r, :].astype(F32)
         resid[m, r, :] = (hidq[r, :].astype(F32) + add).astype(BF16)
-        for j in (2, 1, 3):
-            ag_send(sq, j).start()
+        for to in (right, left):
+            x_copy(resid.at[m, r], resid.at[m, r], X_AG, sq, to).start()
+
+    def ag_pass(sq):
+        x_wait(resid.at[TWO, seq_rows(sq)], X_AG, sq)
+        for i, src, to in ((0, left, right), (1, right, left)):
+            ref = resid.at[src, pl.ds(sq * TOK + i * (TOK // 2), TOK // 2)]
+            x_copy(ref, ref, X_AGH, sq, to).start()
 
     def second_norm(sq):
-        rcx(three(resid, sq), three(resid, sq), x_send.at[1], x_recv.at[1, sq], wrap(m + 1, MP)).wait_recv()
+        x_wait(resid.at[0, seq_rows(sq)], X_AGH, sq)
 
         def norm2_rows(i, _):
             r = pl.ds(pl.multiple_of(sq * TOK + i * 16, 16), 16)
@@ -452,9 +516,8 @@
         turn = (0, 2 * odd - 1, 1 - 2 * odd, 2)[i]
         return wrap(z // 2 + turn, NZ // 2)
 
-    def rs2_send(i, j):
-        q = wrap(m + j, MP)
-        return rcx(stage2.at[i, q], rs2.at[i, m], r_send.at[0], r_recv.at[i], q)
+    def r_copy2(src, dst, ssem, rsem, to):
+        return rcx(src, dst, r_send.at[ssem], r_recv.at[rsem], to)
 
     def down_stage(i):
         rounds = pl.ds(0, (3, 2, 2, 1)[i])
@@ -468,16 +531,22 @@
             ).astype(BF16)
             stage2[i, q0] = part[:, 0:HEAD]
             stage2[i, q0 + 1] = part[:, HEAD:2 * HEAD]
-        for j in (2, 1, 3):
-            rs2_send(i, j).start()
+        far_q = wrap(m + 2, MP)
+        for w, to in ((FROM_LEFT, right), (FROM_RIGHT, left)):
+            r_copy2(stage2.at[i, far_q, pl.ds(w * TOK, TOK)], tr2.at[i, w], 0, i, to).start()
+
+    def rs2_mid(i):
+        r_copy2(tr2.at[i], tr2.at[i], 0, i, right).wait_recv()
+        for w, q in ((FROM_LEFT, right), (FROM_RIGHT, left)):
+            r = slice(w * TOK, (w + 1) * TOK)
+            both_ = stage2[i, q, r, :].astype(F32) + tr2[i, w].astype(F32)
+            stage2[i, q, r, :] = both_.astype(BF16)
+            r_copy2(stage2.at[i, q], rs2.at[i, w], 1, 4 + i, q).start()
 
     def layer_stage(i, so_far):
-        came = rs2.at[i, pl.ds(0, MP - 1)]
-        rcx(came, came, r_send.at[0], r_recv.at[i], wrap(m + 1, MP)).wait_recv()
+        r_copy2(rs2.at[i], rs2.at[i], 1, 4 + i, right).wait_recv()
         cols = pl.ds(pl.multiple_of(z_pair(i) * HEAD, HEAD), HEAD)
-        add = stage2[i, m].astype(F32)
-        for j in range(1, MP):
-            add = add + rs2[i, wrap(m - j, MP)].astype(F32)
+        add = stage2[i, m].astype(F32) + rs2[i, 0].astype(F32) + rs2[i, 1].astype(F32)
         layer = (resid[m, :, cols].astype(F32) + add).astype(BF16)
         layer_v[:, cols] = layer
         wide = layer.astype(F32)
@@ -485,7 +554,7 @@
         return (cp, op) if so_far is None else (so_far[0] + cp, so_far[1] + op)
 
     TASKS.update(
-        op=o_project, re=residual, sn=second_norm, gd=gate_dot, ud=up_dot, ds=down_stage,
+        op=o_project, rm=rs1_mid, re=residual, ap=ag_pass, sn=second_norm, xl=swap_last, dm=rs2_mid, gd=gate_dot, ud=up_dot, ds=down_stage,
     )
     items, before, after = [], [], []
     for name, *args in LATER:
@@ -520,7 +589,7 @@
 
         @pl.when(sq == 1)
         def _():
-            b_wait_recv(0, BD + k, ALL, 0, 0)
+            b_all_wait(0, BD + k, ALL, 0, 0)
 
         attend_round(sq, k)
         return 0
@@ -534,10 +603,13 @@
         a_copy(a_ref(st, ALL, seven, ALL), st, 1, 0, partner).wait_send()
         b_copy(st, b_ref(st, 0, pl.ds(0, 3), 0), 0, 0, partner).wait_send()
         b_copy(st, b_ref(st, ALL, seven, 0), 1, 0, partner).wait_send()
-        b_copy(st, b_ref(st, ALL, ALL, 0), 2, 0, partner).wait_send()
-    six = rs1.at[pl.ds(0, MP - 1)]
-    for phase in range(2):
-        rcx(six, six, x_send.at[phase], x_recv.at[0, 0], wrap(m + 1, MP)).wait_send()
+        b_copy(st, b_full(st, ALL, ALL, 0), 2, 0, partner).wait_send()
+    x_copy(rs1.at[0], rs1.at[0], X_TR, 0, right).wait_send()
+    x_copy(rs1, rs1, X_RS, 0, right).wait_send()
+    x_copy(rs1, rs1, X_AG, 0, right).wait_send()
+    x_copy(rs1.at[0], rs1.at[0], X_AGH, 0, right).wait_send()
+    k_copy(kv.at[1, pl.ds(0, NY - 1), 0, 0, pl.ds(0, TOK // 2)], 0).wait_send()
+    k_copy(kv.at[1, :, seven, 0, pl.ds(0, TOK // 2)], 1).wait_send()
 
     def lane_sums(part):
         return jnp.sum(part.T, axis=0, keepdims=True)
@@ -574,15 +646,13 @@
     one = pl.ds(0, 1)
     tot[s, one, :] = jnp.where(lane < HEAD // 2, t0, t1)
 
-    def t_copy(i):
-        ref = tot.at[s, one]
-        return rc(ref, ref, t_sem.at[0], t_sem.at[1], lax.rem(s + i, NS))
-
-    def t_start(i, _):
-        t_copy(i).start()
-        return 0
-
-    lax.fori_loop(1, NS, t_start, 0)
+    for dy in (2, 1, 3, 0):
+        for dz in (4, 3, 5, 2, 6, 1, 7, 0):
+            for cc in (c, 1 - c):
+                if dy == 0 and dz == 0 and cc is c:
+                    continue
+                ref = tot.at[s, one]
+                rc(ref, ref, t_sem.at[0], t_sem.at[1], dev(y + dy, z + dz, cc)).start()
     every = tot.at[pl.ds(0, NS - 1), one]
     rc(every, every, t_sem.at[0], t_sem.at[1], partner).wait()
     total = jnp.sum(tot[:, 0, :], axis=0, keepdims=True)
@@ -591,8 +661,8 @@
     score_ref[0] = jnp.sum(jnp.where(lane == 0, score, 0.0))
     score_ref[1] = jnp.sum(jnp.where(lane == HEAD - 1, score, 0.0))
 
-    gone = rs2.at[pl.ds(0, MP - 1)]
-    rcx(gone, gone, r_send.at[0], r_recv.at[0], wrap(m + 1, MP)).wait_send()
+    r_copy2(tr2, tr2, 0, 0, right).wait_send()
+    r_copy2(rs2, rs2, 1, 0, right).wait_send()
     out_copy.wait()
 
 
@@ -618,15 +688,7 @@
     mlp_gain, gate_weight, up_weight, down_weight, lengths,
 ):
     seqs_n, tok_n, width = hidden_in.shape
-    seq_rank = lax.axis_index("seq")
-    positions = seq_rank * tok_n + jnp.arange(tok_n, dtype=jnp.int32)
-    half_width = HEAD // 2
-    inv_freq = rope_base ** (-(jnp.arange(half_width, dtype=jnp.float32) * 2.0) / HEAD)
-    angles = positions.astype(jnp.float32)[:, None] * inv_freq[None, :]
-    cos = jnp.cos(angles)
-    sin = jnp.sin(angles)
-    cos_t = jnp.concatenate([cos, cos], axis=-1)
-    sin_t = jnp.concatenate([-sin, sin], axis=-1)
+    near, far = rotation_tables()
 
     hbm = pl.BlockSpec(memory_space=pltpu.HBM)
     vmem = pl.BlockSpec(memory_space=pltpu.VMEM)
@@ -640,10 +702,7 @@
     layer_part, influence, score = pl.pallas_call(
         layer_kernel,
         out_shape=results,
-        in_specs=[
-            hbm, vmem, hbm, vmem, hbm, vmem, hbm, vmem, hbm, vmem,
-            hbm, hbm, hbm, vmem, vmem, smem,
-        ],
+        in_specs=[hbm] * 15 + [smem],
         out_specs=(hbm, vmem, smem),
         scratch_shapes=[
             pltpu.VMEM((ROWS, D), BF16),
@@ -657,14 +716,15 @@
             pltpu.VMEM((NY, NZ, 2, WR, 2 * FFP), BF16),
             pltpu.VMEM((NY, NZ, 2, WR, FFP), BF16),
             pltpu.VMEM((2, OWN_HEADS * TOK, HEAD), F32),
-            pltpu.VMEM((2, OWN_HEADS * TOK, HEAD), F32),
-            pltpu.VMEM((2, OWN_HEADS * TOK, HEAD), F32),
+            pltpu.VMEM((2, OWN_HEADS * TOK, 2 * HEAD), F32),
             pltpu.VMEM((ROWS, QCOLS), BF16),
             pltpu.VMEM((2, MP, TOK, QUART), BF16),
-            pltpu.VMEM((MP, ROWS, QUART), BF16),
+            pltpu.VMEM((2, 2, TOK // 2, QUART), BF16),
+            pltpu.VMEM((2, ROWS, QUART), BF16),
             pltpu.VMEM((MP, ROWS, QUART), BF16),
             pltpu.VMEM((4, MP, ROWS, HEAD), BF16),
-            pltpu.VMEM((4, MP, ROWS, HEAD), BF16),
+            pltpu.VMEM((4, 2, TOK, HEAD), BF16),
+            pltpu.VMEM((4, 2, ROWS, HEAD), BF16),
             pltpu.VMEM((ROWS, D), BF16),
             pltpu.VMEM((ROWS, FFP), BF16),
             pltpu.VMEM((ROWS, HEAD), F32),
@@ -672,16 +732,25 @@
             pltpu.VMEM((NS, 8, HEAD), F32),
             pltpu.VMEM((ROWS, FFP), F32),
             pltpu.VMEM((ROWS, QUART), BF16),
-            dma((13,)),
+            pltpu.VMEM((1, D), F32),
+            pltpu.VMEM((1, D), F32),
+            pltpu.VMEM((1, QCOLS), F32),
+            pltpu.VMEM((KV_HEADS, HEAD), F32),
+            pltpu.VMEM((KV_HEADS, HEAD), F32),
+            pltpu.VMEM((2, TOK, HEAD), F32),
+            pltpu.VMEM((2, NS, HEAD), F32),
+            dma((19,)),
             dma((1,)),
             dma((3, 2)),
             dma((3, 28)),
             dma((3, 3)),
             dma((3, 18)),
             dma((2,)),
-            dma((2, 2)),
-            dma((1,)),
+            dma((NZ,)),
             dma((4,)),
+            dma((4, 2)),
+            dma((2,)),
+            dma((8,)),
             dma((2,)),
             dma((2,)),
         ],
@@ -693,7 +762,7 @@
         hidden_in.reshape(ROWS, width), attn_gain.reshape(1, width), q_weight,
         q_bias.reshape(1, QCOLS), k_weight, k_bias.reshape(KV_HEADS, HEAD), v_weight,
         v_bias.reshape(KV_HEADS, HEAD), o_weight, mlp_gain.reshape(1, width), gate_weight,
-        up_weight, down_weight, cos_t, sin_t, lengths,
+        up_weight, down_weight, near, far, lengths,
     )
     layer_part, influence, score = pl.pallas_call(
         finish_kernel,

time: 110 us -> 110 us (level)
  no operation moved by 1% of the time
where the time goes in v4:
time: 110 us
  Pallas kernels  109 us (99%)
    pallas_call x1, Pallas kernels, local(): pl.pallas_call(layer_kernel, out_shape=results, in_specs=[hbm] * 15 + [sm...  107 us

profile of v4, /device:TPU:1, one launch (start us, length us, event | category | flops | bytes accessed | tf_op | source)
XLA Modules:
  0.0 109.6 jit_solution(4218215104906942389)
XLA Ops:
  0.6 107.3 %layer.1 = (bf16[256,512]{1,0:T(8,128)(2,1)}, f32[2,128]{1,0:T(2,128)}, f32[2]{0:T(128)}) custom-call(bf16[256,2048]{1,0:T(8,128)(2,1)} %bitcast.7, f32[1,2048]{1,0:T(1,128)} %bitcast.8, bf16[2048,512]{1,0:T(8,128)(2,1)} %qw_hbm.1, f32[1,512]{1,0:T(1,128)} %bitcast.10, bf16[2048,256]{1,0:T(8,128)(2,1)} %kw_hbm.1, f32[2,128]{1,0:T(2,128)} %bitcast.11, ...), custom_call_target="tpu_custom_call" | custom-call | tf_op jit(solution)/shard_map/layer/pallas_call | solution.py:702
  107.9 1.7 %finish.1 = (bf16[256,512]{1,0:T(8,128)(2,1)}, f32[2,128]{1,0:T(2,128)}, f32[2]{0:T(128)}) custom-call(bf16[256,512]{1,0:T(8,128)(2,1)} %get-tuple-element.9.layer_hbm, f32[2,128]{1,0:T(2,128)} %get-tuple-element.10.infl_hbm, f32[2]{0:T(128)} %get-tuple-element.11.score_hbm), custom_call_target="tpu_custom_call" | custom-call | tf_op jit(solution)/shard_map/finish/pallas_call | solution.py:767

commit v5 on v4

--- a/solution.py
+++ b/solution.py
@@ -43,34 +43,34 @@
 
 Z_OFF = (0, -1, 1, -2, 2, -3, 3, -4)
 
-FAR_RIGHT = (False, True, True)
+FAR_RIGHT = (True, False, True)
 
 EARLY = (
-    ("bs", 2), ("zs", 2), ("zs", 1), ("bs", 1),
+    ("zs", 1), ("bs", 1), ("bs", 2),
 )
 LATER = (
-    ("ys", 2, 0), ("bs", 0), ("zs", 0), ("ys", 0, 0), ("zh", 2, 1), ("bp", 2), ("bp", 1), ("zh", 1, 1),
-    ("yp", 2, 0), ("bp", 0), ("zh", 0, 1), ("yp", 0, 0), ("zh", 2, 2), ("bl", 2), ("bl", 1), ("yl", 2, 0),
-    ("bl", 0), ("bz", 0), ("ys", 1, 0), ("yp", 0, 1), ("zh", 0, 2), ("yp", 0, 2), ("zh", 2, 3), ("yl", 0, 0),
-    ("xl", 0), ("bh", 0, 1, 0), ("at", 0, 0), ("bh", 0, 1, 1), ("yl", 0, 1), ("yp", 1, 0), ("at", 1, 0),
-    ("zh", 1, 2), ("zh", 2, 4), ("zh", 0, 3), ("yp", 0, 3), ("at", 0, 1), ("bh", 0, 2, 0), ("yp", 0, 4),
-    ("yl", 0, 2), ("bh", 0, 2, 1), ("yl", 1, 0), ("xl", 1), ("at", 0, 2), ("yp", 0, 5), ("ys", 1, 1),
-    ("zh", 1, 3), ("at", 1, 1), ("xl", 2), ("zh", 0, 4), ("yp", 0, 6), ("yl", 0, 3), ("yl", 0, 4),
-    ("bh", 0, 3, 0), ("yl", 0, 5), ("xl", 3), ("bh", 0, 3, 1), ("at", 1, 2), ("ys", 1, 2), ("bz", 1),
-    ("at", 0, 3), ("zh", 1, 4), ("yp", 1, 1), ("at", 0, 4), ("bh", 0, 4, 0), ("xl", 4), ("yl", 0, 6),
-    ("bh", 0, 4, 1), ("yp", 0, 7), ("at", 1, 3), ("at", 0, 5), ("xl", 5), ("ys", 1, 3), ("yp", 1, 2),
-    ("bh", 1, 1, 0), ("at", 1, 4), ("yl", 1, 1), ("yl", 0, 7), ("at", 0, 6), ("xl", 6), ("bh", 1, 1, 1),
-    ("ys", 1, 4), ("at", 1, 5), ("at", 0, 7), ("yp", 1, 3), ("xl", 7), ("yl", 1, 2), ("op", 0), ("bz", 2),
-    ("at", 1, 6), ("ys", 1, 5), ("at", 1, 7), ("yp", 1, 4), ("op", 1), ("bh", 1, 2, 0), ("yl", 1, 3),
-    ("bh", 1, 2, 1), ("rm", 0), ("bh", 2, 1, 0), ("ys", 1, 6), ("yp", 1, 5), ("bh", 2, 1, 1), ("rm", 1),
-    ("yl", 1, 4), ("ys", 1, 7), ("bh", 1, 3, 0), ("re", 0), ("yp", 1, 6), ("yl", 1, 5), ("bh", 1, 3, 1),
-    ("ys", 2, 1), ("re", 1), ("ys", 2, 2), ("yp", 1, 7), ("bh", 2, 2, 0), ("yl", 1, 6), ("ap", 0),
-    ("ys", 2, 3), ("yp", 2, 1), ("bh", 2, 2, 1), ("yp", 2, 2), ("ys", 2, 4), ("yl", 1, 7), ("ys", 2, 5),
-    ("ap", 1), ("yp", 2, 3), ("yl", 2, 1), ("bh", 1, 4, 0), ("bh", 1, 4, 1), ("ys", 2, 6), ("sn", 0),
-    ("yl", 2, 2), ("ys", 2, 7), ("yp", 2, 4), ("yp", 2, 5), ("bh", 2, 3, 0), ("sn", 1), ("gd",),
-    ("bh", 2, 3, 1), ("yp", 2, 6), ("yl", 2, 3), ("yp", 2, 7), ("ud",), ("bh", 2, 4, 0), ("yl", 2, 4),
-    ("yl", 2, 5), ("ds", 0), ("yl", 2, 6), ("yl", 2, 7), ("ds", 1), ("bh", 2, 4, 1), ("ds", 2), ("dm", 0),
-    ("ds", 3), ("dm", 1), ("dm", 2), ("dm", 3),
+    ("bs", 0), ("zs", 0), ("ys", 0, 0), ("qp",), ("bp", 1), ("zs", 2), ("zh", 1, 1), ("bp", 2), ("bp", 0),
+    ("zh", 0, 1), ("yp", 0, 0), ("bl", 1), ("bl", 2), ("bl", 0), ("bz", 0), ("ys", 1, 0), ("yp", 0, 1),
+    ("zh", 0, 2), ("yp", 0, 2), ("yl", 0, 0), ("bh", 0, 1, 0), ("xl", 0), ("bh", 0, 1, 1), ("at", 0, 0),
+    ("zh", 1, 2), ("yp", 1, 0), ("zh", 0, 3), ("yl", 0, 1), ("at", 1, 0), ("bh", 0, 2, 0), ("yp", 0, 3),
+    ("at", 0, 1), ("bh", 0, 2, 1), ("xl", 1), ("yp", 0, 4), ("yl", 0, 2), ("yl", 1, 0), ("at", 1, 1),
+    ("xl", 2), ("yp", 0, 5), ("at", 0, 2), ("bz", 1), ("ys", 1, 1), ("zh", 0, 4), ("yp", 0, 6),
+    ("bh", 0, 3, 0), ("yl", 0, 3), ("at", 1, 2), ("xl", 3), ("yl", 0, 4), ("bh", 0, 3, 1), ("yl", 0, 5),
+    ("at", 0, 3), ("at", 1, 3), ("xl", 4), ("yp", 1, 1), ("bh", 1, 1, 0), ("at", 0, 4), ("ys", 1, 2),
+    ("yp", 0, 7), ("at", 0, 5), ("xl", 5), ("yl", 0, 6), ("at", 1, 4), ("bh", 1, 1, 1), ("yl", 1, 1),
+    ("ys", 1, 3), ("bh", 0, 4, 0), ("bh", 0, 4, 1), ("at", 1, 5), ("xl", 6), ("at", 0, 6), ("ys", 1, 4),
+    ("yp", 1, 2), ("yl", 0, 7), ("bh", 1, 2, 0), ("at", 1, 6), ("xl", 7), ("bh", 1, 2, 1), ("yp", 1, 3),
+    ("at", 0, 7), ("op", 0), ("yp", 1, 4), ("at", 1, 7), ("zh", 1, 3), ("ys", 1, 5), ("yl", 1, 2),
+    ("bh", 1, 3, 0), ("op", 1), ("yl", 1, 3), ("rm", 0), ("yl", 1, 4), ("ys", 1, 6), ("bh", 1, 3, 1),
+    ("rm", 1), ("yp", 1, 5), ("zh", 1, 4), ("zh", 2, 1), ("bh", 1, 4, 0), ("ys", 1, 7), ("bz", 2), ("re", 0),
+    ("yp", 1, 6), ("bh", 1, 4, 1), ("yl", 1, 5), ("re", 1), ("ys", 2, 0), ("zh", 2, 2), ("ys", 2, 1),
+    ("yp", 1, 7), ("bh", 2, 1, 0), ("yl", 1, 6), ("ap", 0), ("ys", 2, 2), ("yp", 2, 0), ("bh", 2, 1, 1),
+    ("yp", 2, 1), ("ys", 2, 3), ("yl", 1, 7), ("ap", 1), ("ys", 2, 4), ("zh", 2, 3), ("yp", 2, 2),
+    ("bh", 2, 2, 0), ("yl", 2, 0), ("sn", 0), ("ys", 2, 5), ("yl", 2, 1), ("yp", 2, 3), ("bh", 2, 2, 1),
+    ("ys", 2, 6), ("sn", 1), ("zh", 2, 4), ("yp", 2, 4), ("gd",), ("ys", 2, 7), ("yl", 2, 2), ("yl", 2, 3),
+    ("yp", 2, 5), ("bh", 2, 3, 0), ("ud",), ("yl", 2, 4), ("yp", 2, 6), ("bh", 2, 3, 1), ("ds", 0),
+    ("yp", 2, 7), ("yl", 2, 5), ("ds", 1), ("bh", 2, 4, 0), ("yl", 2, 6), ("yl", 2, 7), ("dm", 0), ("ds", 2),
+    ("bh", 2, 4, 1), ("dm", 1), ("ds", 3), ("dm", 2), ("dm", 3),
 )
 
 
@@ -78,7 +78,7 @@
     hid_hbm, ag_hbm, qw_hbm, qb_hbm, kw_hbm, kb_hbm, vw_hbm, vb_hbm, ow_hbm, mg_hbm,
     gate_hbm, up_hbm, down_hbm, near_hbm, far_hbm, len_ref,
     out_hbm, infl_ref, score_ref,
-    hid, hidq, normed, qw, kvw, ow, qbuf, kv, gu, down, mbuf, accbuf, attn,
+    hid, hidq, normed, qw, kvw, ow, qbuf, kv, gu, down, mbuf, lbuf, accbuf, attn,
     stage1, tr1, rs1, resid, stage2, tr2, rs2, mlp_in, act, innp, sums, tot, gbuf, layer_v,
     ag_ref, mg_ref, qb_ref, kb_ref, vb_ref, near_ref, far_ref,
     lsem, osem, a_send, a_recv, b_send, b_recv, k_send, k_recv, x_send, x_recv, r_send, r_recv,
@@ -115,6 +115,7 @@
 
     kv_cols = pl.ds(pl.multiple_of(kvi * HEAD, HEAD), HEAD)
     own = gu.at[y, z, c]
+    ow_here = []
 
     def group_of(index, *pairs):
         return [pltpu.make_async_copy(a, b, lsem.at[index + i]) for i, (a, b) in enumerate(pairs)]
@@ -131,13 +132,19 @@
         "down": group_of(12, (down_hbm, down.at[y, z, c])),
         "hidq": group_of(
             13, (hid_hbm.at[:, pl.ds(pl.multiple_of(m * QUART, QUART), QUART)], hidq), (mg_hbm, mg_ref)),
-        "ow": group_of(15, *((ow_hbm.at[:, pl.ds(q * QUART, QUART)], ow.at[q]) for q in range(MP))),
     }
     for copies in loads.values():
         for copy in copies:
             copy.start()
 
+    for q in range(MP):
+        pltpu.make_async_copy(ow_hbm.at[:, pl.ds(q * QUART, QUART)], ow.at[q], lsem.at[15]).start()
+
     def need(name):
+        if name == "ow":
+            if not ow_here:
+                pltpu.make_async_copy(ow, ow, lsem.at[15]).wait()
+                ow_here.append(True)
         for copy in loads.pop(name, ()):
             copy.wait()
 
@@ -171,7 +178,7 @@
         return ref.at[pl.ds(i * A_HALF[st], A_HALF[st])]
 
     def a_copy(ref, st, ssem, rsem, d):
-        return rc(ref, ref, a_send.at[st, ssem], a_recv.at[st, rsem], d)
+        return rc(ref, ref, a_send.at[st, ssem], a_recv.at[(0, 28, 49)[st] + rsem], d)
 
     def a_wait_recv(st, rsem, *size):
         a_copy(a_ref(st, *size), st, 0, rsem, partner).wait_recv()
@@ -242,7 +249,7 @@
         return b_full(st, yy, zz, cc)
 
     def b_copy(st, ref, ssem, rsem, d):
-        return rc(ref, ref, b_send.at[st, ssem], b_recv.at[st, rsem], d)
+        return rc(ref, ref, b_send.at[st, ssem], b_recv.at[(0, 18, 29)[st] + rsem], d)
 
     def b_wait_recv(st, rsem, *size):
         b_copy(st, b_ref(st, *size), 0, rsem, partner).wait_recv()
@@ -286,7 +293,7 @@
 
     def b_all_wait(st, rsem, *size):
         ref = b_full(st, *size)
-        rc(ref, ref, b_send.at[st, 2], b_recv.at[st, rsem], partner).wait_recv()
+        rc(ref, ref, b_send.at[st, 2], b_recv.at[(0, 18, 29)[st] + rsem], partner).wait_recv()
 
     def bd_start(st, k):
         b_copy(st, b_full(st, ALL, wrap(zk_of(k), NZ), c), 2,
@@ -380,22 +387,23 @@
         kv[sq, y, z, c, :, 0:HEAD] = rope(kk).astype(BF16)
         kv[sq, y, z, c, :, HEAD:2 * HEAD] = vv.astype(BF16)
 
-    need("q")
-    q_all = jnp.dot(normed[...], qw[...], preferred_element_type=F32) + qb_ref[...]
-    for sq in range(2):
-        for h in range(OWN_HEADS):
-            u = q_all[sq * TOK:(sq + 1) * TOK, h * HEAD:(h + 1) * HEAD]
-            qbuf[sq, h * TOK:(h + 1) * TOK, :] = rope(u).astype(BF16)
-
     for sq in range(2):
         mbuf[sq] = jnp.full((OWN_HEADS * TOK, HEAD), masked_score, F32)
-        accbuf[sq] = jnp.zeros((OWN_HEADS * TOK, 2 * HEAD), F32)
+        lbuf[sq] = jnp.zeros((OWN_HEADS * TOK, HEAD), F32)
+        accbuf[sq] = jnp.zeros((OWN_HEADS * TOK, HEAD), F32)
+
+    def queries():
+        need("q")
+        q_all = jnp.dot(normed[...], qw[...], preferred_element_type=F32) + qb_ref[...]
+        for sq in range(2):
+            for h in range(OWN_HEADS):
+                u = q_all[sq * TOK:(sq + 1) * TOK, h * HEAD:(h + 1) * HEAD]
+                qbuf[sq, h * TOK:(h + 1) * TOK, :] = rope(u).astype(BF16)
 
     def attend(sq, yks, zk, diagonal):
         pairs = [kv[sq, yk, zk] for yk in yks]
         kb_ = jnp.concatenate([p[:, :, 0:HEAD].reshape(2 * TOK, HEAD) for p in pairs], axis=0)
         vb_ = jnp.concatenate([p[:, :, HEAD:2 * HEAD].reshape(2 * TOK, HEAD) for p in pairs], axis=0)
-        vb_ = jnp.concatenate([vb_, jnp.ones_like(vb_)], axis=1)
         sc = lax.dot_general(qbuf[sq], kb_, (((1,), (1,)), ((), ())), preferred_element_type=F32)
         if diagonal:
             row = lax.rem(lax.broadcasted_iota(jnp.int32, sc.shape, 0), TOK) + c * TOK
@@ -406,7 +414,11 @@
         p = jnp.exp2((sc - jnp.concatenate([m_new] * (2 * len(yks)), axis=1)) * EXP2_SCALE)
         alpha = jnp.exp2((m_old - m_new) * EXP2_SCALE)
         mbuf[sq] = m_new
-        accbuf[sq] = accbuf[sq] * jnp.concatenate([alpha, alpha], axis=1) + jnp.dot(p.astype(BF16), vb_, preferred_element_type=F32)
+        part = p[:, 0:HEAD]
+        for i in range(1, 2 * len(yks)):
+            part = part + p[:, i * HEAD:(i + 1) * HEAD]
+        lbuf[sq] = lbuf[sq] * alpha + part
+        accbuf[sq] = accbuf[sq] * alpha + jnp.dot(p.astype(BF16), vb_, preferred_element_type=F32)
 
     def attend_round(sq, k):
         zk = wrap(zk_of(k), NZ)
@@ -417,15 +429,10 @@
 
         n = y + jnp.where(zk < z, 1, 0)
 
-        def step(i, _):
-            attend(sq, (2 * i, 2 * i + 1), zk, False)
-            return 0
-
-        lax.fori_loop(0, n // 2, step, 0)
-
-        @pl.when(lax.rem(n, 2) == 1)
-        def _():
-            attend(sq, (n - 1,), zk, False)
+        for count in range(1, NY + 1):
+            @pl.when(n == count)
+            def _():
+                attend(sq, tuple(range(count)), zk, False)
 
     def seq_rows(sq):
         return pl.ds(sq * TOK, TOK)
@@ -445,7 +452,7 @@
         for h in range(OWN_HEADS):
             r = slice(h * TOK, (h + 1) * TOK)
             attn[sq * TOK:(sq + 1) * TOK, h * HEAD:(h + 1) * HEAD] = (
-                accbuf[sq, r, 0:HEAD] / accbuf[sq, r, HEAD:2 * HEAD]
+                accbuf[sq, r, :] / jnp.sum(lbuf[sq, r, :], axis=1, keepdims=True)
             ).astype(BF16)
         here = attn[sq * TOK:(sq + 1) * TOK, :]
         for j in (2, 1, 3, 0):
@@ -554,7 +561,7 @@
         return (cp, op) if so_far is None else (so_far[0] + cp, so_far[1] + op)
 
     TASKS.update(
-        op=o_project, rm=rs1_mid, re=residual, ap=ag_pass, sn=second_norm, xl=swap_last, dm=rs2_mid, gd=gate_dot, ud=up_dot, ds=down_stage,
+        qp=queries, op=o_project, rm=rs1_mid, re=residual, ap=ag_pass, sn=second_norm, xl=swap_last, dm=rs2_mid, gd=gate_dot, ud=up_dot, ds=down_stage,
     )
     items, before, after = [], [], []
     for name, *args in LATER:
@@ -716,7 +723,8 @@
             pltpu.VMEM((NY, NZ, 2, WR, 2 * FFP), BF16),
             pltpu.VMEM((NY, NZ, 2, WR, FFP), BF16),
             pltpu.VMEM((2, OWN_HEADS * TOK, HEAD), F32),
-            pltpu.VMEM((2, OWN_HEADS * TOK, 2 * HEAD), F32),
+            pltpu.VMEM((2, OWN_HEADS * TOK, HEAD), F32),
+            pltpu.VMEM((2, OWN_HEADS * TOK, HEAD), F32),
             pltpu.VMEM((ROWS, QCOLS), BF16),
             pltpu.VMEM((2, MP, TOK, QUART), BF16),
             pltpu.VMEM((2, 2, TOK // 2, QUART), BF16),
@@ -739,12 +747,12 @@
             pltpu.VMEM((KV_HEADS, HEAD), F32),
             pltpu.VMEM((2, TOK, HEAD), F32),
             pltpu.VMEM((2, NS, HEAD), F32),
-            dma((19,)),
+            dma((16,)),
             dma((1,)),
             dma((3, 2)),
-            dma((3, 28)),
+            dma((73,)),
             dma((3, 3)),
-            dma((3, 18)),
+            dma((43,)),
             dma((2,)),
             dma((NZ,)),
             dma((4,)),

time: 110 us -> 107 us (0.973)
  Pallas kernels: 109 us -> 106 us
    pallas_call x1, Pallas kernels: 107 us -> 104 us  [local(): pl.pallas_call(layer_kernel, out_shape=results, in_specs=[hbm] * 15 + [sm...]
where the time goes in v5:
time: 107 us; the launch traced here: 106 us
  Pallas kernels  106 us (99%)
    pallas_call x1, Pallas kernels, local(): pl.pallas_call(layer_kernel, out_shape=results, in_specs=[hbm] * 15 + [sm...  104 us

profile of v5, /device:TPU:1, one launch (start us, length us, event | category | flops | bytes accessed | tf_op | source)
XLA Modules:
  0.0 106.5 jit_solution(2795740817761662499)
XLA Ops:
  0.6 104.0 %layer.1 = (bf16[256,512]{1,0:T(8,128)(2,1)}, f32[2,128]{1,0:T(2,128)}, f32[2]{0:T(128)}) custom-call(bf16[256,2048]{1,0:T(8,128)(2,1)} %bitcast.7, f32[1,2048]{1,0:T(1,128)} %bitcast.8, bf16[2048,512]{1,0:T(8,128)(2,1)} %qw_hbm.1, f32[1,512]{1,0:T(1,128)} %bitcast.10, bf16[2048,256]{1,0:T(8,128)(2,1)} %kw_hbm.1, f32[2,128]{1,0:T(2,128)} %bitcast.11, ...), custom_call_target="tpu_custom_call" | custom-call | tf_op jit(solution)/shard_map/layer/pallas_call | solution.py:709
  104.6 1.7 %finish.1 = (bf16[256,512]{1,0:T(8,128)(2,1)}, f32[2,128]{1,0:T(2,128)}, f32[2]{0:T(128)}) custom-call(bf16[256,512]{1,0:T(8,128)(2,1)} %get-tuple-element.9.layer_hbm, f32[2,128]{1,0:T(2,128)} %get-tuple-element.10.infl_hbm, f32[2]{0:T(128)} %get-tuple-element.11.score_hbm), custom_call_target="tpu_custom_call" | custom-call | tf_op jit(solution)/shard_map/finish/pallas_call | solution.py:775

commit v6 on v5

--- a/solution.py
+++ b/solution.py
@@ -43,44 +43,44 @@
 
 Z_OFF = (0, -1, 1, -2, 2, -3, 3, -4)
 
-FAR_RIGHT = (True, False, True)
+FAR_RIGHT = (False, True, True)
 
 EARLY = (
     ("zs", 1), ("bs", 1), ("bs", 2),
 )
 LATER = (
-    ("bs", 0), ("zs", 0), ("ys", 0, 0), ("qp",), ("bp", 1), ("zs", 2), ("zh", 1, 1), ("bp", 2), ("bp", 0),
-    ("zh", 0, 1), ("yp", 0, 0), ("bl", 1), ("bl", 2), ("bl", 0), ("bz", 0), ("ys", 1, 0), ("yp", 0, 1),
-    ("zh", 0, 2), ("yp", 0, 2), ("yl", 0, 0), ("bh", 0, 1, 0), ("xl", 0), ("bh", 0, 1, 1), ("at", 0, 0),
-    ("zh", 1, 2), ("yp", 1, 0), ("zh", 0, 3), ("yl", 0, 1), ("at", 1, 0), ("bh", 0, 2, 0), ("yp", 0, 3),
-    ("at", 0, 1), ("bh", 0, 2, 1), ("xl", 1), ("yp", 0, 4), ("yl", 0, 2), ("yl", 1, 0), ("at", 1, 1),
-    ("xl", 2), ("yp", 0, 5), ("at", 0, 2), ("bz", 1), ("ys", 1, 1), ("zh", 0, 4), ("yp", 0, 6),
-    ("bh", 0, 3, 0), ("yl", 0, 3), ("at", 1, 2), ("xl", 3), ("yl", 0, 4), ("bh", 0, 3, 1), ("yl", 0, 5),
-    ("at", 0, 3), ("at", 1, 3), ("xl", 4), ("yp", 1, 1), ("bh", 1, 1, 0), ("at", 0, 4), ("ys", 1, 2),
-    ("yp", 0, 7), ("at", 0, 5), ("xl", 5), ("yl", 0, 6), ("at", 1, 4), ("bh", 1, 1, 1), ("yl", 1, 1),
-    ("ys", 1, 3), ("bh", 0, 4, 0), ("bh", 0, 4, 1), ("at", 1, 5), ("xl", 6), ("at", 0, 6), ("ys", 1, 4),
-    ("yp", 1, 2), ("yl", 0, 7), ("bh", 1, 2, 0), ("at", 1, 6), ("xl", 7), ("bh", 1, 2, 1), ("yp", 1, 3),
-    ("at", 0, 7), ("op", 0), ("yp", 1, 4), ("at", 1, 7), ("zh", 1, 3), ("ys", 1, 5), ("yl", 1, 2),
-    ("bh", 1, 3, 0), ("op", 1), ("yl", 1, 3), ("rm", 0), ("yl", 1, 4), ("ys", 1, 6), ("bh", 1, 3, 1),
-    ("rm", 1), ("yp", 1, 5), ("zh", 1, 4), ("zh", 2, 1), ("bh", 1, 4, 0), ("ys", 1, 7), ("bz", 2), ("re", 0),
-    ("yp", 1, 6), ("bh", 1, 4, 1), ("yl", 1, 5), ("re", 1), ("ys", 2, 0), ("zh", 2, 2), ("ys", 2, 1),
-    ("yp", 1, 7), ("bh", 2, 1, 0), ("yl", 1, 6), ("ap", 0), ("ys", 2, 2), ("yp", 2, 0), ("bh", 2, 1, 1),
-    ("yp", 2, 1), ("ys", 2, 3), ("yl", 1, 7), ("ap", 1), ("ys", 2, 4), ("zh", 2, 3), ("yp", 2, 2),
-    ("bh", 2, 2, 0), ("yl", 2, 0), ("sn", 0), ("ys", 2, 5), ("yl", 2, 1), ("yp", 2, 3), ("bh", 2, 2, 1),
-    ("ys", 2, 6), ("sn", 1), ("zh", 2, 4), ("yp", 2, 4), ("gd",), ("ys", 2, 7), ("yl", 2, 2), ("yl", 2, 3),
-    ("yp", 2, 5), ("bh", 2, 3, 0), ("ud",), ("yl", 2, 4), ("yp", 2, 6), ("bh", 2, 3, 1), ("ds", 0),
-    ("yp", 2, 7), ("yl", 2, 5), ("ds", 1), ("bh", 2, 4, 0), ("yl", 2, 6), ("yl", 2, 7), ("dm", 0), ("ds", 2),
-    ("bh", 2, 4, 1), ("dm", 1), ("ds", 3), ("dm", 2), ("dm", 3),
+    ("bs", 0), ("qp",), ("zs", 2), ("zs", 0), ("ys", 0, 0), ("bp", 1), ("zh", 1, 1), ("bp", 2), ("bp", 0),
+    ("ys", 1, 0), ("zh", 2, 1), ("yp", 0, 0), ("zh", 0, 1), ("bl", 1), ("bl", 2), ("bl", 0), ("bz", 0),
+    ("yp", 1, 0), ("zh", 1, 2), ("yl", 0, 0), ("zh", 0, 2), ("xl", 0), ("yp", 0, 1), ("bh", 0, 1, 0),
+    ("at", 0, 0), ("bh", 0, 1, 1), ("yp", 0, 2), ("at", 1, 0), ("yl", 1, 0), ("yp", 0, 3), ("ys", 1, 1),
+    ("zh", 1, 3), ("yp", 0, 4), ("zh", 0, 3), ("yl", 0, 1), ("yl", 0, 2), ("bh", 0, 2, 0), ("xl", 1),
+    ("yl", 0, 3), ("at", 0, 1), ("bh", 0, 2, 1), ("at", 0, 2), ("xl", 2), ("yp", 1, 1), ("at", 0, 3),
+    ("bz", 1), ("zh", 1, 4), ("yl", 0, 4), ("zh", 0, 4), ("at", 1, 1), ("bh", 0, 3, 0), ("yp", 0, 5),
+    ("at", 1, 2), ("bh", 0, 3, 1), ("at", 0, 4), ("yl", 1, 1), ("ys", 1, 2), ("xl", 3), ("yp", 0, 6),
+    ("yp", 0, 7), ("bh", 1, 1, 0), ("yl", 0, 5), ("xl", 4), ("at", 1, 3), ("bh", 1, 1, 1), ("ys", 1, 3),
+    ("at", 0, 5), ("xl", 5), ("yp", 1, 2), ("bh", 0, 4, 0), ("bh", 0, 4, 1), ("yl", 0, 6), ("at", 1, 4),
+    ("yl", 0, 7), ("xl", 6), ("ys", 1, 4), ("at", 1, 5), ("bh", 1, 2, 0), ("at", 0, 6), ("yp", 1, 3),
+    ("at", 0, 7), ("xl", 7), ("bh", 1, 2, 1), ("yl", 1, 2), ("ys", 1, 5), ("op", 0), ("at", 1, 6),
+    ("yp", 1, 4), ("at", 1, 7), ("yl", 1, 3), ("zh", 2, 2), ("bh", 1, 3, 0), ("op", 1), ("ys", 1, 6),
+    ("rm", 0), ("yp", 1, 5), ("bh", 1, 3, 1), ("yl", 1, 4), ("rm", 1), ("ys", 1, 7), ("bz", 2), ("yp", 1, 6),
+    ("bh", 1, 4, 0), ("re", 0), ("yl", 1, 5), ("bh", 1, 4, 1), ("ys", 2, 0), ("zh", 2, 3), ("ys", 2, 1),
+    ("yp", 1, 7), ("bh", 2, 1, 0), ("re", 1), ("yl", 1, 6), ("ys", 2, 2), ("yp", 2, 0), ("bh", 2, 1, 1),
+    ("zh", 2, 4), ("yp", 2, 1), ("ap", 0), ("ys", 2, 3), ("yl", 1, 7), ("bh", 2, 2, 0), ("ys", 2, 4),
+    ("yp", 2, 2), ("yl", 2, 0), ("ap", 1), ("ys", 2, 5), ("yl", 2, 1), ("bh", 2, 2, 1), ("ys", 2, 6),
+    ("yp", 2, 3), ("sn", 0), ("yp", 2, 4), ("yl", 2, 2), ("ys", 2, 7), ("bh", 2, 3, 0), ("yp", 2, 5),
+    ("sn", 1), ("gd",), ("yp", 2, 6), ("yl", 2, 3), ("yl", 2, 4), ("bh", 2, 3, 1), ("yp", 2, 7), ("ud",),
+    ("yl", 2, 5), ("bh", 2, 4, 0), ("ds", 0), ("yl", 2, 6), ("ds", 1), ("yl", 2, 7), ("bh", 2, 4, 1),
+    ("ds", 2), ("dm", 0), ("ds", 3), ("dm", 1), ("dm", 2), ("dm", 3),
 )
 
 
 def layer_kernel(
     hid_hbm, ag_hbm, qw_hbm, qb_hbm, kw_hbm, kb_hbm, vw_hbm, vb_hbm, ow_hbm, mg_hbm,
-    gate_hbm, up_hbm, down_hbm, near_hbm, far_hbm, len_ref,
+    gate_hbm, up_hbm, down_hbm, near_hbm, far_hbm, len_hbm,
     out_hbm, infl_ref, score_ref,
     hid, hidq, normed, qw, kvw, ow, qbuf, kv, gu, down, mbuf, lbuf, accbuf, attn,
     stage1, tr1, rs1, resid, stage2, tr2, rs2, mlp_in, act, innp, sums, tot, gbuf, layer_v,
-    ag_ref, mg_ref, qb_ref, kb_ref, vb_ref, near_ref, far_ref,
+    ag_ref, mg_ref, qb_ref, kb_ref, vb_ref, near_ref, far_ref, len_ref,
     lsem, osem, a_send, a_recv, b_send, b_recv, k_send, k_recv, x_send, x_recv, r_send, r_recv,
     s_sem, t_sem,
 ):
@@ -113,6 +113,12 @@
             device_id={"seq": s, "mp": mdev}, device_id_type=MESH,
         )
 
+    bar = pltpu.get_barrier_semaphore()
+    for peer in (zp, zm, yp, ym, partner):
+        pl.semaphore_signal(bar, inc=1, device_id={"seq": peer, "mp": m}, device_id_type=MESH)
+    for i in range(1, MP):
+        pl.semaphore_signal(bar, inc=1, device_id={"seq": s, "mp": wrap(m + i, MP)}, device_id_type=MESH)
+
     kv_cols = pl.ds(pl.multiple_of(kvi * HEAD, HEAD), HEAD)
     own = gu.at[y, z, c]
     ow_here = []
@@ -129,6 +135,7 @@
             (vw_hbm.at[:, kv_cols], kvw.at[:, pl.ds(HEAD, HEAD)]),
             (kb_hbm, kb_ref), (vb_hbm, vb_ref), (near_hbm, near_ref), (far_hbm, far_ref)),
         "q": group_of(10, (qw_hbm, qw), (qb_hbm, qb_ref)),
+        "len": group_of(16, (len_hbm, len_ref)),
         "down": group_of(12, (down_hbm, down.at[y, z, c])),
         "hidq": group_of(
             13, (hid_hbm.at[:, pl.ds(pl.multiple_of(m * QUART, QUART), QUART)], hidq), (mg_hbm, mg_ref)),
@@ -148,11 +155,6 @@
         for copy in loads.pop(name, ()):
             copy.wait()
 
-    bar = pltpu.get_barrier_semaphore()
-    for peer in (zp, zm, yp, ym, partner):
-        pl.semaphore_signal(bar, inc=1, device_id={"seq": peer, "mp": m}, device_id_type=MESH)
-    for i in range(1, MP):
-        pl.semaphore_signal(bar, inc=1, device_id={"seq": s, "mp": wrap(m + i, MP)}, device_id_type=MESH)
     pl.semaphore_wait(bar, 5 + MP - 1)
 
     ALL = slice(None)
@@ -621,6 +623,7 @@
     def lane_sums(part):
         return jnp.sum(part.T, axis=0, keepdims=True)
 
+    need("len")
     in_norm = lane_sums(innp[...])
 
     so_far = None
@@ -709,7 +712,7 @@
     layer_part, influence, score = pl.pallas_call(
         layer_kernel,
         out_shape=results,
-        in_specs=[hbm] * 15 + [smem],
+        in_specs=[hbm] * 16,
         out_specs=(hbm, vmem, smem),
         scratch_shapes=[
             pltpu.VMEM((ROWS, D), BF16),
@@ -747,7 +750,8 @@
             pltpu.VMEM((KV_HEADS, HEAD), F32),
             pltpu.VMEM((2, TOK, HEAD), F32),
             pltpu.VMEM((2, NS, HEAD), F32),
-            dma((16,)),
+            pltpu.SMEM((2,), jnp.int32),
+            dma((17,)),
             dma((1,)),
             dma((3, 2)),
             dma((73,)),

time: 107 us -> 105 us (0.981)
  Pallas kernels: 106 us -> 104 us
    pallas_call x1, Pallas kernels: 104 us -> 103 us  [local(): pl.pallas_call(layer_kernel, out_shape=results, in_specs=[hbm] * 16, out_...]
where the time goes in v6:
time: 105 us
  Pallas kernels  104 us (99%)
    pallas_call x1, Pallas kernels, local(): pl.pallas_call(layer_kernel, out_shape=results, in_specs=[hbm] * 16, out_...  103 us

profile of v6, /device:TPU:1, one launch (start us, length us, event | category | flops | bytes accessed | tf_op | source)
XLA Modules:
  0.0 105.2 jit_solution(7375036645555582991)
XLA Ops:
  0.6 102.7 %layer.1 = (bf16[256,512]{1,0:T(8,128)(2,1)}, f32[2,128]{1,0:T(2,128)}, f32[2]{0:T(128)}) custom-call(bf16[256,2048]{1,0:T(8,128)(2,1)} %bitcast.7, f32[1,2048]{1,0:T(1,128)} %bitcast.8, bf16[2048,512]{1,0:T(8,128)(2,1)} %qw_hbm.1, f32[1,512]{1,0:T(1,128)} %bitcast.10, bf16[2048,256]{1,0:T(8,128)(2,1)} %kw_hbm.1, f32[2,128]{1,0:T(2,128)} %bitcast.11, ...), custom_call_target="tpu_custom_call" | custom-call | tf_op jit(solution)/shard_map/layer/pallas_call | solution.py:712
  103.4 1.7 %finish.1 = (bf16[256,512]{1,0:T(8,128)(2,1)}, f32[2,128]{1,0:T(2,128)}, f32[2]{0:T(128)}) custom-call(bf16[256,512]{1,0:T(8,128)(2,1)} %get-tuple-element.9.layer_hbm, f32[2,128]{1,0:T(2,128)} %get-tuple-element.10.infl_hbm, f32[2]{0:T(128)} %get-tuple-element.11.score_hbm), custom_call_target="tpu_custom_call" | custom-call | tf_op jit(solution)/shard_map/finish/pallas_call | solution.py:779

commit v7 on v6

--- a/solution.py
+++ b/solution.py
@@ -43,33 +43,33 @@
 
 Z_OFF = (0, -1, 1, -2, 2, -3, 3, -4)
 
-FAR_RIGHT = (False, True, True)
+FAR_RIGHT = (True, False, True)
 
 EARLY = (
     ("zs", 1), ("bs", 1), ("bs", 2),
 )
 LATER = (
     ("bs", 0), ("qp",), ("zs", 2), ("zs", 0), ("ys", 0, 0), ("bp", 1), ("zh", 1, 1), ("bp", 2), ("bp", 0),
-    ("ys", 1, 0), ("zh", 2, 1), ("yp", 0, 0), ("zh", 0, 1), ("bl", 1), ("bl", 2), ("bl", 0), ("bz", 0),
-    ("yp", 1, 0), ("zh", 1, 2), ("yl", 0, 0), ("zh", 0, 2), ("xl", 0), ("yp", 0, 1), ("bh", 0, 1, 0),
-    ("at", 0, 0), ("bh", 0, 1, 1), ("yp", 0, 2), ("at", 1, 0), ("yl", 1, 0), ("yp", 0, 3), ("ys", 1, 1),
-    ("zh", 1, 3), ("yp", 0, 4), ("zh", 0, 3), ("yl", 0, 1), ("yl", 0, 2), ("bh", 0, 2, 0), ("xl", 1),
-    ("yl", 0, 3), ("at", 0, 1), ("bh", 0, 2, 1), ("at", 0, 2), ("xl", 2), ("yp", 1, 1), ("at", 0, 3),
-    ("bz", 1), ("zh", 1, 4), ("yl", 0, 4), ("zh", 0, 4), ("at", 1, 1), ("bh", 0, 3, 0), ("yp", 0, 5),
+    ("ys", 1, 0), ("yp", 0, 0), ("zh", 2, 1), ("zh", 0, 1), ("bl", 1), ("bl", 2), ("bl", 0), ("bz", 0),
+    ("zh", 1, 2), ("yp", 1, 0), ("yl", 0, 0), ("zh", 0, 2), ("xl", 0), ("yp", 0, 1), ("bh", 0, 1, 0),
+    ("at", 0, 0), ("bh", 0, 1, 1), ("yp", 0, 2), ("at", 1, 0), ("yl", 1, 0), ("yp", 0, 3), ("zh", 1, 3),
+    ("ys", 1, 1), ("yp", 0, 4), ("zh", 0, 3), ("yl", 0, 1), ("yl", 0, 2), ("bh", 0, 2, 0), ("xl", 1),
+    ("yl", 0, 3), ("at", 0, 1), ("bh", 0, 2, 1), ("at", 0, 2), ("xl", 2), ("yp", 1, 1), ("bz", 1),
+    ("at", 0, 3), ("zh", 1, 4), ("yl", 0, 4), ("zh", 0, 4), ("at", 1, 1), ("bh", 0, 3, 0), ("yp", 0, 5),
     ("at", 1, 2), ("bh", 0, 3, 1), ("at", 0, 4), ("yl", 1, 1), ("ys", 1, 2), ("xl", 3), ("yp", 0, 6),
     ("yp", 0, 7), ("bh", 1, 1, 0), ("yl", 0, 5), ("xl", 4), ("at", 1, 3), ("bh", 1, 1, 1), ("ys", 1, 3),
-    ("at", 0, 5), ("xl", 5), ("yp", 1, 2), ("bh", 0, 4, 0), ("bh", 0, 4, 1), ("yl", 0, 6), ("at", 1, 4),
+    ("at", 0, 5), ("xl", 5), ("bh", 0, 4, 0), ("bh", 0, 4, 1), ("yp", 1, 2), ("yl", 0, 6), ("at", 1, 4),
     ("yl", 0, 7), ("xl", 6), ("ys", 1, 4), ("at", 1, 5), ("bh", 1, 2, 0), ("at", 0, 6), ("yp", 1, 3),
     ("at", 0, 7), ("xl", 7), ("bh", 1, 2, 1), ("yl", 1, 2), ("ys", 1, 5), ("op", 0), ("at", 1, 6),
     ("yp", 1, 4), ("at", 1, 7), ("yl", 1, 3), ("zh", 2, 2), ("bh", 1, 3, 0), ("op", 1), ("ys", 1, 6),
-    ("rm", 0), ("yp", 1, 5), ("bh", 1, 3, 1), ("yl", 1, 4), ("rm", 1), ("ys", 1, 7), ("bz", 2), ("yp", 1, 6),
-    ("bh", 1, 4, 0), ("re", 0), ("yl", 1, 5), ("bh", 1, 4, 1), ("ys", 2, 0), ("zh", 2, 3), ("ys", 2, 1),
-    ("yp", 1, 7), ("bh", 2, 1, 0), ("re", 1), ("yl", 1, 6), ("ys", 2, 2), ("yp", 2, 0), ("bh", 2, 1, 1),
-    ("zh", 2, 4), ("yp", 2, 1), ("ap", 0), ("ys", 2, 3), ("yl", 1, 7), ("bh", 2, 2, 0), ("ys", 2, 4),
-    ("yp", 2, 2), ("yl", 2, 0), ("ap", 1), ("ys", 2, 5), ("yl", 2, 1), ("bh", 2, 2, 1), ("ys", 2, 6),
+    ("rm", 0), ("yp", 1, 5), ("bh", 1, 3, 1), ("yl", 1, 4), ("rm", 1), ("ys", 1, 7), ("zh", 2, 3), ("bz", 2),
+    ("yp", 1, 6), ("bh", 1, 4, 0), ("re", 0), ("yl", 1, 5), ("bh", 1, 4, 1), ("zh", 2, 4), ("ys", 2, 0),
+    ("ys", 2, 1), ("yp", 1, 7), ("re", 1), ("bh", 2, 1, 0), ("yl", 1, 6), ("ys", 2, 2), ("yp", 2, 0),
+    ("bh", 2, 1, 1), ("yp", 2, 1), ("ap", 0), ("ys", 2, 3), ("yl", 1, 7), ("ys", 2, 4), ("bh", 2, 2, 0),
+    ("yp", 2, 2), ("yl", 2, 0), ("ys", 2, 5), ("ap", 1), ("yl", 2, 1), ("ys", 2, 6), ("bh", 2, 2, 1),
     ("yp", 2, 3), ("sn", 0), ("yp", 2, 4), ("yl", 2, 2), ("ys", 2, 7), ("bh", 2, 3, 0), ("yp", 2, 5),
-    ("sn", 1), ("gd",), ("yp", 2, 6), ("yl", 2, 3), ("yl", 2, 4), ("bh", 2, 3, 1), ("yp", 2, 7), ("ud",),
-    ("yl", 2, 5), ("bh", 2, 4, 0), ("ds", 0), ("yl", 2, 6), ("ds", 1), ("yl", 2, 7), ("bh", 2, 4, 1),
+    ("sn", 1), ("gd",), ("yl", 2, 3), ("yp", 2, 6), ("yl", 2, 4), ("bh", 2, 3, 1), ("yp", 2, 7), ("ud",),
+    ("yl", 2, 5), ("ds", 0), ("yl", 2, 6), ("bh", 2, 4, 0), ("ds", 1), ("yl", 2, 7), ("bh", 2, 4, 1),
     ("ds", 2), ("dm", 0), ("ds", 3), ("dm", 1), ("dm", 2), ("dm", 3),
 )
 

time: 105 us -> 105 us (level)
  no operation moved by 1% of the time
where the time goes in v7:
time: 105 us
  Pallas kernels  104 us (99%)
    pallas_call x1, Pallas kernels, local(): pl.pallas_call(layer_kernel, out_shape=results, in_specs=[hbm] * 16, out_...  102 us

profile of v7, /device:TPU:1, one launch (start us, length us, event | category | flops | bytes accessed | tf_op | source)
XLA Modules:
  0.0 104.6 jit_solution(4802670296418601884)
XLA Ops:
  0.6 102.1 %layer.1 = (bf16[256,512]{1,0:T(8,128)(2,1)}, f32[2,128]{1,0:T(2,128)}, f32[2]{0:T(128)}) custom-call(bf16[256,2048]{1,0:T(8,128)(2,1)} %bitcast.7, f32[1,2048]{1,0:T(1,128)} %bitcast.8, bf16[2048,512]{1,0:T(8,128)(2,1)} %qw_hbm.1, f32[1,512]{1,0:T(1,128)} %bitcast.10, bf16[2048,256]{1,0:T(8,128)(2,1)} %kw_hbm.1, f32[2,128]{1,0:T(2,128)} %bitcast.11, ...), custom_call_target="tpu_custom_call" | custom-call | tf_op jit(solution)/shard_map/layer/pallas_call | solution.py:712
  102.8 1.7 %finish.1 = (bf16[256,512]{1,0:T(8,128)(2,1)}, f32[2,128]{1,0:T(2,128)}, f32[2]{0:T(128)}) custom-call(bf16[256,512]{1,0:T(8,128)(2,1)} %get-tuple-element.9.layer_hbm, f32[2,128]{1,0:T(2,128)} %get-tuple-element.10.infl_hbm, f32[2]{0:T(128)} %get-tuple-element.11.score_hbm), custom_call_target="tpu_custom_call" | custom-call | tf_op jit(solution)/shard_map/finish/pallas_call | solution.py:779
